TPU v7x, 32 devices: a whole 2x2x4 slice. The times are simulated.
32 devices in a mesh: dp: 8 (over z, y), fsdp: 4 (over x, core).
Axes of the slice: x: 2, y: 2, z: 4, core: 2. Of those that a mesh axis runs over, the one named last changes fastest.
Arguments:
- hidden: bfloat16 [32768, 1536], P(('dp', 'fsdp')), may hold values from -6 to 6
- grad_out: bfloat16 [32768, 1536], P(('dp', 'fsdp')), may hold values from -6 to 6
- segment_ids: int32 [32768], P(('dp', 'fsdp')), may hold values from 0 to 189, as said below
- w_zx: bfloat16 [1536, 6144], P(('dp', 'fsdp')), may hold values from -0.15625 to 0.15625
- w_bc: bfloat16 [1536, 256], P(('dp', 'fsdp')), may hold values from -0.15625 to 0.15625
- w_dt: bfloat16 [1536, 48], P(('dp', 'fsdp')), may hold values from -0.15625 to 0.15625
- w_out: bfloat16 [3072, 1536], P(('dp', 'fsdp')), may hold values from -0.109375 to 0.109375
- conv_params: bfloat16 [5, 3328], P(None, ('dp', 'fsdp')), may hold values from -3 to 3
- norm_gain: bfloat16 [1536], P(('dp', 'fsdp')), may hold values from 0.5 to 1.5
- gate_gain: bfloat16 [3072], P(('dp', 'fsdp')), may hold values from 0.5 to 1.5
- head_params: float32 [3, 48], replicated, may hold values from -7 to 3, as said below
Outputs:
- output: bfloat16 [32768, 1536], P(('dp', 'fsdp'))
- grad_input: bfloat16 [32768, 1536], P(('dp', 'fsdp'))
- grad_w_zx: float32 [1536, 6144], P(('dp', 'fsdp'))
- grad_w_bc: float32 [1536, 256], P(('dp', 'fsdp'))
- grad_w_dt: float32 [1536, 48], P(('dp', 'fsdp'))
- grad_w_out: float32 [3072, 1536], P(('dp', 'fsdp'))
- grad_conv: float32 [5, 3328], P(None, ('dp', 'fsdp'))
- grad_norm_gain: float32 [1536], P(('dp', 'fsdp'))
- grad_gate_gain: float32 [3072], P(('dp', 'fsdp'))
- grad_heads: float32 [3, 48], replicated
Inputs may be any that keep to these rules, and one draw needn't show every extreme that they name: `segment_ids`: ids never fall along the array and a new id begins at every multiple of 512 positions. The first block of 512 positions holds one sequence that fills it; every other block holds exactly 3 sequences of uneven lengths, whose boundaries fall anywhere inside the block, so the largest id is 189. `head_params`: row 0 is the log of a positive decay rate, row 1 a step bias, row 2 a skip weight.
All inputs are finite; a program needn't handle non-finite values.
Results may differ from a plain program's by a relative error of at most 0.012.
Values may be sent and summed in bfloat16 or wider, within the bound.
A program may use at most 448 MiB of HBM per device.

v0:
```python
import jax
import jax.numpy as jnp
from jax import lax
from jax.sharding import PartitionSpec as P

GROUP = 256
SLOT = 512


EPS = 1e-05
HIGHEST = lax.Precision.HIGHEST


def pre_norm(rows, gain):
    return rows * lax.rsqrt(jnp.mean(rows * rows, axis=-1, keepdims=True) + EPS) * gain


def causal_conv(signal, taps_bias, seg):
    width_taps = taps_bias.shape[0] - 1
    length = signal.shape[0]
    summed = taps_bias[width_taps] + taps_bias[width_taps - 1] * signal
    for offset in range(1, width_taps):
        moved = jnp.pad(signal, ((offset, 0), (0, 0)))[:length]
        earlier = jnp.pad(seg, (offset, 0), constant_values=-1)[:length]
        summed = summed + taps_bias[width_taps - 1 - offset] * jnp.where(
            (earlier == seg)[:, None], moved, 0.0
        )
    return summed


def group_step(carried, sliced):
    head_x, b_rows, c_rows, step_sizes, decays, seg_rows, prev_id = sliced
    cumul = jnp.cumsum(decays, axis=0)
    length = seg_rows.shape[0]
    places = jnp.arange(length)
    allowed = (places[:, None] >= places[None, :]) & (seg_rows[:, None] == seg_rows[None, :])
    cumul_t = cumul.T
    spread = cumul_t[:, :, None] - cumul_t[:, None, :]
    within = jnp.where(allowed[None], jnp.exp(jnp.where(allowed[None], spread, 0.0)), 0.0)
    scores = jnp.einsum("in,jn->ij", c_rows, b_rows, precision=HIGHEST)
    mixing = within * scores[None] * step_sizes.T[:, None, :]
    inner = jnp.einsum("hij,jhp->ihp", mixing, head_x, precision=HIGHEST)
    entering = jnp.where((seg_rows == prev_id)[:, None], jnp.exp(cumul), 0.0)
    outer = jnp.einsum("in,hpn->ihp", c_rows, carried, precision=HIGHEST) * entering[:, :, None]
    leaving = (
        jnp.where((seg_rows == seg_rows[-1])[:, None], jnp.exp(cumul[-1][None, :] - cumul), 0.0)
        * step_sizes
    )
    kept_part = jnp.where(seg_rows[-1] == prev_id, jnp.exp(cumul[-1]), 0.0)
    updated = carried * kept_part[:, None, None] + jnp.einsum(
        "jh,jhp,jn->hpn", leaving, head_x, b_rows, precision=HIGHEST
    )
    return (updated, inner + outer)


def mixer(zx_part, bc_part, dt_part, conv_part, heads, gate_scale, seg):
    width = gate_scale.shape[0]
    head_count = heads.shape[1]
    head_size = width // head_count
    state_size = bc_part.shape[1] // 2
    length = zx_part.shape[0]
    gate_part = zx_part[:, :width]
    joined = jnp.concatenate([zx_part[:, width:], bc_part], axis=1)
    activated = jax.nn.silu(causal_conv(joined, conv_part, seg))
    head_x = activated[:, :width].reshape(length, head_count, head_size)
    b_rows = activated[:, width : width + state_size]
    c_rows = activated[:, width + state_size :]
    step_sizes = jax.nn.softplus(dt_part + heads[1])
    decays = -jnp.exp(heads[0]) * step_sizes
    blocks = length // GROUP
    prev_ids = jnp.concatenate([jnp.full((1,), -1, jnp.int32), seg[GROUP - 1 : length - 1 : GROUP]])
    initial = jnp.zeros((head_count, head_size, state_size), head_x.dtype)
    sliced = (
        head_x.reshape(blocks, GROUP, head_count, head_size),
        b_rows.reshape(blocks, GROUP, state_size),
        c_rows.reshape(blocks, GROUP, state_size),
        step_sizes.reshape(blocks, GROUP, head_count),
        decays.reshape(blocks, GROUP, head_count),
        seg.reshape(blocks, GROUP),
        prev_ids,
    )
    final_state, scanned = lax.scan(jax.checkpoint(group_step), initial, sliced)
    scan_y = scanned.reshape(length, head_count, head_size) + heads[2][None, :, None] * head_x
    gated = scan_y.reshape(length, width) * jax.nn.silu(gate_part)
    return gated * lax.rsqrt(jnp.mean(gated * gated, axis=-1, keepdims=True) + EPS) * gate_scale


def layer_forward(rows, seg, weights, heads):
    w_zx, w_bc, w_dt, w_out, conv_params, norm_gain, gate_gain = weights
    rows_f = rows.astype(jnp.float32)
    normed, norm_back = jax.vjp(pre_norm, rows_f, norm_gain.astype(jnp.float32))
    normed_bf = normed.astype(jnp.bfloat16)
    zx_bf = lax.optimization_barrier(
        jnp.dot(normed_bf, w_zx, preferred_element_type=jnp.float32).astype(jnp.bfloat16)
    )
    bc_bf = lax.optimization_barrier(
        jnp.dot(normed_bf, w_bc, preferred_element_type=jnp.float32).astype(jnp.bfloat16)
    )
    dt_bf = lax.optimization_barrier(
        jnp.dot(normed_bf, w_dt, preferred_element_type=jnp.float32).astype(jnp.bfloat16)
    )

    def local_mixer(zx_part, bc_part, dt_part, conv_part, head_part, gate_scale):
        return mixer(zx_part, bc_part, dt_part, conv_part, head_part, gate_scale, seg)

    mixed, mixer_back = jax.vjp(
        local_mixer,
        zx_bf.astype(jnp.float32),
        bc_bf.astype(jnp.float32),
        dt_bf.astype(jnp.float32),
        conv_params.astype(jnp.float32),
        heads,
        gate_gain.astype(jnp.float32),
    )
    mixed_bf = mixed.astype(jnp.bfloat16)
    output = (rows_f + jnp.dot(mixed_bf, w_out, preferred_element_type=jnp.float32)).astype(
        jnp.bfloat16
    )
    return (output, (normed_bf, mixed_bf, norm_back, mixer_back))


def layer_backward(cotangent, saved, weights):
    w_zx, w_bc, w_dt, w_out, conv_params, norm_gain, gate_gain = weights
    normed_bf, mixed_bf, norm_back, mixer_back = saved
    back_mixed = jnp.dot(cotangent, w_out.T, preferred_element_type=jnp.float32)
    grad_out_w = jnp.dot(mixed_bf.T, cotangent, preferred_element_type=jnp.float32)
    d_zx, d_bc, d_dt, d_conv, d_heads, d_gate = mixer_back(back_mixed)
    d_zx_bf = d_zx.astype(jnp.bfloat16)
    d_bc_bf = d_bc.astype(jnp.bfloat16)
    d_dt_bf = d_dt.astype(jnp.bfloat16)
    grad_zx = jnp.dot(normed_bf.T, d_zx_bf, preferred_element_type=jnp.float32)
    grad_bc = jnp.dot(normed_bf.T, d_bc_bf, preferred_element_type=jnp.float32)
    grad_dt = jnp.dot(normed_bf.T, d_dt_bf, preferred_element_type=jnp.float32)
    back_normed = jnp.dot(d_zx_bf, w_zx.T, preferred_element_type=jnp.float32)
    back_normed = back_normed + jnp.dot(d_bc_bf, w_bc.T, preferred_element_type=jnp.float32)
    back_normed = back_normed + jnp.dot(d_dt_bf, w_dt.T, preferred_element_type=jnp.float32)
    d_rows, d_norm = norm_back(back_normed)
    grad_in = (cotangent.astype(jnp.float32) + d_rows).astype(jnp.bfloat16)
    return (grad_in, (grad_zx, grad_bc, grad_dt, grad_out_w, d_conv, d_norm, d_gate), d_heads)


def per_device(
    hidden,
    grad_out,
    segment_ids,
    w_zx,
    w_bc,
    w_dt,
    w_out,
    conv_params,
    norm_gain,
    gate_gain,
    head_params,
):
    owned = (w_zx, w_bc, w_dt, w_out, conv_params, norm_gain, gate_gain)
    count = hidden.shape[0] // SLOT
    totals = None
    shares = tuple((jnp.zeros(weight.shape, jnp.float32) for weight in owned))
    head_total = jnp.zeros(head_params.shape, jnp.float32)
    outputs = []
    grad_ins = []
    for micro_index in range(count):
        first_row = micro_index * SLOT
        rows = hidden[first_row : first_row + SLOT]
        cotangent = grad_out[first_row : first_row + SLOT]
        seg = segment_ids[first_row : first_row + SLOT]
        forward_set = (
            lax.all_gather(w_zx, ("dp", "fsdp"), axis=0, tiled=True),
            lax.all_gather(w_bc, ("dp", "fsdp"), axis=0, tiled=True),
            lax.all_gather(w_dt, ("dp", "fsdp"), axis=0, tiled=True),
            lax.all_gather(w_out, ("dp", "fsdp"), axis=0, tiled=True),
            lax.all_gather(conv_params, ("dp", "fsdp"), axis=1, tiled=True),
            lax.all_gather(norm_gain, ("dp", "fsdp"), axis=0, tiled=True),
            lax.all_gather(gate_gain, ("dp", "fsdp"), axis=0, tiled=True),
        )
        output, saved = layer_forward(rows, seg, forward_set, head_params)
        backward_set = (
            lax.all_gather(w_zx, ("dp", "fsdp"), axis=0, tiled=True),
            lax.all_gather(w_bc, ("dp", "fsdp"), axis=0, tiled=True),
            lax.all_gather(w_dt, ("dp", "fsdp"), axis=0, tiled=True),
            lax.all_gather(w_out, ("dp", "fsdp"), axis=0, tiled=True),
            lax.all_gather(conv_params, ("dp", "fsdp"), axis=1, tiled=True),
            lax.all_gather(norm_gain, ("dp", "fsdp"), axis=0, tiled=True),
            lax.all_gather(gate_gain, ("dp", "fsdp"), axis=0, tiled=True),
        )
        grad_in, grads, head_grad = layer_backward(cotangent, saved, backward_set)
        outputs.append(output)
        grad_ins.append(grad_in)
        head_total = head_total + head_grad
        totals = grads if totals is None else jax.tree.map(jnp.add, totals, grads)
    shares = (
        lax.psum_scatter(totals[0], ("dp", "fsdp"), scatter_dimension=0, tiled=True),
        lax.psum_scatter(totals[1], ("dp", "fsdp"), scatter_dimension=0, tiled=True),
        lax.psum_scatter(totals[2], ("dp", "fsdp"), scatter_dimension=0, tiled=True),
        lax.psum_scatter(totals[3], ("dp", "fsdp"), scatter_dimension=0, tiled=True),
        lax.psum_scatter(totals[4], ("dp", "fsdp"), scatter_dimension=1, tiled=True),
        lax.psum_scatter(totals[5], ("dp", "fsdp"), scatter_dimension=0, tiled=True),
        lax.psum_scatter(totals[6], ("dp", "fsdp"), scatter_dimension=0, tiled=True),
    )
    head_sum = lax.psum(head_total, ("dp", "fsdp"))
    return (
        jnp.concatenate(outputs, axis=0),
        jnp.concatenate(grad_ins, axis=0),
        shares[0],
        shares[1],
        shares[2],
        shares[3],
        shares[4],
        shares[5],
        shares[6],
        head_sum,
    )


def solution(mesh):
    return jax.shard_map(
        per_device,
        mesh=mesh,
        in_specs=(
            P(("dp", "fsdp"), None),
            P(("dp", "fsdp"), None),
            P(("dp", "fsdp")),
            P(("dp", "fsdp"), None),
            P(("dp", "fsdp"), None),
            P(("dp", "fsdp"), None),
            P(("dp", "fsdp"), None),
            P(None, ("dp", "fsdp")),
            P(("dp", "fsdp")),
            P(("dp", "fsdp")),
            P(),
        ),
        out_specs=(
            P(("dp", "fsdp"), None),
            P(("dp", "fsdp"), None),
            P(("dp", "fsdp"), None),
            P(("dp", "fsdp"), None),
            P(("dp", "fsdp"), None),
            P(("dp", "fsdp"), None),
            P(None, ("dp", "fsdp")),
            P(("dp", "fsdp")),
            P(("dp", "fsdp")),
            P(),
        ),
        check_vma=False,
    )
```

profile of v0, /device:TPU:0, one launch (start us, length us, event | category | flops | bytes accessed | tf_op | source)
XLA Modules:
  0.0 2195.1 jit_solution(1246851679272170119)
XLA Ops:
  10.4 43.8 %all-reduce.54 = (bf16[1536]{0:T(1024)(128)(2,1)S(1)}, bf16[3072]{0:T(1024)(128)(2,1)}) all-reduce(bf16[1536]{0:T(1024)(128)(2,1)S(1)} %dynamic-update-slice, bf16[3072]{0:T(1024)(128)(2,1)S(1)} %dynamic-update-slice.1), channel_id=1, replica_groups=mesh['dp'=8,'fsdp'=4] {'dp','fsdp'}, use_global_device_ids=true, to_apply=%add.48 | all-reduce | flops 4608 | bytes 18432
  56.9 45.8 %all_gather.18 = bf16[1536,256]{1,0:T(8,128)(2,1)S(1)} all-gather(bf16[48,256]{1,0:T(8,128)(2,1)} %param.24), channel_id=1, replica_groups=mesh['dp'=8,'fsdp'=4] {'dp','fsdp'}, dimensions={0}, use_global_device_ids=true | all-gather | bytes 811008 | tf_op jit(solution)/shard_map/all_gather | solution.py:169
  106.4 40.1 %all_gather.15 = bf16[1536,48]{1,0:T(8,128)(2,1)S(1)} all-gather(bf16[48,48]{1,0:T(8,128)(2,1)S(1)} %copy-done.78), channel_id=1, replica_groups=mesh['dp'=8,'fsdp'=4] {'dp','fsdp'}, dimensions={0}, use_global_device_ids=true | all-gather | bytes 152064 | tf_op jit(solution)/shard_map/all_gather | solution.py:170
  151.5 38.9 %all-gather = bf16[32,104,5]{1,2,0:T(8,128)(2,1)S(1)} all-gather(bf16[1,104,5]{1,2,0:T(8,128)(2,1)S(1)} %bitcast.766), channel_id=1, replica_groups=mesh['dp'=8,'fsdp'=4] {'dp','fsdp'}, dimensions={0}, use_global_device_ids=true | all-gather | bytes 34320 | tf_op jit(solution)/shard_map/all_gather | solution.py:172
  256.2 31.9 %fusion.197 = (f32[512,3328]{1,0:T(8,128)S(1)}, f32[512,3328]{1,0:T(8,128)}, f32[512,3328]{1,0:T(8,128)}, f32[512,3328]{1,0:T(8,128)}) fusion(f32[512,3328]{1,0:T(8,128)} %pad_maximum_fusion, pred[512]{0:T(512)(128)(4,1)S(1)} %copy-done.85, f32[3328]{0:T(1024)S(1)} %get-tuple-element.1597, pred[512]{0:T(512)(128)(4,1)S(1)} %copy-done.83, ...), kind=kLoop, calls=%fused_computation.338 | loop fusion | flops 51118080 | bytes 40964096 | tf_op jit(solution)/shard_map/jvp(jit(silu))/mul | solution.py:64
  322.6 70.1 %while.84 = (s32[]{:T(128)}, f32[48,64,128]{2,1,0:T(8,128)S(1)}, f32[2,256,48,64]{1,3,2,0:T(8,128)}, f32[2,48,64,128]{3,2,1,0:T(8,128)}, s32[2,256]{1,0:T(2,128)...) while((s32[]{:T(128)}, f32[48,64,128]{2,1,0:T(8,128)S(1)}, ...), condition=%wide.region_4.6_spmd.clone, body=%wide.region_1.5_spmd.clone.sunk | while | flops 4954387456 | bytes 25769504 | solution.py:82
  360.2 16.9 fusion.423
  494.1 259.5 %while.86 = (s32[]{:T(128)}, f32[48,64,128]{2,1,0:T(8,128)}, f32[2,256,48,64]{1,3,2,0:T(8,128)}, f32[2,256,128]{2,1,0:T(8,128)}, f32[2,256,128]{2,1,0:T(8,128)},...) while((s32[]{:T(128)}, f32[48,64,128]{2,1,0:T(8,128)}, ...), condition=%wide.region_25.27_spmd.clone, body=%wide.region_13.26_spmd.clone.sunk | while | flops 11249172480 | bytes 99515456 | solution.py:82
  552.0 22.5 %fusion.455 = (f32[48,256]{1,0:T(8,128)}, f32[48,256]{1,0:T(8,128)}, f32[48,256]{1,0:T(8,128)}, f32[256,256]{1,0:T(8,128)}) fusion(f32[48,256]{1,0:T(8,128)} %copy.570, f32[256,256]{1,0:T(8,128)} %fusion.453, f32[48,256]{1,0:T(8,128)} %copy_bitcast_fusion.25, pred[256,256]{1,0:T(8,128)(4,1)} %fusion.454, f32[256,48,64]{0,2,1:T(8,128)} %get-tuple-element.2231, ...), kind=kOutput, calls=%fused_computation.127.clone.1 | convolution fusion | flops 2463002624 | bytes 7127040 | tf_op jit(solution)/shard_map/transpose(jvp())/while/body/eval_jaxpr/checkpoint/hij,jhp->ihp/dot_general | solution.py:42
  672.4 22.5 %fusion.455 = (f32[48,256]{1,0:T(8,128)}, f32[48,256]{1,0:T(8,128)}, f32[48,256]{1,0:T(8,128)}, f32[256,256]{1,0:T(8,128)}) fusion(f32[48,256]{1,0:T(8,128)} %copy.570, f32[256,256]{1,0:T(8,128)} %fusion.453, f32[48,256]{1,0:T(8,128)} %copy_bitcast_fusion.25, pred[256,256]{1,0:T(8,128)(4,1)} %fusion.454, f32[256,48,64]{0,2,1:T(8,128)} %get-tuple-element.2231, ...), kind=kOutput, calls=%fused_computation.127.clone.1 | convolution fusion | flops 2463002624 | bytes 7127040 | tf_op jit(solution)/shard_map/transpose(jvp())/while/body/eval_jaxpr/checkpoint/hij,jhp->ihp/dot_general | solution.py:42
  802.2 68.8 %while.85 = (s32[]{:T(128)}, f32[48,64,128]{2,1,0:T(8,128)S(1)}, f32[2,256,48,64]{1,3,2,0:T(8,128)}, f32[2,48,64,128]{3,2,1,0:T(8,128)}, s32[2,256]{1,0:T(2,128)...) while((s32[]{:T(128)}, f32[48,64,128]{2,1,0:T(8,128)S(1)}, ...), condition=%wide.region_10.12_spmd.clone, body=%wide.region_7.11_spmd.clone.sunk | while | flops 4954387456 | bytes 25769824 | solution.py:82
  893.1 17.6 multiply_reduce_fusion.24
  964.6 265.0 %while.87 = (s32[]{:T(128)}, f32[48,64,128]{2,1,0:T(8,128)}, f32[2,256,48,64]{1,3,2,0:T(8,128)}, f32[2,256,128]{2,1,0:T(8,128)}, f32[2,256,128]{2,1,0:T(8,128)},...) while((s32[]{:T(128)}, f32[48,64,128]{2,1,0:T(8,128)}, ...), condition=%wide.region_40.42_spmd.clone, body=%wide.region_28.41_spmd.clone.sunk | while | flops 11249172480 | bytes 101612656 | solution.py:82
  1021.2 22.4 %fusion.483 = (f32[48,256]{1,0:T(8,128)}, f32[48,256]{1,0:T(8,128)}, f32[48,256]{1,0:T(8,128)}, f32[256,256]{1,0:T(8,128)}) fusion(f32[48,256]{1,0:T(8,128)} %copy.585, f32[256,256]{1,0:T(8,128)} %fusion.481, f32[48,256]{1,0:T(8,128)} %copy_bitcast_fusion.27, pred[256,256]{1,0:T(8,128)(4,1)} %fusion.482, f32[256,48,64]{0,2,1:T(8,128)} %get-tuple-element.2274, ...), kind=kOutput, calls=%fused_computation.207.clone.1 | convolution fusion | flops 2463002624 | bytes 7127040 | tf_op jit(solution)/shard_map/transpose(jvp())/while/body/eval_jaxpr/checkpoint/hij,jhp->ihp/dot_general | solution.py:42
  1140.7 22.4 %fusion.483 = (f32[48,256]{1,0:T(8,128)}, f32[48,256]{1,0:T(8,128)}, f32[48,256]{1,0:T(8,128)}, f32[256,256]{1,0:T(8,128)}) fusion(f32[48,256]{1,0:T(8,128)} %copy.585, f32[256,256]{1,0:T(8,128)} %fusion.481, f32[48,256]{1,0:T(8,128)} %copy_bitcast_fusion.27, pred[256,256]{1,0:T(8,128)(4,1)} %fusion.482, f32[256,48,64]{0,2,1:T(8,128)} %get-tuple-element.2274, ...), kind=kOutput, calls=%fused_computation.207.clone.1 | convolution fusion | flops 2463002624 | bytes 7127040 | tf_op jit(solution)/shard_map/transpose(jvp())/while/body/eval_jaxpr/checkpoint/hij,jhp->ihp/dot_general | solution.py:42
  1318.1 18.4 fusion.188
  1371.2 21.3 fusion.235
  1392.6 31.3 %convolution_add_fusion.4 = f32[1536,6144]{1,0:T(8,128)} fusion(f32[1536,6144]{1,0:T(8,128)} %fusion.235, f32[512,3072]{1,0:T(8,128)} %get-tuple-element.1773, f32[512,3072]{1,0:T(8,128)} %split.20, f32[512]{0:T(512)S(1)} %copy-done.50, f32[1536]{0:T(1024)S(1)} %copy-done.41, bf16[1024,1536]{1,0:T(8,128)(2,1)S(1)} %copy-done.13), kind=kOutput, calls=%fused_computation.278 | convolution fusion | flops 9682550784 | bytes 89663488 | tf_op jit(solution)/shard_map/dot_general | solution.py:131
  1442.3 18.8 fusion.208
  1461.2 20.2 fusion.213
  1482.2 37.5 %all-reduce.53 = (f32[1536]{0:T(1024)S(1)}, f32[3072]{0:T(1024)S(1)}, f32[3,48]{1,0:T(4,128)}) all-reduce(f32[1536]{0:T(1024)S(1)} %add.380, f32[3072]{0:T(1024)S(1)} %add.381, f32[3,48]{1,0:T(4,128)S(1)} %add_add_fusion.5), channel_id=7, replica_groups=mesh['dp'=8,'fsdp'=4] {'dp','fsdp'}, use_global_device_ids=true, to_apply=%region_59.61.clone | all-reduce | flops 4752 | bytes 38016
  1544.9 75.3 %reduce-scatter.8.cloned.1.call-done = f32[48,256]{1,0:T(8,128)} async-done(((f32[1536,256]{1,0:T(8,128)}), f32[48,256]{1,0:T(8,128)}) %reduce-scatter.8.cloned.1.call-update) | async-done | bytes 49168 | tf_op jit(solution)/shard_map/reduce_scatter | solution.py:193
  1620.3 212.8 %reduce-scatter.12.cloned.1.call-done = f32[96,1536]{1,0:T(8,128)} async-done(((f32[3072,1536]{1,0:T(8,128)}), f32[96,1536]{1,0:T(8,128)}) %reduce-scatter.12.cloned.1.call-update) | async-done | bytes 589840 | tf_op jit(solution)/shard_map/reduce_scatter | solution.py:195
  1833.0 355.0 %reduce-scatter.6.cloned.1.call-done = f32[48,6144]{1,0:T(8,128)} async-done(((f32[1536,6144]{1,0:T(8,128)}), f32[48,6144]{1,0:T(8,128)}) %reduce-scatter.6.cloned.1.call-update) | async-done | bytes 1179664 | tf_op jit(solution)/shard_map/reduce_scatter | solution.py:192
  (734 shorter events, 1005.7 us)
Async XLA Ops:
  7.2 98.6 %copy-start.11 = (bf16[1024,1536]{1,0:T(8,128)(2,1)S(1)}, bf16[1024,1536]{1,0:T(8,128)(2,1)}, u32[]{:S(2)}) copy-start(bf16[1024,1536]{1,0:T(8,128)(2,1)} %param.20) | copy-start | bytes 9437188
  7.2 189.5 %all-gather.4.cloned.1.call-start = ((), (), s32[]{:S(2)}) async-start(), calls=%async_computation.4 | async-start | bytes 19464192 | tf_op jit(solution)/shard_map/all_gather | solution.py:168
  7.9 432.0 %all-gather.6.cloned.1.call-start = ((), (), s32[]{:S(2)}) async-start(), calls=%async_computation.5 | async-start | bytes 9732096 | tf_op jit(solution)/shard_map/all_gather | solution.py:171
  8.7 1534.9 %all-reduce.57.cloned.1.call-start = ((), (), s32[]{:S(2)}) async-start(), calls=%async_computation.10 | async-start | bytes 212992
  54.3 164.6 %copy-start.40 = (f32[1536]{0:T(1024)}, f32[1536]{0:T(1024)S(1)}, u32[]{:S(2)}) copy-start(f32[1536]{0:T(1024)S(1)} %convert_element_type.108) | copy-start | bytes 18436
  56.9 90.4 %copy-start.76 = (f32[512]{0:T(512)}, f32[512]{0:T(512)S(1)}, u32[]{:S(2)}) copy-start(f32[512]{0:T(512)S(1)} %get-tuple-element.1595) | copy-start | bytes 6148
  56.9 139.8 %copy-start.51 = (f32[512]{0:T(512)}, f32[512]{0:T(512)S(1)}, u32[]{:S(2)}) copy-start(f32[512]{0:T(512)S(1)} %fusion.258) | copy-start | bytes 6148
  102.7 116.1 %copy-start.49 = (f32[512]{0:T(512)}, f32[512]{0:T(512)S(1)}, u32[]{:S(2)}) copy-start(f32[512]{0:T(512)S(1)} %fusion.260) | copy-start | bytes 6148
  105.8 85.0 %copy-start.105 = (f32[3,48]{1,0:T(4,128)S(1)}, f32[3,48]{1,0:T(4,128)}, u32[]{:S(2)}) copy-start(f32[3,48]{1,0:T(4,128)} %param.30) | copy-start | bytes 1732
  147.2 64.4 %copy-start.59 = (bf16[512,48]{0,1:T(8,128)(2,1)}, bf16[512,48]{0,1:T(8,128)(2,1)S(1)}, u32[]{:S(2)}) copy-start(bf16[512,48]{0,1:T(8,128)(2,1)S(1)} %convolution_convert_fusion.5) | copy-start | bytes 147460
  147.9 63.7 %copy-start.60 = (bf16[512,48]{0,1:T(8,128)(2,1)}, bf16[512,48]{0,1:T(8,128)(2,1)S(1)}, u32[]{:S(2)}) copy-start(bf16[512,48]{0,1:T(8,128)(2,1)S(1)} %convolution_convert_fusion.4) | copy-start | bytes 147460
  148.6 107.5 %copy-start.81 = (pred[512]{0:T(512)(128)(4,1)}, pred[512]{0:T(512)(128)(4,1)S(1)}, u32[]{:S(2)}) copy-start(pred[512]{0:T(512)(128)(4,1)S(1)} %get-tuple-element.1808) | copy-start | bytes 1540
  151.5 98.0 %copy-start.30 = (f32[512,256]{1,0:T(8,128)}, f32[512,256]{1,0:T(8,128)S(1)}, u32[]{:S(2)}) copy-start(f32[512,256]{1,0:T(8,128)S(1)} %convert_element_type.116) | copy-start | bytes 1572868
  151.5 101.2 %copy-start.28 = (f32[512,256]{1,0:T(8,128)}, f32[512,256]{1,0:T(8,128)S(1)}, u32[]{:S(2)}) copy-start(f32[512,256]{1,0:T(8,128)S(1)} %convert_element_type.127) | copy-start | bytes 1572868
  190.8 65.3 %copy-start.61 = (f32[3328]{0:T(1024)}, f32[3328]{0:T(1024)S(1)}, u32[]{:S(2)}) copy-start(f32[3328]{0:T(1024)S(1)} %get-tuple-element.1597) | copy-start | bytes 39940
  190.8 65.3 %copy-start.63 = (f32[3328]{0:T(1024)}, f32[3328]{0:T(1024)S(1)}, u32[]{:S(2)}) copy-start(f32[3328]{0:T(1024)S(1)} %get-tuple-element.1598) | copy-start | bytes 39940
  190.8 65.3 %copy-start.65 = (f32[3328]{0:T(1024)}, f32[3328]{0:T(1024)S(1)}, u32[]{:S(2)}) copy-start(f32[3328]{0:T(1024)S(1)} %get-tuple-element.1599) | copy-start | bytes 39940
  190.8 65.3 %copy-start.66 = (f32[3328]{0:T(1024)}, f32[3328]{0:T(1024)S(1)}, u32[]{:S(2)}) copy-start(f32[3328]{0:T(1024)S(1)} %get-tuple-element.1600) | copy-start | bytes 39940
  1294.7 250.2 %reduce-scatter.10.cloned.1.call-start = ((), (), s32[]{:S(2)}) async-start(), calls=%async_computation.8 | async-start | bytes 811008 | tf_op jit(solution)/shard_map/reduce_scatter | solution.py:194
  1318.1 302.2 %reduce-scatter.8.cloned.1.call-start = ((), (), s32[]{:S(2)}) async-start(), calls=%async_computation.7 | async-start | bytes 1622016 | tf_op jit(solution)/shard_map/reduce_scatter | solution.py:193
  1343.4 489.6 %reduce-scatter.12.cloned.1.call-start = ((), (), s32[]{:S(2)}) async-start(), calls=%async_computation.9 | async-start | bytes 19464192 | tf_op jit(solution)/shard_map/reduce_scatter | solution.py:195
  1358.8 829.3 %reduce-scatter.6.cloned.1.call-start = ((), (), s32[]{:S(2)}) async-start(), calls=%async_computation.6 | async-start | bytes 38928384 | tf_op jit(solution)/shard_map/reduce_scatter | solution.py:192
  1461.2 59.6 %copy-start.75 = (f32[512]{0:T(512)S(1)}, f32[512]{0:T(512)}, u32[]{:S(2)}) copy-start(f32[512]{0:T(512)} %copy-done.74) | copy-start | bytes 6148
  1461.2 59.6 %copy-start.77 = (f32[512]{0:T(512)S(1)}, f32[512]{0:T(512)}, u32[]{:S(2)}) copy-start(f32[512]{0:T(512)} %copy-done.76) | copy-start | bytes 6148
  (127 other events, 1557.6 us)
Sparse Core Ops, SparseCore 0:
  10.9 134.6 all-gather.3
  148.4 80.8 all-gather.5
  1294.8 119.9 all-reduce.56
  1420.4 97.1 reduce-scatter.9
  1523.2 96.9 reduce-scatter.7
  1627.1 205.8 reduce-scatter.11
  1840.0 347.9 reduce-scatter.5
where the time goes:
time: 2210 us; the launch traced here: 2200 us
  waiting for transfers between devices  645 us (29%)
  matrix products  603 us (27%)
  local copies, waits for them, and re-layouts  371 us (17%)
  other arithmetic  296 us (13%)
  blocking collectives  206 us (9%)
  loops' own time  58 us (3%)
    reduce_scatter x1, waiting for transfers between devices, per_device(): lax.psum_scatter(totals[0], ('dp', 'fsdp'), scatter_dimension=0, tiled=True)  355 us
    dot_general x12, matrix products, group_step(): inner = jnp.einsum('hij,jhp->ihp', mixing, head_x, precision=HIGHEST)  214 us
    reduce_scatter x1, waiting for transfers between devices, per_device(): lax.psum_scatter(totals[3], ('dp', 'fsdp'), scatter_dimension=0, tiled=True)  213 us
    dot_general x16, matrix products, group_step(): jnp.einsum('in,hpn->ihp', c_rows, carried, precision=HIGHEST)  81.3 us
    unnamed x2, blocking collectives  81.3 us
    reduce_scatter x1, waiting for transfers between devices, per_device(): lax.psum_scatter(totals[1], ('dp', 'fsdp'), scatter_dimension=0, tiled=True)  75.3 us
    dot_general x12, matrix products, group_step(): jnp.einsum('jh,jhp,jn->hpn', leaving, head_x, b_rows, precision=HIGHEST)  71.7 us
    reshape x6, local copies, waits for them, and re-layouts, mixer(): scanned.reshape(length, head_count, head_size)  64.2 us
  transfers between devices with their start and end apart: 7, of which 3 were waited for; matrix products, arithmetic and copies ran while one was open for 21% of the time, Pallas kernels for 0%

commit v1 on v0

v1 whole, which is shorter than its diff:
```python
import functools
import jax
import jax.numpy as jnp
from jax import lax
from jax.experimental import pallas as pl
from jax.experimental.pallas import tpu as pltpu
from jax.sharding import PartitionSpec as P

EPS = 1e-05
L = 128
HG = 4
LOG2E = 1.4426950408889634
bf16, f32 = jnp.bfloat16, jnp.float32
HIGHEST = lax.Precision.HIGHEST


def dot(a, b, dims=((1,), (0,)), precision=None):
    return lax.dot_general(a, b, (dims, ((), ())), preferred_element_type=f32, precision=precision)


def sigmoid(x):
    return 1.0 / (1.0 + jnp.exp(-x))


def conv_rows(ext, taps, masks, halo):
    rows = ext.shape[0] - halo
    width = 4
    v = ext[halo:]
    out = taps[4:5] + taps[3:4] * v
    for k in range(1, width):
        moved = pltpu.roll(ext, k, 0)[halo:]
        out = out + (taps[3 - k : 4 - k] * masks[:, k : k + 1]) * moved
    return out


def prep_kernel(bcdt_ref, taps_ref, heads_ref, m_ref, segc_ref, segr_ref,
                b_ref, c_ref, bt_ref, ct_ref, pre_ref, gm_ref, cum4_ref, cumr_ref, sc_ref, dt_ref):
    T = bcdt_ref.shape[0]
    nc = T // L
    N = b_ref.shape[1]
    H = dt_ref.shape[1]
    groups = cum4_ref.shape[0]
    taps = taps_ref[...]
    tri = (lax.broadcasted_iota(jnp.int32, (L, L), 0) >= lax.broadcasted_iota(jnp.int32, (L, L), 1))
    trif = tri.astype(f32)
    neg_rate = -jnp.exp(heads_ref[0:1, :H]) * LOG2E
    bias = heads_ref[1:2, :H]

    def chunk(c, carry):
        t0 = pl.multiple_of(c * L, L)
        here = pl.ds(t0, L)
        h0 = pl.multiple_of(jnp.maximum(t0 - 16, 0), 16)
        before = bcdt_ref[pl.ds(h0, 16), : 2 * N].astype(f32)
        v = bcdt_ref[here, : 2 * N].astype(f32)
        pre = conv_rows(jnp.concatenate([before, v], axis=0), taps, m_ref[here, :], 16)
        pre_ref[here, :] = pre
        act = pre * sigmoid(pre)
        b = act[:, :N]
        cc = act[:, N:]
        bb = b.astype(bf16)
        cb = cc.astype(bf16)
        b_ref[here, :] = bb
        c_ref[here, :] = cb
        bt_ref[:, here] = b.T.astype(bf16)
        ct_ref[:, here] = cc.T.astype(bf16)
        segc = segc_ref[here, 0:1]
        prev = segc_ref[here, 1:2]
        last = segc_ref[here, 2:3]
        same = segc == segr_ref[:, here]
        g = dot(cb, bb, ((1,), (1,)))
        gm_ref[pl.ds(c, 1)] = jnp.where(tri & same, g, 0.0)[None]
        raw = bcdt_ref[here, 2 * N : 2 * N + 128].astype(f32)[:, :H] + bias
        dt = jnp.maximum(raw, 0.0) + jnp.log1p(jnp.exp(-jnp.abs(raw)))
        a2 = neg_rate * dt
        cum = dot(trif, a2, precision=HIGHEST)
        end = cum[L - 1 : L]
        ein = jnp.where(segc == prev, jnp.exp2(cum), 0.0)
        lv = jnp.where(segc == last, jnp.exp2(end - cum), 0.0)
        dt_ref[here, :] = dt
        cumt = cum.T
        s0 = pl.multiple_of(c * (3 * L), L)
        for k in range(groups):
            cols = slice(HG * k, HG * (k + 1))
            cum4_ref[k, here, :] = cum[:, cols]
            cumr_ref[k, :, here] = cumt[cols]
            sc_ref[k, pl.ds(s0, L), :] = dt[:, cols].astype(bf16)
            sc_ref[k, pl.ds(s0 + L, L), :] = ein[:, cols].astype(bf16)
            sc_ref[k, pl.ds(s0 + 2 * L, L), :] = lv[:, cols].astype(bf16)
        return carry

    lax.fori_loop(0, nc, chunk, 0)


def prep(bcdt, taps, heads, masks, segc, segr, N, H):
    T = bcdt.shape[0]
    nc = T // L
    G = H // HG
    S = jax.ShapeDtypeStruct
    return pl.pallas_call(
        prep_kernel,
        out_shape=(S((T, N), bf16), S((T, N), bf16), S((N, T), bf16), S((N, T), bf16), S((T, 2 * N), f32),
                   S((nc, L, L), f32), S((G, T, HG), f32), S((G, HG, T), f32), S((G, 3 * T, HG), bf16), S((T, H), f32)),
        compiler_params=pltpu.CompilerParams(vmem_limit_bytes=60 << 20),
    )(bcdt, taps, heads, masks, segc, segr)


def lane_onehot(width, per):
    return (lax.broadcasted_iota(jnp.int32, (HG, width), 1) // per == lax.broadcasted_iota(jnp.int32, (HG, width), 0)).astype(bf16)


def half_masks(P):
    lane = lax.broadcasted_iota(jnp.int32, (1, 2 * P), 1)
    first = (lane < P).astype(f32)
    return first.astype(bf16), (1.0 - first).astype(bf16)


def decay(cum4, cumr, k):
    return jnp.exp2(jnp.minimum(cum4[:, k : k + 1] - cumr[k : k + 1, :], 0.0))


def fwd_kernel(u_ref, gate_ref, taps_ref, m_ref, b_ref, c_ref, bt_ref, gm_ref, cum4_ref, cumr_ref, sc_ref,
               gg_ref, ssq_ref, pre_ref, st_ref, state):
    T, W = u_ref.shape
    P = W // HG
    nc = T // L
    step = pl.program_id(0)
    taps = taps_ref[...]
    gain = taps[5:6]
    skip = taps[6:7]
    onehot = lane_onehot(W, P)
    ma, mb = half_masks(P)
    state[...] = jnp.zeros_like(state)

    @pl.when(step == 0)
    def _():
        ssq_ref[...] = jnp.zeros_like(ssq_ref)

    def chunk(c, carry):
        t0 = pl.multiple_of(c * L, L)
        here = pl.ds(t0, L)
        h0 = pl.multiple_of(jnp.maximum(t0 - 16, 0), 16)
        ext = jnp.concatenate([u_ref[pl.ds(h0, 16), :], u_ref[here, :]], axis=0).astype(f32)
        pre = conv_rows(ext, taps, m_ref[here, :], 16)
        pre_ref[here, :] = pre.astype(bf16)
        x = pre * sigmoid(pre)
        s0 = pl.multiple_of(c * (3 * L), L)
        exp = dot(sc_ref[0, pl.ds(s0, 3 * L), :], onehot)
        dtx, einx, lvx = exp[:L], exp[L : 2 * L], exp[2 * L :]
        xd = x * dtx
        xdb = xd.astype(bf16)
        gm = gm_ref[c]
        cum4 = cum4_ref[0, here, :]
        cumr = cumr_ref[0, :, here]
        sb = state[...].astype(bf16)
        st_ref[c] = sb
        inner = []
        for p in range(HG // 2):
            m0 = (decay(cum4, cumr, 2 * p) * gm).astype(bf16)
            m1 = (decay(cum4, cumr, 2 * p + 1) * gm).astype(bf16)
            xp = xdb[:, 2 * P * p : 2 * P * (p + 1)]
            inner.append(dot(jnp.concatenate([m0, m1], axis=1), jnp.concatenate([xp * ma, xp * mb], axis=0)))
        y = jnp.concatenate(inner, axis=1) + dot(c_ref[here, :], sb) * einx + skip * x
        state[...] = state[...] * einx[L - 1 : L] + dot(bt_ref[:, here], (xd * lvx).astype(bf16))
        gate = gate_ref[here, :].astype(f32)
        g = y * (gate * sigmoid(gate))
        gg_ref[here, :] = (g * gain).astype(bf16)
        g2 = g * g
        tot = g2[:, :128]
        for j in range(1, W // 128):
            tot = tot + g2[:, 128 * j : 128 * (j + 1)]
        ssq_ref[here, :] += tot
        return carry

    lax.fori_loop(0, nc, chunk, 0)


def fwd(zx, taps, masks, b, c, bt, gm, cum4, cumr, sc):
    T = zx.shape[0]
    E = zx.shape[1] // 2
    N = b.shape[1]
    G = cum4.shape[0]
    W = E // G
    nc = T // L
    S = jax.ShapeDtypeStruct
    col = lambda off: pl.BlockSpec((T, W), lambda g: (0, g + off))
    full = lambda a: pl.BlockSpec(a.shape, lambda g: (0,) * a.ndim)
    grp = lambda a: pl.BlockSpec((1,) + a.shape[1:], lambda g: (g, 0, 0))
    return pl.pallas_call(
        fwd_kernel,
        grid=(G,),
        in_specs=[col(G), col(0), pl.BlockSpec((8, W), lambda g: (0, g)), full(masks), full(b), full(c), full(bt), full(gm),
                  grp(cum4), grp(cumr), grp(sc)],
        out_specs=[col(0), pl.BlockSpec((T, 128), lambda g: (0, 0)), col(0), pl.BlockSpec((nc, N, W), lambda g: (0, 0, g))],
        out_shape=(S((T, E), bf16), S((T, 128), f32), S((T, E), bf16), S((nc, N, E), bf16)),
        scratch_shapes=[pltpu.VMEM((N, W), f32)],
        compiler_params=pltpu.CompilerParams(vmem_limit_bytes=60 << 20),
        cost_estimate=pl.CostEstimate(flops=T * E * (2 * L + 4 * N) * 2, bytes_accessed=T * E * 12, transcendentals=T * E * 4),
    )(zx, zx, taps, masks, b, c, bt, gm, cum4, cumr, sc)


def bwd_kernel(u_ref, gate_ref, pre_ref, dm_ref, rq_ref, taps_ref, m_ref, b_ref, c_ref, ct_ref, gm_ref, cum4_ref, cumr_ref, sc_ref, st_ref,
               du_ref, dgate_ref, dg_ref, db_ref, dc_ref, rs_ref, small_ref, kk_ref, ds, nxt, acc):
    T, W = u_ref.shape
    P = W // HG
    nc = T // L
    step = pl.program_id(0)
    taps = taps_ref[...]
    gain = taps[5:6]
    skip = taps[6:7]
    onehot = lane_onehot(W, P)
    ma, mb = half_masks(P)
    ds[...] = jnp.zeros_like(ds)
    nxt[...] = jnp.zeros_like(nxt)
    acc[...] = jnp.zeros_like(acc)

    @pl.when(step == 0)
    def _():
        dg_ref[...] = jnp.zeros_like(dg_ref)
        db_ref[...] = jnp.zeros_like(db_ref)
        dc_ref[...] = jnp.zeros_like(dc_ref)

    ri = lax.broadcasted_iota(jnp.int32, (4 * W, 16), 0)
    ci = lax.broadcasted_iota(jnp.int32, (4 * W, 16), 1)
    part = ri // W
    want = jnp.maximum(part - 1, 0) * HG + (ri % W) // P
    fold = (want == ci).astype(bf16)

    def eight(z):
        return jnp.sum(z.reshape(L // 8, 8, W), axis=0)

    def chunk(i, carry):
        c = nc - 1 - i
        t0 = pl.multiple_of(c * L, L)
        here = pl.ds(t0, L)
        u = u_ref[here, :].astype(f32)
        pre = pre_ref[here, :].astype(f32)
        sig = sigmoid(pre)
        x = pre * sig
        dsilu = sig + x * (1.0 - sig)
        s0 = pl.multiple_of(c * (3 * L), L)
        exp = dot(sc_ref[0, pl.ds(s0, 3 * L), :], onehot)
        dtx, einx, lvx = exp[:L], exp[L : 2 * L], exp[2 * L :]
        xdb = (x * dtx).astype(bf16)
        xd = xdb.astype(f32)
        gm = gm_ref[c]
        cum4 = cum4_ref[0, here, :]
        cumr = cumr_ref[0, :, here]
        sb = st_ref[c]
        es, ms, inner = [], [], []
        for p in range(HG // 2):
            e0 = decay(cum4, cumr, 2 * p)
            e1 = decay(cum4, cumr, 2 * p + 1)
            m0 = (e0 * gm).astype(bf16)
            m1 = (e1 * gm).astype(bf16)
            xp = xdb[:, 2 * P * p : 2 * P * (p + 1)]
            inner.append(dot(jnp.concatenate([m0, m1], axis=1), jnp.concatenate([xp * ma, xp * mb], axis=0)))
            es.append((e0, e1))
            ms.append((m0, m1))
        yn = jnp.concatenate(inner, axis=1) + dot(c_ref[here, :], sb) * einx
        y = yn + skip * x
        gate = gate_ref[here, :].astype(f32)
        sgate = sigmoid(gate)
        silu_g = gate * sgate
        g = y * silu_g
        r = rq_ref[here, 0:1]
        q = rq_ref[here, 1:2]
        dmr = dm_ref[here, :].astype(f32) * r
        dgg = gain * dmr - g * q
        dyb = (dgg * silu_g).astype(bf16)
        dy = dyb.astype(f32)
        dgate_ref[here, :] = (dgg * y * (sgate + silu_g * (1.0 - sgate))).astype(bf16)
        dxi = []
        dgc = dg_ref[c]
        for p in range(HG // 2):
            cols = slice(2 * P * p, 2 * P * (p + 1))
            dp = dyb[:, cols]
            dstack = jnp.concatenate([dp * ma, dp * mb], axis=0)
            dmm = dot(dstack, xdb[:, cols], ((1,), (1,)))
            dgc = dgc + dmm[:L] * es[p][0] + dmm[L:] * es[p][1]
            dxi.append(dot(jnp.concatenate(ms[p], axis=0), dstack, ((0,), (0,))))
        dg_ref[c] = dgc
        dxi = jnp.concatenate(dxi, axis=1)
        dsn = ds[...]
        dsb = dsn.astype(bf16)
        dye = (dy * einx).astype(bf16)
        dc_ref[here, :] += dot(dye, sb, ((1,), (1,)))
        kept = einx[L - 1 : L]
        kk_ref[pl.ds(c, 1), :] = kept * jnp.sum(sb.astype(f32) * dsn, axis=0, keepdims=True)
        db_ref[here, :] += dot((xd * lvx).astype(bf16), dsb, ((1,), (1,)))
        dxe = dot(b_ref[here, :], dsb) * lvx
        ds[...] = dsn * kept + dot(ct_ref[:, here], dye)
        dxd = dxi + dxe
        r1 = dy * yn - xd * dxi
        r1h = r1.astype(bf16)
        r1l = (r1 - r1h.astype(f32)).astype(bf16)
        rs_ref[0, here, :] = dot(jnp.concatenate([r1h, r1l, (xd * dxe).astype(bf16), (x * dxd).astype(bf16)], axis=1), fold)
        dpre = (dxd * dtx + skip * dy) * dsilu
        ext = jnp.concatenate([dpre, nxt[...]], axis=0)
        nxt[...] = dpre[:8]
        du = taps[3:4] * dpre
        acc[0:8, :] += eight(dmr * g)
        acc[8:16, :] += eight(dy * x)
        acc[16:24, :] += eight(dpre)
        acc[24:32, :] += eight(dpre * u)
        mrows = m_ref[pl.ds(t0, L + 8), :]
        for k in range(1, 4):
            sk = pltpu.roll(ext * mrows[:, k : k + 1], L + 8 - k, 0)[:L]
            du = du + taps[3 - k : 4 - k] * sk
            acc[24 + 8 * k : 32 + 8 * k, :] += eight(sk * u)
        du_ref[here, :] = du.astype(bf16)
        return carry

    lax.fori_loop(0, nc, chunk, 0)
    for j in range(7):
        small_ref[j : j + 1, :] = jnp.sum(acc[8 * j : 8 * j + 8, :], axis=0, keepdims=True)
    small_ref[7:8, :] = jnp.zeros((1, W), f32)


def bwd(zx, pre, dm, rq, taps, masks, b, c, ct, gm, cum4, cumr, sc, st):
    T = zx.shape[0]
    E = zx.shape[1] // 2
    N = b.shape[1]
    G = cum4.shape[0]
    W = E // G
    nc = T // L
    S = jax.ShapeDtypeStruct
    col = lambda off: pl.BlockSpec((T, W), lambda g: (0, g + off))
    full = lambda a: pl.BlockSpec(a.shape, lambda g: (0,) * a.ndim)
    whole = lambda s: pl.BlockSpec(s, lambda g: (0,) * len(s))
    grp = lambda a: pl.BlockSpec((1,) + a.shape[1:], lambda g: (g, 0, 0))
    masks = jnp.pad(masks, ((0, 8), (0, 0)))
    return pl.pallas_call(
        bwd_kernel,
        grid=(G,),
        in_specs=[col(G), col(0), col(0), col(0), full(rq), pl.BlockSpec((8, W), lambda g: (0, g)), full(masks), full(b), full(c),
                  full(ct), full(gm), grp(cum4), grp(cumr), grp(sc), pl.BlockSpec((nc, N, W), lambda g: (0, 0, g))],
        out_specs=[col(0), col(0), whole((nc, L, L)), whole((T, N)), whole((T, N)), pl.BlockSpec((1, T, 16), lambda g: (g, 0, 0)),
                   pl.BlockSpec((8, W), lambda g: (0, g)), pl.BlockSpec((nc, W), lambda g: (0, g))],
        out_shape=(S((T, E), bf16), S((T, E), bf16), S((nc, L, L), f32), S((T, N), f32), S((T, N), f32), S((G, T, 16), f32),
                   S((8, E), f32), S((nc, E), f32)),
        scratch_shapes=[pltpu.VMEM((N, W), f32), pltpu.VMEM((8, W), f32), pltpu.VMEM((56, W), f32)],
        compiler_params=pltpu.CompilerParams(vmem_limit_bytes=60 << 20),
        cost_estimate=pl.CostEstimate(flops=T * E * (8 * L + 12 * N), bytes_accessed=T * E * 16, transcendentals=T * E * 4),
    )(zx, zx, pre, dm, rq, taps, masks, b, c, ct, gm, cum4, cumr, sc, st)


def post_kernel(bcdt_ref, pre_ref, taps_ref, heads_ref, m_ref, segc_ref, segr_ref, b_ref, c_ref, dg_ref, db_ref, dc_ref, rs_ref, kk_ref, dt_ref,
                out_ref, small_ref, hs_ref, nxt, acc, hacc):
    T = bcdt_ref.shape[0]
    nc = T // L
    N = b_ref.shape[1]
    H = dt_ref.shape[1]
    G = H // HG
    taps = taps_ref[...]
    tri = (lax.broadcasted_iota(jnp.int32, (L, L), 0) >= lax.broadcasted_iota(jnp.int32, (L, L), 1))
    upper = (lax.broadcasted_iota(jnp.int32, (L, L), 0) <= lax.broadcasted_iota(jnp.int32, (L, L), 1)).astype(f32)
    strict = 1.0 - upper
    rate = -jnp.exp(heads_ref[0:1, :H])
    bias = heads_ref[1:2, :H]
    nxt[...] = jnp.zeros_like(nxt)
    acc[...] = jnp.zeros_like(acc)
    hacc[...] = jnp.zeros_like(hacc)

    def eight(z):
        return jnp.sum(z.reshape(L // 8, 8, z.shape[1]), axis=0)

    def chunk(i, carry):
        c = nc - 1 - i
        t0 = pl.multiple_of(c * L, L)
        here = pl.ds(t0, L)
        same = segc_ref[here, 0:1] == segr_ref[:, here]
        dg = jnp.where(tri & same, dg_ref[c], 0.0)
        dgb = dg.astype(bf16)
        dcv = dc_ref[here, :] + dot(dgb, b_ref[here, :])
        dbv = db_ref[here, :] + dot(dg.T.astype(bf16), c_ref[here, :])
        pre = pre_ref[here, :]
        sig = sigmoid(pre)
        dpre = jnp.concatenate([dbv, dcv], axis=1) * (sig + pre * sig * (1.0 - sig))
        v = bcdt_ref[here, : 2 * N].astype(f32)
        ext = jnp.concatenate([dpre, nxt[...]], axis=0)
        nxt[...] = dpre[:8]
        dv = taps[3:4] * dpre
        acc[0:8, :] += eight(dpre)
        acc[8:16, :] += eight(dpre * v)
        mrows = m_ref[pl.ds(t0, L + 8), :]
        for k in range(1, 4):
            sk = pltpu.roll(ext * mrows[:, k : k + 1], L + 8 - k, 0)[:L]
            dv = dv + taps[3 - k : 4 - k] * sk
            acc[8 + 8 * k : 16 + 8 * k, :] += eight(sk * v)
        out_ref[here, : 2 * N] = dv.astype(bf16)
        r1 = jnp.concatenate([rs_ref[k, here, 0:HG] for k in range(G)], axis=1)
        r2 = jnp.concatenate([rs_ref[k, here, HG : 2 * HG] for k in range(G)], axis=1)
        r3 = jnp.concatenate([rs_ref[k, here, 2 * HG : 3 * HG] for k in range(G)], axis=1)
        da = dot(upper, r1, precision=HIGHEST) + dot(strict, r2, precision=HIGHEST) + kk_ref[pl.ds(c, 1), :]
        dt = dt_ref[here, :]
        raw = bcdt_ref[here, 2 * N : 2 * N + 128].astype(f32)[:, :H] + bias
        ddt = (r3 + da * rate) * sigmoid(raw)
        hacc[0:8, :] += eight(da * rate * dt)
        hacc[8:16, :] += eight(ddt)
        out_ref[here, 2 * N :] = jnp.concatenate([ddt, jnp.zeros((L, out_ref.shape[1] - 2 * N - H), f32)], axis=1).astype(bf16)
        return carry

    lax.fori_loop(0, nc, chunk, 0)
    for j in range(5):
        small_ref[j : j + 1, :] = jnp.sum(acc[8 * j : 8 * j + 8, :], axis=0, keepdims=True)
    small_ref[5:8, :] = jnp.zeros((3, 2 * N), f32)
    for j in range(2):
        hs_ref[j : j + 1, :] = jnp.sum(hacc[8 * j : 8 * j + 8, :], axis=0, keepdims=True)


def post(bcdt, pre, taps, heads, masks, segc, segr, b, c, dg, db, dc, rs, kk, dt):
    T = bcdt.shape[0]
    N = b.shape[1]
    H = dt.shape[1]
    S = jax.ShapeDtypeStruct
    masks = jnp.pad(masks, ((0, 8), (0, 0)))
    return pl.pallas_call(
        post_kernel,
        out_shape=(S(bcdt.shape, bf16), S((8, 2 * N), f32), S((2, H), f32)),
        scratch_shapes=[pltpu.VMEM((8, 2 * N), f32), pltpu.VMEM((40, 2 * N), f32), pltpu.VMEM((16, H), f32)],
        compiler_params=pltpu.CompilerParams(vmem_limit_bytes=60 << 20),
    )(bcdt, pre, taps, heads, masks, segc, segr, b, c, dg, db, dc, rs, kk, dt)


def layer(hidden, grad_out, seg, w_zx, w_bcdt, w_out, conv, norm_gain, gate_gain, heads):
    T, D = hidden.shape
    E = w_out.shape[0]
    H = heads.shape[1]
    N = (conv.shape[1] - E) // 2
    rows = hidden.astype(f32)
    rinv = lax.rsqrt(jnp.mean(rows * rows, axis=-1, keepdims=True) + EPS)
    xhat = rows * rinv
    normed = (xhat * norm_gain).astype(bf16)
    zx = dot(normed, w_zx).astype(bf16)
    bcdt = dot(normed, w_bcdt).astype(bf16)
    pos = jnp.arange(T, dtype=jnp.int32)
    masks = jnp.stack([jnp.ones((T,), f32)] + [((jnp.roll(seg, k) == seg) & (pos >= k)).astype(f32) for k in range(1, 4)], axis=1)
    lastid = seg[L - 1 :: L]
    previd = jnp.concatenate([jnp.full((1,), -1, jnp.int32), lastid[:-1]])
    segc = jnp.stack([seg, jnp.repeat(previd, L), jnp.repeat(lastid, L)], axis=1)
    segr = seg[None, :]
    taps_u = jnp.concatenate([conv[:, :E], gate_gain[None], jnp.repeat(heads[2], E // H)[None], jnp.zeros((1, E), f32)], axis=0)
    taps_bc = jnp.concatenate([conv[:, E:], jnp.zeros((3, 2 * N), f32)], axis=0)
    heads_p = jnp.pad(heads, ((0, 5), (0, 128 - H)))
    b, c, bt, ct, pre_bc, gm, cum4, cumr, sc, dt = prep(bcdt, taps_bc, heads_p, masks, segc, segr, N, H)
    gg, ssq, pre, st = fwd(zx, taps_u, masks, b, c, bt, gm, cum4, cumr, sc)
    r = lax.rsqrt(jnp.sum(ssq, axis=1, keepdims=True) / E + EPS)
    output = (rows + r * dot(gg, w_out)).astype(bf16)
    dm = dot(grad_out, w_out, ((1,), (1,))).astype(bf16)
    gos = (grad_out.astype(f32) * r).astype(bf16)
    g_out = dot(gg, gos, ((0,), (0,))).astype(bf16)
    s = jnp.sum(gg.astype(f32) * dm.astype(f32), axis=1, keepdims=True)
    rq = jnp.concatenate([r, r * r * r * s / E], axis=1)
    du, dgate, dg, db, dc, rs, small, kk = bwd(zx, pre, dm, rq, taps_u, masks, b, c, ct, gm, cum4, cumr, sc, st)
    kkh = jnp.sum(kk.reshape(kk.shape[0], H, E // H), axis=2)
    dbcdt, small_bc, hs = post(bcdt, pre_bc, taps_bc, heads_p, masks, segc, segr, b, c, dg, db, dc, rs, kkh, dt)
    g_gate = dot(normed, dgate, ((0,), (0,))).astype(bf16)
    g_u = dot(normed, du, ((0,), (0,))).astype(bf16)
    g_bcdt = dot(normed, dbcdt, ((0,), (0,))).astype(bf16)
    bn = dot(dgate, w_zx[:, :E], ((1,), (1,))) + dot(du, w_zx[:, E:], ((1,), (1,))) + dot(dbcdt, w_bcdt, ((1,), (1,)))
    gb = bn * norm_gain
    d_rows = rinv * (gb - xhat * jnp.mean(gb * xhat, axis=-1, keepdims=True))
    grad_in = (grad_out.astype(f32) + d_rows).astype(bf16)
    d_norm = jnp.sum(bn * xhat, axis=0)
    d_conv_u = jnp.stack([small[6], small[5], small[4], small[3], small[2]])
    d_conv_bc = jnp.stack([small_bc[4], small_bc[3], small_bc[2], small_bc[1], small_bc[0]])
    d_conv = jnp.concatenate([d_conv_u, d_conv_bc], axis=1)
    d_heads = jnp.concatenate([hs, jnp.sum(small[1].reshape(1, H, E // H), axis=2)], axis=0)
    return output, grad_in, g_gate, g_u, g_bcdt, g_out, d_conv, d_norm, small[0], d_heads


AXES = ("dp", "fsdp")


def per_device(hidden, grad_out, segment_ids, w_zx, w_bc, w_dt, w_out, conv_params, norm_gain, gate_gain, head_params):
    n = lax.axis_size(AXES)
    E = w_out.shape[0] * n
    H = w_dt.shape[1]
    gather = lambda w, axis=0: lax.all_gather(w, AXES, axis=axis, tiled=True)
    scatter = lambda w, axis=0: lax.psum_scatter(w, AXES, scatter_dimension=axis, tiled=True)
    pad = 128 - H
    full_zx = gather(w_zx)
    full_bcdt = gather(jnp.concatenate([w_bc, w_dt, jnp.zeros((w_dt.shape[0], pad), bf16)], axis=1))
    full_out = gather(w_out)
    small = jnp.concatenate([conv_params.reshape(-1), norm_gain, gate_gain])
    smalls = gather(small[None])
    nc_, k1 = conv_params.shape[1], conv_params.shape[0]
    conv = smalls[:, : k1 * nc_].reshape(n, k1, nc_).transpose(1, 0, 2).reshape(k1, n * nc_).astype(f32)
    ng = smalls[:, k1 * nc_ : k1 * nc_ + norm_gain.shape[0]].reshape(-1).astype(f32)
    gg = smalls[:, k1 * nc_ + norm_gain.shape[0] :].reshape(-1).astype(f32)
    output, grad_in, g_gate, g_u, g_bcdt, g_out, d_conv, d_norm, d_gg, d_heads = layer(
        hidden, grad_out, segment_ids, full_zx, full_bcdt, full_out, conv, ng, gg, head_params)
    s_out = scatter(g_out).astype(f32)
    s_zx = scatter(jnp.concatenate([g_gate, g_u], axis=1)).astype(f32)
    s_bcdt = scatter(g_bcdt).astype(f32)
    rows = jnp.concatenate([d_conv.reshape(k1, n, nc_).transpose(1, 0, 2).reshape(n, -1), d_norm.reshape(n, -1), d_gg.reshape(n, -1)], axis=1)
    s_small = scatter(rows)[0]
    N2 = w_bc.shape[1]
    return (output, grad_in, s_zx, s_bcdt[:, :N2], s_bcdt[:, N2 : N2 + H], s_out, s_small[: k1 * nc_].reshape(k1, nc_),
            s_small[k1 * nc_ : k1 * nc_ + norm_gain.shape[0]], s_small[k1 * nc_ + norm_gain.shape[0] :], lax.psum(d_heads, AXES))


def solution(mesh):
    row, col, vec, rep = P(AXES, None), P(None, AXES), P(AXES), P()
    return jax.shard_map(
        per_device,
        mesh=mesh,
        in_specs=(row, row, vec, row, row, row, row, col, vec, vec, rep),
        out_specs=(row, row, row, row, row, row, col, vec, vec, rep),
        check_vma=False,
    )
```

time: 2210 us -> 1050 us (0.48)
  matrix products: 603 us -> 149 us
  local copies, waits for them, and re-layouts: 371 us -> 23.2 us
  other arithmetic: 296 us -> 31.6 us
  Pallas kernels: 0 us -> 179 us
  blocking collectives: 206 us -> 81.7 us
  waiting for transfers between devices: 645 us -> 564 us
  loops' own time: 58 us -> 0 us
    dot_general x80 -> x11, matrix products: 603 us -> 149 us  [dot(): lax.dot_general(a, b, (dims, ((), ())), preferred_element_type=f32, preci...]
    reduce_scatter x4 -> x3, waiting for transfers between devices: 643 us -> 448 us  [per_device(): lax.psum_scatter(w, AXES, scatter_dimension=axis, tiled=True)]
    pallas_call x0 -> x4, Pallas kernels: none -> 179 us  [the longest x1 102 us: bwd(): pl.pallas_call(bwd_kernel, grid=(G,), in_specs=[col(G), col(0), col(0), c...]
    reshape x28 -> x7, local copies, waits for them, and re-layouts: 133 us -> 2.74 us  [the longest x1 0.99 us: layer(): kkh = jnp.sum(kk.reshape(kk.shape[0], H, E // H), axis=2)]
    all_gather x3 -> x0, blocking collectives: 125 us -> none  [the longest x1 45.8 us: per_device(): lax.all_gather(w_bc, ('dp', 'fsdp'), axis=0, tiled=True)]
    all_gather x2 -> x3, waiting for transfers between devices: 0.01 us -> 112 us  [per_device(): gather = lambda w, axis=0: lax.all_gather(w, AXES, axis=axis, tiled=True)]
    reduce_sum x18 -> x4, other arithmetic: 104 us -> 2.75 us  [the longest x1 1.25 us: layer(): r = lax.rsqrt(jnp.sum(ssq, axis=1, keepdims=True) / E + EPS)]
    another operation x4 -> x0, loops' own time: 58 us -> none  [mixer(): final_state, scanned = lax.scan(jax.checkpoint(group_step), initial, sliced)]
  transfers between devices with their start and end apart: 7 -> 7, of which waited for: 3 -> 6; matrix products, arithmetic and copies ran while one was open for 21% -> 13% of each run, Pallas kernels for 0% -> 6%
where the time goes in v1:
time: 1050 us; the launch traced here: 1040 us
  waiting for transfers between devices  564 us (54%)
  Pallas kernels  179 us (17%)
  matrix products  149 us (14%)
  blocking collectives  81.7 us (8%)
  other arithmetic  31.6 us (3%)
  local copies, waits for them, and re-layouts  23.2 us (2%)
  between operations  14.8 us (1%)
    reduce_scatter x3, waiting for transfers between devices, per_device(): lax.psum_scatter(w, AXES, scatter_dimension=axis, tiled=True)  448 us
    dot_general x11, matrix products, dot(): lax.dot_general(a, b, (dims, ((), ())), preferred_element_type=f32, preci...  149 us
    all_gather x3, waiting for transfers between devices, per_device(): gather = lambda w, axis=0: lax.all_gather(w, AXES, axis=axis, tiled=True)  112 us
    pallas_call x1, Pallas kernels, bwd(): pl.pallas_call(bwd_kernel, grid=(G,), in_specs=[col(G), col(0), col(0), c...  102 us
    pallas_call x1, Pallas kernels, fwd(): pl.pallas_call(fwd_kernel, grid=(G,), in_specs=[col(G), col(0), pl.BlockS...  47.5 us
    unnamed x1, blocking collectives  42.5 us
    psum x1, blocking collectives, per_device(): lax.psum(d_heads, AXES)  39.2 us
  transfers between devices with their start and end apart: 7, of which 6 were waited for; matrix products, arithmetic and copies ran while one was open for 13% of the time, Pallas kernels for 6%

profile of v1, /device:TPU:0, one launch (start us, length us, event | category | flops | bytes accessed | tf_op | source)
XLA Modules:
  0.0 1044.1 jit_solution(13919948734887836548)
XLA Ops:
  15.0 42.5 %all-reduce.3 = bf16[21248]{0:T(1024)(128)(2,1)S(1)} all-reduce(bf16[21248]{0:T(1024)(128)(2,1)S(1)} %dynamic-update-slice), channel_id=2, replica_groups=mesh['dp'=8,'fsdp'=4] {'dp','fsdp'}, use_global_device_ids=true, to_apply=%add.3 | all-reduce | flops 21248 | bytes 84992
  69.7 4.0 convolution_convert_fusion.6.bcdt_ref
  73.7 17.3 %shard_map.186 = (bf16[1024,128]{1,0:T(8,128)(2,1)}, bf16[1024,128]{1,0:T(8,128)(2,1)}, bf16[128,1024]{1,0:T(8,128)(2,1)}, bf16[128,1024]{1,0:T(8,128)(2,1)}, f3...) custom-call(bf16[1024,384]{1,0:T(8,128)(2,1)} %convolution_convert_f, ...), custom_call_target="tpu_custom_call" | custom-call | tf_op jit(solution)/shard_map/pallas_call | solution.py:99
  91.1 103.0 %all-gather.5.cloned.1.call-done = bf16[1536,6144]{1,0:T(8,128)(2,1)} async-done(((bf16[48,6144]{1,0:T(8,128)(2,1)}), bf16[1536,6144]{1,0:T(8,128)(2,1)}) %all-gather.5.cloned.1.call-update) | async-done | bytes 18874384 | tf_op jit(solution)/shard_map/all_gather | solution.py:479
  194.1 24.9 %convolution_convert_fusion.3.u_ref.gate_ref = bf16[1024,6144]{1,0:T(8,128)(2,1)} fusion(bf16[1536,6144]{1,0:T(8,128)(2,1)} %all-gather.5.cloned.1.call-done, bf16[1024,1536]{1,0:T(8,128)(2,1)S(1)} %copy-done, f32[1536]{0:T(1024)S(1)} %reshape.133, f32[1024]{0:T(1024)S(1)} %add_rsqrt_fusion.1), kind=kOutput, calls=%fused_computation.5 | convolution fusion | flops 19339935744 | bytes 34613248 | tf_op jit(solution)/shard_map/dot_general | solution.py:18
  219.0 47.5 %shard_map.187 = (bf16[1024,3072]{1,0:T(8,128)(2,1)}, f32[1024,128]{1,0:T(8,128)}, bf16[1024,3072]{1,0:T(8,128)(2,1)}, bf16[8,128,3072]{2,1,0:T(8,128)(2,1)}) custom-call(bf16[1024,6144]{1,0:T(8,128)(2,1)} %convolution_convert_fusion.3.u_ref.gate_ref, bf16[1024,6144]{1,0:T(8,128)(2,1)} %convolution_convert_fusion.3.u_ref.gate_ref, ...), custom_call_target="tpu_custom_call" | custom-call | flops 4831838208 | bytes 37748736 | tf_op jit(solution)/shard_map/pallas_call | solution.py:188
  267.8 9.1 all-gather.9.cloned.1.call-done
  276.8 17.4 %multiply_reduce_fusion = (f32[1024]{0:T(1024)S(1)}, bf16[1024,3072]{1,0:T(8,128)(2,1)}) fusion(bf16[1024,3072]{1,0:T(8,128)(2,1)} %get-tuple-element.43, bf16[1024,1536]{1,0:T(8,128)(2,1)} %param.12, bf16[3072,1536]{1,0:T(8,128)(2,1)} %all-gather.9.cloned.1.call-done), kind=kOutput, calls=%fused_computation.1 | convolution fusion | flops 9679404032 | bytes 25169920 | tf_op jit(solution)/shard_map/dot_general | solution.py:18
  295.3 101.7 %shard_map.188 = (bf16[1024,3072]{1,0:T(8,128)(2,1)}, bf16[1024,3072]{1,0:T(8,128)(2,1)}, f32[8,128,128]{2,1,0:T(8,128)}, f32[1024,128]{1,0:T(8,128)}, f32[1024,...) custom-call(bf16[1024,6144]{1,0:T(8,128)(2,1)} %convolution_convert_fusion.3.u_ref.gate_ref, ...), custom_call_target="tpu_custom_call" | custom-call | flops 8053063680 | bytes 50331648 | tf_op jit(solution)/shard_map/pallas_call | solution.py:332
  400.2 12.6 %shard_map.189 = (bf16[1024,384]{1,0:T(8,128)(2,1)}, f32[8,256]{1,0:T(8,128)}, f32[2,48]{1,0:T(2,128)}) custom-call(bf16[1024,384]{1,0:T(8,128)(2,1)} %convolution_convert_fusion.6.bcdt_ref, f32[1024,256]{1,0:T(8,128)} %get-tuple-element.49.pre_ref, f32[8,256]{1,0:T(8,128)} %concatenate.48.taps_ref, f32[8,128]{1,0:T(8,128)} %pad.10.heads_ref, ...), custom_call_target="tpu_custom_call" | custom-call | tf_op jit(solution)/shard_map/pallas_call | solution.py:417
  412.8 5.9 fusion.35
  418.7 15.5 %fusion.4 = f32[1024,1536]{1,0:T(8,128)} fusion(bf16[1024,3072]{1,0:T(8,128)(2,1)} %get-tuple-element.48, bf16[1536,6144]{1,0:T(8,128)(2,1)} %all-gather.5.cloned.1.call-done), kind=kOutput, calls=%fused_computation.13 | convolution fusion | flops 9663676416 | bytes 22020096 | tf_op jit(solution)/shard_map/dot_general | solution.py:18
  434.2 21.0 %fusion.14 = (f32[1536]{0:T(1024)S(1)}, f32[1024]{0:T(1024)S(1)}, f32[1024,1536]{1,0:T(8,128)}) fusion(bf16[1024,1536]{1,0:T(8,128)(2,1)S(1)} %copy-done, f32[1024]{0:T(1024)S(1)} %add_rsqrt_fusion.1, f32[1536]{0:T(1024)S(1)} %reshape.133, f32[1024,1536]{1,0:T(8,128)} %fusion.35, f32[1024,1536]{1,0:T(8,128)} %fusion.4, ...), kind=kOutput, calls=%fused_computation.25 | convolution fusion | flops 9677829120 | bytes 37769216 | tf_op jit(solution)/shard_map/dot_general | solution.py:18
  456.5 4.1 convolution_convert_fusion.5
  460.7 15.7 %convolution_convert_fusion = bf16[3072,1536]{1,0:T(8,128)(2,1)} fusion(bf16[1024,3072]{1,0:T(8,128)(2,1)} %get-tuple-element.43, bf16[1024,1536]{1,0:T(8,128)(2,1)} %param.12, f32[1024]{0:T(1024)S(1)} %add_rsqrt_fusion), kind=kOutput, calls=%fused_computation.2 | convolution fusion | flops 9673113600 | bytes 18878464 | tf_op jit(solution)/shard_map/dot_general | solution.py:18
  476.5 12.8 %convolution_convert_fusion.1 = bf16[1536,3072]{1,0:T(8,128)(2,1)S(1)} fusion(bf16[1024,3072]{1,0:T(8,128)(2,1)} %get-tuple-element.48, bf16[1024,1536]{1,0:T(8,128)(2,1)S(1)} %copy-done, f32[1536]{0:T(1024)S(1)} %reshape.133, f32[1024]{0:T(1024)S(1)} %add_rsqrt_fusion.1), kind=kOutput, calls=%fused_computation.3 | convolution fusion | flops 9674686464 | bytes 18884608 | tf_op jit(solution)/shard_map/dot_general | solution.py:18
  489.3 12.6 %convolution_convert_fusion.2 = bf16[1536,3072]{1,0:T(8,128)(2,1)S(1)} fusion(bf16[1024,3072]{1,0:T(8,128)(2,1)} %get-tuple-element.47, bf16[1024,1536]{1,0:T(8,128)(2,1)S(1)} %copy-done, f32[1536]{0:T(1024)S(1)} %reshape.133, f32[1024]{0:T(1024)S(1)} %add_rsqrt_fusion.1), kind=kOutput, calls=%fused_computation.4 | convolution fusion | flops 9674686464 | bytes 18884608 | tf_op jit(solution)/shard_map/dot_general | solution.py:18
  501.9 12.6 %pad_maximum_fusion = bf16[1536,6144]{1,0:T(8,128)(2,1)} fusion(bf16[1536,3072]{1,0:T(8,128)(2,1)S(1)} %convolution_convert_fusion.1, bf16[1536,3072]{1,0:T(8,128)(2,1)S(1)} %convolution_convert_fusion.2), kind=kLoop, calls=%fused_computation | loop fusion | flops 37748736 | bytes 37748736 | tf_op jit(solution)/shard_map/concatenate | solution.py:494
  515.2 39.2 %psum.7 = f32[3,48]{1,0:T(4,128)} all-reduce(f32[3,48]{1,0:T(4,128)S(1)} %pad_maximum_fusion.6), channel_id=1, replica_groups=mesh['dp'=8,'fsdp'=4] {'dp','fsdp'}, use_global_device_ids=true, to_apply=%region_11.12 | all-reduce | flops 144 | bytes 1152 | tf_op jit(solution)/shard_map/psum | solution.py:500
  554.5 6.0 fusion.8
  560.4 15.5 %fusion.16 = bf16[1024,1536]{1,0:T(8,128)(2,1)} fusion(bf16[1024,1536]{1,0:T(8,128)(2,1)S(1)} %copy-done, bf16[1024,3072]{1,0:T(8,128)(2,1)} %get-tuple-element.43, bf16[3072,1536]{1,0:T(8,128)(2,1)} %all-gather.9.cloned.1.call-done, f32[1024]{0:T(1024)S(1)} %add_rsqrt_fusion), kind=kOutput, calls=%fused_computation.27 | convolution fusion | flops 9669967872 | bytes 22024192 | tf_op jit(solution)/shard_map/dot_general | solution.py:18
  581.8 99.5 %reduce-scatter.6.cloned.1.call-done = bf16[48,384]{1,0:T(8,128)(2,1)} async-done(((bf16[1536,384]{1,0:T(8,128)(2,1)}), bf16[48,384]{1,0:T(8,128)(2,1)}) %reduce-scatter.6.cloned.1.call-update) | async-done | bytes 36880 | tf_op jit(solution)/shard_map/reduce_scatter | solution.py:480
  684.0 138.4 %reduce-scatter.8.cloned.1.call-done = bf16[96,1536]{1,0:T(8,128)(2,1)} async-done(((bf16[3072,1536]{1,0:T(8,128)(2,1)}), bf16[96,1536]{1,0:T(8,128)(2,1)}) %reduce-scatter.8.cloned.1.call-update) | async-done | bytes 294928 | tf_op jit(solution)/shard_map/reduce_scatter | solution.py:480
  824.2 210.4 %reduce-scatter.4.cloned.1.call-done = bf16[48,6144]{1,0:T(8,128)(2,1)} async-done(((bf16[1536,6144]{1,0:T(8,128)(2,1)}), bf16[48,6144]{1,0:T(8,128)(2,1)}) %reduce-scatter.4.cloned.1.call-update) | async-done | bytes 589840 | tf_op jit(solution)/shard_map/reduce_scatter | solution.py:480
  (93 shorter events, 39.9 us)
Async XLA Ops:
  7.2 61.1 %copy-start = (bf16[1024,1536]{1,0:T(8,128)(2,1)S(1)}, bf16[1024,1536]{1,0:T(8,128)(2,1)}, u32[]{:S(2)}) copy-start(bf16[1024,1536]{1,0:T(8,128)(2,1)} %param.11) | copy-start | bytes 9437188
  7.2 62.5 %all-gather.7.cloned.1.call-start = ((), (), s32[]{:S(2)}) async-start(), calls=%async_computation.4 | async-start | bytes 1216512 | tf_op jit(solution)/shard_map/all_gather | solution.py:479
  8.9 185.2 %all-gather.5.cloned.1.call-start = ((), (), s32[]{:S(2)}) async-start(), calls=%async_computation.3 | async-start | bytes 19464192 | tf_op jit(solution)/shard_map/all_gather | solution.py:479
  9.6 267.2 %all-gather.9.cloned.1.call-start = ((), (), s32[]{:S(2)}) async-start(), calls=%async_computation.5 | async-start | bytes 9732096 | tf_op jit(solution)/shard_map/all_gather | solution.py:479
  10.4 567.4 %all-reduce.7.cloned.1.call-start = ((), (), s32[]{:S(2)}) async-start(), calls=%async_computation.9 | async-start | bytes 196608
  434.2 21.1 %copy-start.1 = (f32[8,256]{1,0:T(8,128)S(1)}, f32[8,256]{1,0:T(8,128)}, u32[]{:S(2)}) copy-start(f32[8,256]{1,0:T(8,128)} %get-tuple-element.58) | copy-start | bytes 24580
  456.5 224.8 %reduce-scatter.6.cloned.1.call-start = ((), (), s32[]{:S(2)}) async-start(), calls=%async_computation.7 | async-start | bytes 1216512 | tf_op jit(solution)/shard_map/reduce_scatter | solution.py:480
  460.6 361.7 %reduce-scatter.8.cloned.1.call-start = ((), (), s32[]{:S(2)}) async-start(), calls=%async_computation.8 | async-start | bytes 9732096 | tf_op jit(solution)/shard_map/reduce_scatter | solution.py:480
  476.4 558.2 %reduce-scatter.4.cloned.1.call-start = ((), (), s32[]{:S(2)}) async-start(), calls=%async_computation.6 | async-start | bytes 19464192 | tf_op jit(solution)/shard_map/reduce_scatter | solution.py:480
  514.5 0.7 copy-start.2
Sparse Core Ops, SparseCore 0:
  11.5 56.7 all-gather.6
  71.1 122.9 all-gather.4
  197.0 79.7 all-gather.8
  456.6 121.1 all-reduce.6
  583.3 97.9 reduce-scatter.5
  687.1 135.2 reduce-scatter.7
  828.8 205.8 reduce-scatter.3

commit v2 on v1

--- a/solution.py
+++ b/solution.py
@@ -174,9 +174,8 @@
     lax.fori_loop(0, nc, chunk, 0)
 
 
-def fwd(zx, taps, masks, b, c, bt, gm, cum4, cumr, sc):
-    T = zx.shape[0]
-    E = zx.shape[1] // 2
+def fwd(u, gate, taps, masks, b, c, bt, gm, cum4, cumr, sc):
+    T, E = gate.shape
     N = b.shape[1]
     G = cum4.shape[0]
     W = E // G
@@ -188,14 +187,14 @@
     return pl.pallas_call(
         fwd_kernel,
         grid=(G,),
-        in_specs=[col(G), col(0), pl.BlockSpec((8, W), lambda g: (0, g)), full(masks), full(b), full(c), full(bt), full(gm),
+        in_specs=[col(0), col(0), pl.BlockSpec((8, W), lambda g: (0, g)), full(masks), full(b), full(c), full(bt), full(gm),
                   grp(cum4), grp(cumr), grp(sc)],
         out_specs=[col(0), pl.BlockSpec((T, 128), lambda g: (0, 0)), col(0), pl.BlockSpec((nc, N, W), lambda g: (0, 0, g))],
         out_shape=(S((T, E), bf16), S((T, 128), f32), S((T, E), bf16), S((nc, N, E), bf16)),
         scratch_shapes=[pltpu.VMEM((N, W), f32)],
         compiler_params=pltpu.CompilerParams(vmem_limit_bytes=60 << 20),
         cost_estimate=pl.CostEstimate(flops=T * E * (2 * L + 4 * N) * 2, bytes_accessed=T * E * 12, transcendentals=T * E * 4),
-    )(zx, zx, taps, masks, b, c, bt, gm, cum4, cumr, sc)
+    )(u, gate, taps, masks, b, c, bt, gm, cum4, cumr, sc)
 
 
 def bwd_kernel(u_ref, gate_ref, pre_ref, dm_ref, rq_ref, taps_ref, m_ref, b_ref, c_ref, ct_ref, gm_ref, cum4_ref, cumr_ref, sc_ref, st_ref,
@@ -316,9 +315,8 @@
     small_ref[7:8, :] = jnp.zeros((1, W), f32)
 
 
-def bwd(zx, pre, dm, rq, taps, masks, b, c, ct, gm, cum4, cumr, sc, st):
-    T = zx.shape[0]
-    E = zx.shape[1] // 2
+def bwd(u, gate, pre, dm, rq, taps, masks, b, c, ct, gm, cum4, cumr, sc, st):
+    T, E = gate.shape
     N = b.shape[1]
     G = cum4.shape[0]
     W = E // G
@@ -332,7 +330,7 @@
     return pl.pallas_call(
         bwd_kernel,
         grid=(G,),
-        in_specs=[col(G), col(0), col(0), col(0), full(rq), pl.BlockSpec((8, W), lambda g: (0, g)), full(masks), full(b), full(c),
+        in_specs=[col(0), col(0), col(0), col(0), full(rq), pl.BlockSpec((8, W), lambda g: (0, g)), full(masks), full(b), full(c),
                   full(ct), full(gm), grp(cum4), grp(cumr), grp(sc), pl.BlockSpec((nc, N, W), lambda g: (0, 0, g))],
         out_specs=[col(0), col(0), whole((nc, L, L)), whole((T, N)), whole((T, N)), pl.BlockSpec((1, T, 16), lambda g: (g, 0, 0)),
                    pl.BlockSpec((8, W), lambda g: (0, g)), pl.BlockSpec((nc, W), lambda g: (0, g))],
@@ -341,7 +339,7 @@
         scratch_shapes=[pltpu.VMEM((N, W), f32), pltpu.VMEM((8, W), f32), pltpu.VMEM((56, W), f32)],
         compiler_params=pltpu.CompilerParams(vmem_limit_bytes=60 << 20),
         cost_estimate=pl.CostEstimate(flops=T * E * (8 * L + 12 * N), bytes_accessed=T * E * 16, transcendentals=T * E * 4),
-    )(zx, zx, pre, dm, rq, taps, masks, b, c, ct, gm, cum4, cumr, sc, st)
+    )(u, gate, pre, dm, rq, taps, masks, b, c, ct, gm, cum4, cumr, sc, st)
 
 
 def post_kernel(bcdt_ref, pre_ref, taps_ref, heads_ref, m_ref, segc_ref, segr_ref, b_ref, c_ref, dg_ref, db_ref, dc_ref, rs_ref, kk_ref, dt_ref,
@@ -422,88 +420,486 @@
     )(bcdt, pre, taps, heads, masks, segc, segr, b, c, dg, db, dc, rs, kk, dt)
 
 
-def layer(hidden, grad_out, seg, w_zx, w_bcdt, w_out, conv, norm_gain, gate_gain, heads):
+AXES = ("dp", "fsdp")
+MESH = pl.DeviceIdType.MESH
+
+
+class Place:
+    def __init__(self, nd, nf):
+        self.zn, self.nf = nd // 2, nf
+        d, f = lax.axis_index("dp"), lax.axis_index("fsdp")
+        self.z, self.y = d // 2, d % 2
+        self.x, self.c = f // 2, f % 2
+
+    def dev(self, z, y, x, c):
+        return (z * 2 + y, x * 2 + c)
+
+    def idx(self, z, y, x, c):
+        return (z * 2 + y) * self.nf + x * 2 + c
+
+    def barrier(self):
+        z, y, x, c, zn = self.z, self.y, self.x, self.c, self.zn
+        sem = pltpu.get_barrier_semaphore()
+        for there in ((z, y, 1 - x, c), (z, 1 - y, x, c), (z, y, x, 1 - c)):
+            pl.semaphore_signal(sem, inc=1, device_id=self.dev(*there), device_id_type=MESH)
+
+        @pl.when(z > 0)
+        def _():
+            pl.semaphore_signal(sem, inc=1, device_id=self.dev(z - 1, y, x, c), device_id_type=MESH)
+
+        @pl.when(z < zn - 1)
+        def _():
+            pl.semaphore_signal(sem, inc=1, device_id=self.dev(z + 1, y, x, c), device_id_type=MESH)
+
+        pl.semaphore_wait(sem, 3 + (z + zn - 1) // zn + (2 * zn - 2 - z) // zn)
+
+
+def gather_kernel(nd, nf, src_ref, out_ref, own_sem, z_send, z_recv, x_send, x_recv, y_send, y_recv, dx_send, dx_recv, dy_send, dy_recv, c_send, c_recv):
+    at = Place(nd, nf)
+    z, y, x, c, zn = at.z, at.y, at.x, at.c, at.zn
+    half = out_ref.shape[2] // 256 * 128
+    lo, hi = pl.ds(0, half), pl.ds(half, out_ref.shape[2] - half)
+    at.barrier()
+
+    def copy(block, to, send, recv, cols=None, src=None):
+        ref = out_ref.at[block] if cols is None else out_ref.at[block, :, cols]
+        return pltpu.make_async_remote_copy(src_ref=ref if src is None else src, dst_ref=ref, send_sem=send, recv_sem=recv,
+                                            device_id=at.dev(*to), device_id_type=MESH)
+
+    def block(zs, col):
+        return at.idx(zs, 1 - y if col & 2 else y, 1 - x if col & 1 else x, c)
+
+    def up(zs, src=None):
+        return copy(block(zs, 0), (z + 1, y, x, c), z_send.at[0, zs], z_recv.at[zs], src=src)
+
+    def down(zs, src=None):
+        return copy(block(zs, 0), (z - 1, y, x, c), z_send.at[1, zs], z_recv.at[zs], src=src)
+
+    def to_x(zs, src=None):
+        return copy(block(zs, 0), (z, y, 1 - x, c), x_send.at[zs], x_recv.at[zs], src=src)
+
+    def to_y(zs, src=None):
+        return copy(block(zs, 0), (z, 1 - y, x, c), y_send.at[zs], y_recv.at[zs], src=src)
+
+    def diag_y(zs):
+        return copy(block(zs, 1), (z, 1 - y, x, c), dy_send.at[zs], dy_recv.at[zs], lo)
+
+    def diag_x(zs):
+        return copy(block(zs, 2), (z, y, 1 - x, c), dx_send.at[zs], dx_recv.at[zs], hi)
+
+    def to_core(zs, col, src=None):
+        return copy(block(zs, col), (z, y, x, 1 - c), c_send.at[zs, col], c_recv.at[zs, col], src=src)
+
+    own = pltpu.make_async_copy(src_ref, out_ref.at[block(z, 0)], own_sem)
+    own.start()
+
+    @pl.when(z < zn - 1)
+    def _():
+        up(z, src_ref).start()
+
+    @pl.when(z > 0)
+    def _():
+        down(z, src_ref).start()
+
+    to_x(z, src_ref).start()
+    to_y(z, src_ref).start()
+    to_core(z, 0, src_ref).start()
+
+    def each(dist, fn):
+        if dist == 0:
+            fn(z, 0)
+            return
+
+        @pl.when(z - dist >= 0)
+        def _():
+            fn(z - dist, 1)
+
+        @pl.when(z + dist < zn)
+        def _():
+            fn(z + dist, -1)
+
+    def from_z(zs, way):
+        copy(block(zs, 0), (z, y, x, c), z_send.at[0, zs], z_recv.at[zs]).wait_recv()
+        if way > 0:
+            @pl.when(z < zn - 1)
+            def _():
+                up(zs).start()
+        else:
+            @pl.when(z > 0)
+            def _():
+                down(zs).start()
+        to_x(zs).start()
+        to_y(zs).start()
+        to_core(zs, 0).start()
+
+    def from_xy(zs, way):
+        to_x(zs).wait_recv()
+        diag_y(zs).start()
+        to_core(zs, 1).start()
+        to_y(zs).wait_recv()
+        diag_x(zs).start()
+        to_core(zs, 2).start()
+
+    def from_diag(zs, way):
+        diag_y(zs).wait_recv()
+        diag_x(zs).wait_recv()
+        to_core(zs, 3).start()
+
+    for dist in range(zn):
+        if dist:
+            each(dist, from_z)
+        each(dist, from_xy)
+    for dist in range(zn):
+        each(dist, from_diag)
+    own.wait()
+
+    def sent(zs, way):
+        for col in range(4):
+            to_core(zs, col).wait_recv()
+            to_core(zs, col).wait_send()
+        to_x(zs).wait_send()
+        to_y(zs).wait_send()
+        diag_x(zs).wait_send()
+        diag_y(zs).wait_send()
+        if way >= 0:
+            @pl.when(z < zn - 1)
+            def _():
+                up(zs).wait_send()
+        if way <= 0:
+            @pl.when(z > 0)
+            def _():
+                down(zs).wait_send()
+
+    for dist in range(zn):
+        each(dist, sent)
+
+
+def gather_rows(shard, nd, nf, cid):
+    zn = nd // 2
+    D = pltpu.SemaphoreType.DMA
+    return pl.pallas_call(
+        functools.partial(gather_kernel, nd, nf),
+        out_shape=jax.ShapeDtypeStruct((nd * nf,) + shard.shape, shard.dtype),
+        in_specs=[pl.BlockSpec(memory_space=pl.ANY)],
+        out_specs=pl.BlockSpec(memory_space=pl.ANY),
+        scratch_shapes=[D(()), D((2, zn)), D((zn,)), D((zn,)), D((zn,)), D((zn,)), D((zn,)), D((zn,)), D((zn,)), D((zn,)), D((zn,)),
+                        D((zn, 4)), D((zn, 4))],
+        compiler_params=pltpu.CompilerParams(collective_id=cid, has_side_effects=True),
+    )(shard)
+
+
+def scatter_kernel(nd, nf, parts, *refs):
+    scatter_body(nd, nf, refs[:parts], *refs[parts:])
+
+
+def scatter_body(nd, nf, g_refs, out_ref, acc, c_in, d_in, xy_in, z_in,
+                   load_sem, c_send, c_recv, dx_send, dx_recv, dy_send, dy_recv, x_send, x_recv, y_send, y_recv, z_send, z_recv):
+    at = Place(nd, nf)
+    z, y, x, c, zn = at.z, at.y, at.x, at.c, at.zn
+    cols = out_ref.shape[1]
+    offs = [sum(r.shape[2] for r in g_refs[:k]) for k in range(len(g_refs))]
+    half = cols // 256 * 128
+    lo, hi = pl.ds(0, half), pl.ds(half, cols - half)
+    at.barrier()
+
+    def idx(zs, col, core):
+        return at.idx(zs, 1 - y if col & 2 else y, 1 - x if col & 1 else x, core)
+
+    def remote(src, dst, to, send, recv):
+        return pltpu.make_async_remote_copy(src_ref=src, dst_ref=dst, send_sem=send, recv_sem=recv, device_id=at.dev(*to), device_id_type=MESH)
+
+    def load(zs, col):
+        return [pltpu.make_async_copy(r.at[idx(zs, col, c)], acc.at[zs, col, :, pl.ds(o, r.shape[2])], load_sem.at[zs, col, k])
+                for k, (r, o) in enumerate(zip(g_refs, offs))]
+
+    def core(zs, col):
+        return [remote(r.at[idx(zs, col, 1 - c)], c_in.at[zs, col, :, pl.ds(o, r.shape[2])], (z, y, x, 1 - c),
+                       c_send.at[zs, col, k], c_recv.at[zs, col, k])
+                for k, (r, o) in enumerate(zip(g_refs, offs))]
+
+    def diag_x(zs):
+        return remote(acc.at[zs, 3, :, lo], d_in.at[0, zs, :, lo], (z, y, 1 - x, c), dx_send.at[zs], dx_recv.at[zs])
+
+    def diag_y(zs):
+        return remote(acc.at[zs, 3, :, hi], d_in.at[1, zs, :, hi], (z, 1 - y, x, c), dy_send.at[zs], dy_recv.at[zs])
+
+    def to_x(zs):
+        return remote(acc.at[zs, 1], xy_in.at[0, zs], (z, y, 1 - x, c), x_send.at[zs], x_recv.at[zs])
+
+    def to_y(zs):
+        return remote(acc.at[zs, 2], xy_in.at[1, zs], (z, 1 - y, x, c), y_send.at[zs], y_recv.at[zs])
+
+    def up(zs):
+        return remote(acc.at[zs, 0], z_in.at[0, zs], (z + 1, y, x, c), z_send.at[zs], z_recv.at[0, zs])
+
+    def down(zs):
+        return remote(acc.at[zs, 0], z_in.at[1, zs], (z - 1, y, x, c), z_send.at[zs], z_recv.at[1, zs])
+
+    def each(dist, fn):
+        if dist == 0:
+            fn(z)
+            return
+
+        @pl.when(z - dist >= 0)
+        def _():
+            fn(z - dist)
+
+        @pl.when(z + dist < zn)
+        def _():
+            fn(z + dist)
+
+    order = list(range(zn - 1, -1, -1))
+    for col in (3, 1, 2, 0):
+        for dist in order:
+            def begin(zs):
+                for cp in core(zs, col) + load(zs, col):
+                    cp.start()
+            each(dist, begin)
+
+    def ready(zs, col):
+        for cp in load(zs, col):
+            cp.wait()
+        for cp in core(zs, col):
+            cp.wait_recv()
+
+    def diag(zs):
+        ready(zs, 3)
+        acc[zs, 3] = acc[zs, 3] + c_in[zs, 3]
+        diag_x(zs).start()
+        diag_y(zs).start()
+
+    def sides(zs):
+        ready(zs, 1)
+        diag_y(zs).wait_recv()
+        acc[zs, 1, :, lo] = acc[zs, 1, :, lo] + c_in[zs, 1, :, lo]
+        acc[zs, 1, :, hi] = (acc[zs, 1, :, hi].astype(f32) + c_in[zs, 1, :, hi].astype(f32) + d_in[1, zs, :, hi].astype(f32)).astype(bf16)
+        to_x(zs).start()
+        ready(zs, 2)
+        diag_x(zs).wait_recv()
+        acc[zs, 2, :, lo] = (acc[zs, 2, :, lo].astype(f32) + c_in[zs, 2, :, lo].astype(f32) + d_in[0, zs, :, lo].astype(f32)).astype(bf16)
+        acc[zs, 2, :, hi] = acc[zs, 2, :, hi] + c_in[zs, 2, :, hi]
+        to_y(zs).start()
+
+    def column(zs):
+        ready(zs, 0)
+        to_x(zs).wait_recv()
+        to_y(zs).wait_recv()
+        return (acc[zs, 0].astype(f32) + c_in[zs, 0].astype(f32)) + (xy_in[0, zs].astype(f32) + xy_in[1, zs].astype(f32))
+
+    def pass_on(zs):
+        total = column(zs)
+
+        @pl.when(zs > z)
+        def _():
+            @pl.when(z > 0)
+            def _():
+                up(zs).wait_recv()
+                acc[zs, 0] = (total + z_in[0, zs].astype(f32)).astype(bf16)
+
+            @pl.when(z == 0)
+            def _():
+                acc[zs, 0] = total.astype(bf16)
+            up(zs).start()
+
+        @pl.when(zs < z)
+        def _():
+            @pl.when(z < zn - 1)
+            def _():
+                down(zs).wait_recv()
+                acc[zs, 0] = (total + z_in[1, zs].astype(f32)).astype(bf16)
+
+            @pl.when(z == zn - 1)
+            def _():
+                acc[zs, 0] = total.astype(bf16)
+            down(zs).start()
+
+    for dist in order:
+        each(dist, diag)
+    for dist in order:
+        each(dist, sides)
+    for dist in order[:-1]:
+        each(dist, pass_on)
+    out_ref[...] = column(z)
+
+    @pl.when(z > 0)
+    def _():
+        up(z).wait_recv()
+        out_ref[...] += z_in[0, z].astype(f32)
+
+    @pl.when(z < zn - 1)
+    def _():
+        down(z).wait_recv()
+        out_ref[...] += z_in[1, z].astype(f32)
+
+    def sent(zs):
+        for col in range(4):
+            for cp in core(zs, col):
+                cp.wait_send()
+        diag_x(zs).wait_send()
+        diag_y(zs).wait_send()
+        to_x(zs).wait_send()
+        to_y(zs).wait_send()
+
+    for dist in order:
+        each(dist, sent)
+        if dist:
+            each(dist, lambda zs: up(zs).wait_send())
+
+
+def scatter_rows(gs, nd, nf, cid):
+    zn, parts = nd // 2, len(gs)
+    rows, cols = gs[0].shape[1], sum(g.shape[2] for g in gs)
+    D = pltpu.SemaphoreType.DMA
+    V = pltpu.VMEM
+    return pl.pallas_call(
+        functools.partial(scatter_kernel, nd, nf, parts),
+        out_shape=jax.ShapeDtypeStruct((rows, cols), f32),
+        in_specs=[pl.BlockSpec(memory_space=pl.ANY)] * parts,
+        out_specs=pl.BlockSpec(memory_space=pltpu.VMEM),
+        scratch_shapes=[V((zn, 4, rows, cols), bf16), V((zn, 4, rows, cols), bf16), V((2, zn, rows, cols), bf16), V((2, zn, rows, cols), bf16),
+                        V((2, zn, rows, cols), bf16), D((zn, 4, parts)), D((zn, 4, parts)), D((zn, 4, parts)), D((zn,)), D((zn,)), D((zn,)), D((zn,)), D((zn,)), D((zn,)),
+                        D((zn,)), D((zn,)), D((zn,)), D((2, zn))],
+        compiler_params=pltpu.CompilerParams(collective_id=cid, has_side_effects=True, vmem_limit_bytes=62 << 20),
+    )(*gs)
+
+
+def exchange_kernel(nd, nf, g_ref, out_ref, got, send, recv):
+    n = nd * nf
+    me = lax.axis_index("dp") * nf + lax.axis_index("fsdp")
+    sem = pltpu.get_barrier_semaphore()
+
+    def peer(k):
+        return lax.rem(me + k, n)
+
+    def greet(k, carry):
+        pl.semaphore_signal(sem, inc=1, device_id=(peer(k) // nf, peer(k) % nf), device_id_type=MESH)
+        return carry
+
+    lax.fori_loop(1, n, greet, 0)
+    pl.semaphore_wait(sem, n - 1)
+
+    def copy(k):
+        p = peer(k)
+        return pltpu.make_async_remote_copy(src_ref=g_ref.at[p], dst_ref=got.at[k], send_sem=send.at[k], recv_sem=recv.at[k],
+                                            device_id=(p // nf, p % nf), device_id_type=MESH)
+
+    def begin(k, carry):
+        copy(k).start()
+        return carry
+
+    lax.fori_loop(1, n, begin, 0)
+
+    def add(k, total):
+        copy(k).wait_recv()
+        return total + got[k]
+
+    out_ref[...] = lax.fori_loop(1, n, add, g_ref[me])
+
+    def end(k, carry):
+        copy(k).wait_send()
+        return carry
+
+    lax.fori_loop(1, n, end, 0)
+
+
+def exchange(g, nd, nf, cid):
+    n = nd * nf
+    D = pltpu.SemaphoreType.DMA
+    vm = pl.BlockSpec(memory_space=pltpu.VMEM)
+    return pl.pallas_call(
+        functools.partial(exchange_kernel, nd, nf),
+        out_shape=jax.ShapeDtypeStruct(g.shape[1:], g.dtype),
+        in_specs=[vm],
+        out_specs=vm,
+        scratch_shapes=[pltpu.VMEM(g.shape, g.dtype), D((n,)), D((n,))],
+        compiler_params=pltpu.CompilerParams(collective_id=cid, has_side_effects=True),
+    )(g)
+
+
+def layer(nd, nf, hidden, grad_out, seg, shard_a, shard_gate, shard_out, head_params, sizes):
+    n = nd * nf
+    E, N, H, K1, S = sizes
     T, D = hidden.shape
-    E = w_out.shape[0]
-    H = heads.shape[1]
-    N = (conv.shape[1] - E) // 2
+    wide = 2 * N + 128
+    full_gate = lax.all_gather(shard_gate, AXES, axis=0, tiled=True)
+    full_out = lax.all_gather(shard_out, AXES, axis=0, tiled=True)
+    full_a = gather_rows(shard_a, nd, nf, 0)
+    off = E + 2 * N + H
+    flat = full_a[:, :, off : off + S].reshape(n, -1)
+    ncol, nrow, ngate = (E + 2 * N) // n, D // n, E // n
+    conv = flat[:, : K1 * ncol].reshape(n, K1, ncol).transpose(1, 0, 2).reshape(K1, n * ncol).astype(f32)
+    norm_gain = flat[:, K1 * ncol : K1 * ncol + nrow].reshape(-1).astype(f32)
+    gate_gain = flat[:, K1 * ncol + nrow : K1 * ncol + nrow + ngate].reshape(-1).astype(f32)
+    full_a = full_a.reshape(D, E + wide)
     rows = hidden.astype(f32)
     rinv = lax.rsqrt(jnp.mean(rows * rows, axis=-1, keepdims=True) + EPS)
     xhat = rows * rinv
     normed = (xhat * norm_gain).astype(bf16)
-    zx = dot(normed, w_zx).astype(bf16)
-    bcdt = dot(normed, w_bcdt).astype(bf16)
+    ubc = dot(normed, full_a).astype(bf16)
+    gate = dot(normed, full_gate).astype(bf16)
+    bcdt = ubc[:, E:]
     pos = jnp.arange(T, dtype=jnp.int32)
     masks = jnp.stack([jnp.ones((T,), f32)] + [((jnp.roll(seg, k) == seg) & (pos >= k)).astype(f32) for k in range(1, 4)], axis=1)
     lastid = seg[L - 1 :: L]
     previd = jnp.concatenate([jnp.full((1,), -1, jnp.int32), lastid[:-1]])
     segc = jnp.stack([seg, jnp.repeat(previd, L), jnp.repeat(lastid, L)], axis=1)
     segr = seg[None, :]
-    taps_u = jnp.concatenate([conv[:, :E], gate_gain[None], jnp.repeat(heads[2], E // H)[None], jnp.zeros((1, E), f32)], axis=0)
+    taps_u = jnp.concatenate([conv[:, :E], gate_gain[None], jnp.repeat(head_params[2], E // H)[None], jnp.zeros((1, E), f32)], axis=0)
     taps_bc = jnp.concatenate([conv[:, E:], jnp.zeros((3, 2 * N), f32)], axis=0)
-    heads_p = jnp.pad(heads, ((0, 5), (0, 128 - H)))
+    heads_p = jnp.pad(head_params, ((0, 5), (0, 128 - H)))
     b, c, bt, ct, pre_bc, gm, cum4, cumr, sc, dt = prep(bcdt, taps_bc, heads_p, masks, segc, segr, N, H)
-    gg, ssq, pre, st = fwd(zx, taps_u, masks, b, c, bt, gm, cum4, cumr, sc)
+    gg, ssq, pre, st = fwd(ubc, gate, taps_u, masks, b, c, bt, gm, cum4, cumr, sc)
     r = lax.rsqrt(jnp.sum(ssq, axis=1, keepdims=True) / E + EPS)
-    output = (rows + r * dot(gg, w_out)).astype(bf16)
-    dm = dot(grad_out, w_out, ((1,), (1,))).astype(bf16)
     gos = (grad_out.astype(f32) * r).astype(bf16)
     g_out = dot(gg, gos, ((0,), (0,))).astype(bf16)
+    s_out = lax.psum_scatter(g_out, AXES, scatter_dimension=0, tiled=True).astype(f32)
+    output = (rows + r * dot(gg, full_out)).astype(bf16)
+    dm = dot(grad_out, full_out, ((1,), (1,))).astype(bf16)
     s = jnp.sum(gg.astype(f32) * dm.astype(f32), axis=1, keepdims=True)
     rq = jnp.concatenate([r, r * r * r * s / E], axis=1)
-    du, dgate, dg, db, dc, rs, small, kk = bwd(zx, pre, dm, rq, taps_u, masks, b, c, ct, gm, cum4, cumr, sc, st)
+    du, dgate, dg, db, dc, rs, small, kk = bwd(ubc, gate, pre, dm, rq, taps_u, masks, b, c, ct, gm, cum4, cumr, sc, st)
     kkh = jnp.sum(kk.reshape(kk.shape[0], H, E // H), axis=2)
     dbcdt, small_bc, hs = post(bcdt, pre_bc, taps_bc, heads_p, masks, segc, segr, b, c, dg, db, dc, rs, kkh, dt)
     g_gate = dot(normed, dgate, ((0,), (0,))).astype(bf16)
     g_u = dot(normed, du, ((0,), (0,))).astype(bf16)
     g_bcdt = dot(normed, dbcdt, ((0,), (0,))).astype(bf16)
-    bn = dot(dgate, w_zx[:, :E], ((1,), (1,))) + dot(du, w_zx[:, E:], ((1,), (1,))) + dot(dbcdt, w_bcdt, ((1,), (1,)))
+    s_in = scatter_rows([g.reshape(n, D // n, -1) for g in (g_gate, g_u, g_bcdt)], nd, nf, 1)
+    bn = dot(dgate, full_gate, ((1,), (1,))) + dot(du, full_a[:, :E], ((1,), (1,))) + dot(dbcdt, full_a[:, E:], ((1,), (1,)))
     gb = bn * norm_gain
     d_rows = rinv * (gb - xhat * jnp.mean(gb * xhat, axis=-1, keepdims=True))
     grad_in = (grad_out.astype(f32) + d_rows).astype(bf16)
     d_norm = jnp.sum(bn * xhat, axis=0)
-    d_conv_u = jnp.stack([small[6], small[5], small[4], small[3], small[2]])
-    d_conv_bc = jnp.stack([small_bc[4], small_bc[3], small_bc[2], small_bc[1], small_bc[0]])
-    d_conv = jnp.concatenate([d_conv_u, d_conv_bc], axis=1)
+    d_conv = jnp.concatenate([jnp.stack([small[6], small[5], small[4], small[3], small[2]]),
+                              jnp.stack([small_bc[4], small_bc[3], small_bc[2], small_bc[1], small_bc[0]])], axis=1)
     d_heads = jnp.concatenate([hs, jnp.sum(small[1].reshape(1, H, E // H), axis=2)], axis=0)
-    return output, grad_in, g_gate, g_u, g_bcdt, g_out, d_conv, d_norm, small[0], d_heads
-
-
-AXES = ("dp", "fsdp")
-
-
-def per_device(hidden, grad_out, segment_ids, w_zx, w_bc, w_dt, w_out, conv_params, norm_gain, gate_gain, head_params):
-    n = lax.axis_size(AXES)
-    E = w_out.shape[0] * n
-    H = w_dt.shape[1]
-    gather = lambda w, axis=0: lax.all_gather(w, AXES, axis=axis, tiled=True)
-    scatter = lambda w, axis=0: lax.psum_scatter(w, AXES, scatter_dimension=axis, tiled=True)
-    pad = 128 - H
-    full_zx = gather(w_zx)
-    full_bcdt = gather(jnp.concatenate([w_bc, w_dt, jnp.zeros((w_dt.shape[0], pad), bf16)], axis=1))
-    full_out = gather(w_out)
+    mine = jnp.concatenate([d_conv.reshape(K1, n, ncol).transpose(1, 0, 2).reshape(n, -1), d_norm.reshape(n, -1), small[0].reshape(n, -1),
+                            jnp.broadcast_to(d_heads.reshape(1, -1), (n, d_heads.size))], axis=1)
+    tiles = -(-mine.shape[1] // 1024)
+    mine = jnp.pad(mine, ((0, 0), (0, tiles * 1024 - mine.shape[1]))).reshape(n, tiles * 8, 128)
+    tot = exchange(mine, nd, nf, 2).reshape(-1)
+    cut = [0, K1 * ncol, nrow, ngate, d_heads.size]
+    ends = [sum(cut[: k + 1]) for k in range(5)]
+    t_conv, t_norm, t_gate, t_heads = (tot[ends[k] : ends[k + 1]] for k in range(4))
+    return (output, grad_in, s_in[:, : 2 * E], s_in[:, 2 * E : 2 * E + 2 * N], s_in[:, 2 * E + 2 * N : 2 * E + 2 * N + H], s_out,
+            t_conv.reshape(K1, ncol), t_norm, t_gate, t_heads.reshape(d_heads.shape))
+
+
+def per_device(nd, nf, hidden, grad_out, segment_ids, w_zx, w_bc, w_dt, w_out, conv_params, norm_gain, gate_gain, head_params):
+    n = nd * nf
+    E, N2, H = w_out.shape[0] * n, w_bc.shape[1], w_dt.shape[1]
+    rows = w_zx.shape[0]
     small = jnp.concatenate([conv_params.reshape(-1), norm_gain, gate_gain])
-    smalls = gather(small[None])
-    nc_, k1 = conv_params.shape[1], conv_params.shape[0]
-    conv = smalls[:, : k1 * nc_].reshape(n, k1, nc_).transpose(1, 0, 2).reshape(k1, n * nc_).astype(f32)
-    ng = smalls[:, k1 * nc_ : k1 * nc_ + norm_gain.shape[0]].reshape(-1).astype(f32)
-    gg = smalls[:, k1 * nc_ + norm_gain.shape[0] :].reshape(-1).astype(f32)
-    output, grad_in, g_gate, g_u, g_bcdt, g_out, d_conv, d_norm, d_gg, d_heads = layer(
-        hidden, grad_out, segment_ids, full_zx, full_bcdt, full_out, conv, ng, gg, head_params)
-    s_out = scatter(g_out).astype(f32)
-    s_zx = scatter(jnp.concatenate([g_gate, g_u], axis=1)).astype(f32)
-    s_bcdt = scatter(g_bcdt).astype(f32)
-    rows = jnp.concatenate([d_conv.reshape(k1, n, nc_).transpose(1, 0, 2).reshape(n, -1), d_norm.reshape(n, -1), d_gg.reshape(n, -1)], axis=1)
-    s_small = scatter(rows)[0]
-    N2 = w_bc.shape[1]
-    return (output, grad_in, s_zx, s_bcdt[:, :N2], s_bcdt[:, N2 : N2 + H], s_out, s_small[: k1 * nc_].reshape(k1, nc_),
-            s_small[k1 * nc_ : k1 * nc_ + norm_gain.shape[0]], s_small[k1 * nc_ + norm_gain.shape[0] :], lax.psum(d_heads, AXES))
+    S = -(-small.shape[0] // rows)
+    assert S + H <= 128
+    small = jnp.pad(small, (0, S * rows - small.shape[0])).reshape(rows, S)
+    shard_a = jnp.concatenate([w_zx[:, E:], w_bc, w_dt, small, jnp.zeros((rows, 128 - H - S), bf16)], axis=1)
+    return layer(nd, nf, hidden, grad_out, segment_ids, shard_a, w_zx[:, :E], w_out, head_params, (E, N2 // 2, H, conv_params.shape[0], S))
 
 
 def solution(mesh):
     row, col, vec, rep = P(AXES, None), P(None, AXES), P(AXES), P()
     return jax.shard_map(
-        per_device,
+        functools.partial(per_device, mesh.shape["dp"], mesh.shape["fsdp"]),
         mesh=mesh,
         in_specs=(row, row, vec, row, row, row, row, col, vec, vec, rep),
         out_specs=(row, row, row, row, row, row, col, vec, vec, rep),

time: 1050 us -> 592 us (0.56)
  waiting for transfers between devices: 564 us -> 0.73 us
  Pallas kernels: 179 us -> 363 us
  blocking collectives: 81.7 us -> 0 us
  other arithmetic: 31.6 us -> 17.7 us
  local copies, waits for them, and re-layouts: 23.2 us -> 34.3 us
    reduce_scatter x3 -> x1, waiting for transfers between devices: 448 us -> 0.01 us  [layer(): lax.psum_scatter(g_out, AXES, scatter_dimension=0, tiled=True).astype(f32)]
    pallas_call x2 -> x5, Pallas kernels: 149 us -> 333 us  [the longest x1 101 us: bwd(): pl.pallas_call(bwd_kernel, grid=(G,), in_specs=[col(0), col(0), col(0), c...]
    all_gather x3 -> x2, waiting for transfers between devices: 112 us -> 0.01 us  [the longest x1 0.01 us: layer(): full_gate = lax.all_gather(shard_gate, AXES, axis=0, tiled=True)]
    unnamed x1 -> x0, blocking collectives: 42.5 us -> none
    psum x1 -> x0, blocking collectives: 39.2 us -> none  [per_device(): lax.psum(d_heads, AXES)]
    concatenate x5 -> x3, other arithmetic: 15.6 us -> 0.81 us  [the longest x1 0.71 us: layer(): jnp.concatenate([conv[:, :E], gate_gain[None], jnp.repeat(head_params[2],...]
  transfers between devices with their start and end apart: 7 -> 3, of which waited for: 6 -> 0; matrix products, arithmetic and copies ran while one was open for 13% -> 31% of each run, Pallas kernels for 6% -> 62%
where the time goes in v2:
time: 592 us; the launch traced here: 583 us
  Pallas kernels  363 us (61%)
  matrix products  153 us (26%)
  local copies, waits for them, and re-layouts  34.3 us (6%)
  other arithmetic  17.7 us (3%)
  between operations  14.4 us (2%)
    dot_general x11, matrix products, dot(): lax.dot_general(a, b, (dims, ((), ())), preferred_element_type=f32, preci...  153 us
    pallas_call x1, Pallas kernels, bwd(): pl.pallas_call(bwd_kernel, grid=(G,), in_specs=[col(0), col(0), col(0), c...  101 us
    pallas_call x1, Pallas kernels, scatter_rows(): pl.pallas_call(functools.partial(scatter_kernel, nd, nf, parts), out_shap...  94.8 us
    pallas_call x1, Pallas kernels, gather_rows(): pl.pallas_call(functools.partial(gather_kernel, nd, nf), out_shape=jax.Sh...  79 us
    pallas_call x1, Pallas kernels, fwd(): pl.pallas_call(fwd_kernel, grid=(G,), in_specs=[col(0), col(0), pl.BlockS...  47.8 us
    pallas_call x1, Pallas kernels, prep(): pl.pallas_call(prep_kernel, out_shape=(S((T, N), bf16), S((T, N), bf16),...  17.4 us
    pallas_call x1, Pallas kernels, post(): pl.pallas_call(post_kernel, out_shape=(S(bcdt.shape, bf16), S((8, 2 * N),...  12.6 us
  transfers between devices with their start and end apart: 3, of which 0 were waited for; matrix products, arithmetic and copies ran while one was open for 31% of the time, Pallas kernels for 62%

profile of v2, /device:TPU:0, one launch (start us, length us, event | category | flops | bytes accessed | tf_op | source)
XLA Modules:
  0.0 582.8 jit_solution(18420645262227584229)
XLA Ops:
  7.2 1.8 fusion.39
  17.1 79.0 %shard_map.186 = bf16[32,48,3456]{2,1,0:T(8,128)(2,1)} custom-call(bf16[48,3456]{1,0:T(8,128)(2,1)} %concatenate.40.src_ref), custom_call_target="tpu_custom_call" | custom-call | tf_op jit(solution)/shard_map/pallas_call | solution.py:580
  104.6 2.0 pad.20.m_ref
  109.6 14.4 %convolution_convert_fusion.3.u_ref = bf16[1024,3456]{1,0:T(8,128)(2,1)S(1)} fusion(bf16[1536,3456]{1,0:T(8,128)(2,1)} %bitcast.45, bf16[1024,1536]{1,0:T(8,128)(2,1)S(1)} %copy-done.1, f32[1536]{0:T(1024)S(1)} %reshape.167, f32[1024]{0:T(1024)S(1)} %add_rsqrt_fusion.1), kind=kOutput, calls=%fused_computation.15 | convolution fusion | flops 10881466368 | bytes 20850688 | tf_op jit(solution)/shard_map/dot_general | solution.py:18
  124.1 2.9 copy-done
  128.0 17.4 %shard_map.187 = (bf16[1024,128]{1,0:T(8,128)(2,1)}, bf16[1024,128]{1,0:T(8,128)(2,1)}, bf16[128,1024]{1,0:T(8,128)(2,1)}, bf16[128,1024]{1,0:T(8,128)(2,1)}, f3...) custom-call(bf16[1024,384]{1,0:T(8,128)(2,1)} %slice.166.bcdt_ref, ...), custom_call_target="tpu_custom_call" | custom-call | tf_op jit(solution)/shard_map/pallas_call | solution.py:99
  146.1 14.3 %convolution_convert_fusion.5.gate_ref = bf16[1024,3072]{1,0:T(8,128)(2,1)} fusion(bf16[1536,3072]{1,0:T(8,128)(2,1)} %all-gather.3.cloned.1.call-done, bf16[1024,1536]{1,0:T(8,128)(2,1)S(1)} %copy-done.1, f32[1536]{0:T(1024)S(1)} %reshape.167, f32[1024]{0:T(1024)S(1)} %add_rsqrt_fusion.1), kind=kOutput, calls=%fused_computation.27 | convolution fusion | flops 9673113600 | bytes 18884608 | tf_op jit(solution)/shard_map/dot_general | solution.py:18
  160.3 47.8 %shard_map.188 = (bf16[1024,3072]{1,0:T(8,128)(2,1)}, f32[1024,128]{1,0:T(8,128)}, bf16[1024,3072]{1,0:T(8,128)(2,1)}, bf16[8,128,3072]{2,1,0:T(8,128)(2,1)}) custom-call(bf16[1024,3456]{1,0:T(8,128)(2,1)} %copy-done, bf16[1024,3072]{1,0:T(8,128)(2,1)} %convolution_convert_fusion.5.gate_ref, f32[8,3072]{1,0:T(8,128)} %maximum_maximum_fusion.1.taps_ref, ...), custom_call_target="tpu_custom_call" | custom-call | flops 4831838208 | bytes 37748736 | tf_op jit(solution)/shard_map/pallas_call | solution.py:187
  209.4 15.8 %convolution_convert_fusion = bf16[3072,1536]{1,0:T(8,128)(2,1)} fusion(bf16[1024,3072]{1,0:T(8,128)(2,1)} %get-tuple-element.43, bf16[1024,1536]{1,0:T(8,128)(2,1)} %param.12, f32[1024]{0:T(1024)S(1)} %add_rsqrt_fusion), kind=kOutput, calls=%fused_computation.1 | convolution fusion | flops 9673113600 | bytes 18878464 | tf_op jit(solution)/shard_map/dot_general | solution.py:18
  225.2 17.0 %multiply_reduce_fusion = (f32[1024]{0:T(1024)S(1)}, bf16[1024,3072]{1,0:T(8,128)(2,1)}) fusion(bf16[1024,3072]{1,0:T(8,128)(2,1)} %get-tuple-element.43, bf16[1024,1536]{1,0:T(8,128)(2,1)} %param.12, bf16[3072,1536]{1,0:T(8,128)(2,1)} %all-gather.5.cloned.1.call-done), kind=kOutput, calls=%fused_computation | convolution fusion | flops 9679404032 | bytes 25169920 | tf_op jit(solution)/shard_map/dot_general | solution.py:18
  243.3 101.2 %shard_map.189 = (bf16[1024,3072]{1,0:T(8,128)(2,1)}, bf16[1024,3072]{1,0:T(8,128)(2,1)}, f32[8,128,128]{2,1,0:T(8,128)}, f32[1024,128]{1,0:T(8,128)}, f32[1024,...) custom-call(bf16[1024,3456]{1,0:T(8,128)(2,1)} %copy-done, ...), custom_call_target="tpu_custom_call" | custom-call | flops 8053063680 | bytes 50331648 | tf_op jit(solution)/shard_map/pallas_call | solution.py:330
  344.6 15.9 %fusion.41 = f32[1024,1536]{1,0:T(8,128)} fusion(bf16[1024,3072]{1,0:T(8,128)(2,1)} %get-tuple-element.47, bf16[1536,3072]{1,0:T(8,128)(2,1)} %all-gather.3.cloned.1.call-done), kind=kOutput, calls=%fused_computation.74 | convolution fusion | flops 9663676416 | bytes 22020096 | tf_op jit(solution)/shard_map/dot_general | solution.py:18
  361.7 12.6 %shard_map.190 = (bf16[1024,384]{1,0:T(8,128)(2,1)}, f32[8,256]{1,0:T(8,128)}, f32[2,48]{1,0:T(2,128)}) custom-call(bf16[1024,384]{1,0:T(8,128)(2,1)} %slice.166.bcdt_ref, f32[1024,256]{1,0:T(8,128)} %get-tuple-element.49.pre_ref, f32[8,256]{1,0:T(8,128)} %concatenate.45.taps_ref, f32[8,128]{1,0:T(8,128)} %pad.19.heads_ref, f32[1032,4]{1,0:T(8,128)} %pad.20.m_ref, ...), custom_call_target="tpu_custom_call" | custom-call | tf_op jit(solution)/shard_map/pallas_call | solution.py:415
  376.4 5.9 %fusion.19 = f32[1024,1536]{1,0:T(8,128)} fusion(bf16[1024,384]{1,0:T(8,128)(2,1)} %get-tuple-element.56, bf16[1536,3456]{1,0:T(8,128)(2,1)} %bitcast.46), kind=kOutput, calls=%fused_computation.30 | convolution fusion | flops 1207959552 | bytes 8257536 | tf_op jit(solution)/shard_map/dot_general | solution.py:18
  382.3 20.9 %fusion.12 = (f32[1536]{0:T(1024)S(1)}, f32[1024]{0:T(1024)S(1)}, f32[1024,1536]{1,0:T(8,128)}) fusion(bf16[1024,1536]{1,0:T(8,128)(2,1)S(1)} %copy-done.1, f32[1024]{0:T(1024)S(1)} %add_rsqrt_fusion.1, f32[1536]{0:T(1024)S(1)} %reshape.167, f32[1024,1536]{1,0:T(8,128)} %fusion.19, f32[1024,1536]{1,0:T(8,128)} %fusion.41, ...), kind=kOutput, calls=%fused_computation.22 | convolution fusion | flops 9677829120 | bytes 37769216 | tf_op jit(solution)/shard_map/dot_general | solution.py:18
  404.1 10.0 %shard_map.192 = f32[8,128]{1,0:T(8,128)} custom-call(f32[32,8,128]{2,1,0:T(8,128)} %bitcast.51), custom_call_target="tpu_custom_call" | custom-call | tf_op jit(solution)/shard_map/pallas_call | solution.py:809
  417.4 4.2 convolution_convert_fusion.6
  421.6 15.5 %convolution_convert_fusion.2 = bf16[1536,3072]{1,0:T(8,128)(2,1)} fusion(bf16[1024,3072]{1,0:T(8,128)(2,1)} %get-tuple-element.47, bf16[1024,1536]{1,0:T(8,128)(2,1)S(1)} %copy-done.1, f32[1536]{0:T(1024)S(1)} %reshape.167, f32[1024]{0:T(1024)S(1)} %add_rsqrt_fusion.1), kind=kOutput, calls=%fused_computation.3 | convolution fusion | flops 9674686464 | bytes 18884608 | tf_op jit(solution)/shard_map/dot_general | solution.py:18
  437.1 13.2 %convolution_convert_fusion.1 = bf16[1536,3072]{1,0:T(8,128)(2,1)} fusion(bf16[1024,3072]{1,0:T(8,128)(2,1)S(1)} %bitcast.75, bf16[1024,1536]{1,0:T(8,128)(2,1)S(1)} %copy-done.1, f32[1536]{0:T(1024)S(1)} %reshape.167, f32[1024]{0:T(1024)S(1)} %add_rsqrt_fusion.1), kind=kOutput, calls=%fused_computation.2 | convolution fusion | flops 9674686464 | bytes 18884608 | tf_op jit(solution)/shard_map/dot_general | solution.py:18
  450.3 94.8 %shard_map.191 = f32[48,6528]{1,0:T(8,128)} custom-call(bf16[32,48,3072]{2,1,0:T(8,128)(2,1)} %bitcast.48, bf16[32,48,3072]{2,1,0:T(8,128)(2,1)} %bitcast.49, bf16[32,48,384]{2,1,0:T(8,128)(2,1)} %bitcast.50), custom_call_target="tpu_custom_call" | custom-call | tf_op jit(solution)/shard_map/pallas_call | solution.py:754
  547.9 2.4 slice.143
  551.6 6.9 %fusion.6 = bf16[1024,1536]{1,0:T(8,128)(2,1)} fusion(bf16[1024,1536]{1,0:T(8,128)(2,1)} %param.12, bf16[1024,1536]{1,0:T(8,128)(2,1)} %param.11, f32[1024,1536]{1,0:T(8,128)} %get-tuple-element.81, f32[1024]{0:T(1024)S(1)} %broadcast_multiply_fusion, f32[1536]{0:T(1024)S(1)} %reshape.167, f32[1024]{0:T(1024)S(1)} %add_rsqrt_fusion.1), kind=kLoop, calls=%fused_computation.16 | loop fusion | flops 14155776 | bytes 15742976 | tf_op jit(solution)/shard_map/convert_element_type | solution.py:870
  558.5 15.5 %fusion.14 = bf16[1024,1536]{1,0:T(8,128)(2,1)} fusion(bf16[1024,1536]{1,0:T(8,128)(2,1)S(1)} %copy-done.2, bf16[1024,3072]{1,0:T(8,128)(2,1)} %get-tuple-element.43, bf16[3072,1536]{1,0:T(8,128)(2,1)} %all-gather.5.cloned.1.call-done, f32[1024]{0:T(1024)S(1)} %add_rsqrt_fusion), kind=kOutput, calls=%fused_computation.24 | convolution fusion | flops 9669967872 | bytes 22024192 | tf_op jit(solution)/shard_map/dot_general | solution.py:18
  574.0 1.8 convert_element_type.119
  (102 shorter events, 35.1 us)
Async XLA Ops:
  7.2 138.9 %all-gather.3.cloned.1.call-start = ((), (), s32[]{:S(2)}) async-start(), calls=%async_computation.1 | async-start | bytes 9732096 | tf_op jit(solution)/shard_map/all_gather | solution.py:824
  9.0 216.2 %all-gather.5.cloned.1.call-start = ((), (), s32[]{:S(2)}) async-start(), calls=%async_computation.2 | async-start | bytes 9732096 | tf_op jit(solution)/shard_map/all_gather | solution.py:825
  9.8 564.2 %reduce-scatter.2.cloned.1.call-start = ((), (), s32[]{:S(2)}) async-start(), calls=%async_computation.3 | async-start | bytes 9732096 | tf_op jit(solution)/shard_map/reduce_scatter | solution.py:855
  17.1 82.3 %copy-start.7 = (f32[3,48]{1,0:T(4,128)S(1)}, f32[3,48]{1,0:T(4,128)}, u32[]{:S(2)}) copy-start(f32[3,48]{1,0:T(4,128)} %param.21) | copy-start | bytes 1732
  17.1 83.0 %copy-start.3 = (s32[1024]{0:T(1024)S(1)}, s32[1024]{0:T(1024)}, u32[]{:S(2)}) copy-start(s32[1024]{0:T(1024)} %param.13) | copy-start | bytes 12292
  17.1 91.8 %copy-start.1 = (bf16[1024,1536]{1,0:T(8,128)(2,1)S(1)}, bf16[1024,1536]{1,0:T(8,128)(2,1)}, u32[]{:S(2)}) copy-start(bf16[1024,1536]{1,0:T(8,128)(2,1)} %param.11) | copy-start | bytes 9437188
  124.1 2.9 copy-start
  344.5 15.9 %copy-start.5 = (f32[8,3072]{1,0:T(8,128)S(1)}, f32[8,3072]{1,0:T(8,128)}, u32[]{:S(2)}) copy-start(f32[8,3072]{1,0:T(8,128)} %get-tuple-element.57) | copy-start | bytes 294916
  344.6 16.3 %copy-start.4 = (f32[8,3072]{1,0:T(8,128)S(1)}, f32[8,3072]{1,0:T(8,128)}, u32[]{:S(2)}) copy-start(f32[8,3072]{1,0:T(8,128)} %get-tuple-element.54) | copy-start | bytes 294916
  417.4 19.8 %slice-start = ((s8[6291456]{0:T(1024)(128)(4,1)}), s8[4194304]{0:T(1024)(128)(4,1)S(1)}, s32[]{:S(2)}) async-start(s8[6291456]{0:T(1024)(128)(4,1)} %bitcast.74), calls=%async_computation.4 | async-start | bytes 8388608
  421.6 15.5 %slice-start.1 = ((s8[6291456]{0:T(1024)(128)(4,1)}), s8[2097152]{0:T(1024)(128)(4,1)S(1)}, s32[]{:S(2)}) async-start(s8[6291456]{0:T(1024)(128)(4,1)} %bitcast.74), calls=%async_computation.5 | async-start | bytes 4194304
  450.3 100.6 %copy-start.6 = (f32[8,128]{1,0:T(8,128)S(1)}, f32[8,128]{1,0:T(8,128)}, u32[]{:S(2)}) copy-start(f32[8,128]{1,0:T(8,128)} %shard_map.192) | copy-start | bytes 12292
  551.6 6.9 %copy-start.2 = (bf16[1024,1536]{1,0:T(8,128)(2,1)S(1)}, bf16[1024,1536]{1,0:T(8,128)(2,1)}, u32[]{:S(2)}) copy-start(bf16[1024,1536]{1,0:T(8,128)(2,1)} %param.11) | copy-start | bytes 9437188
Sparse Core Ops, SparseCore 0:
  10.9 97.8 all-gather.2
  111.7 82.6 all-gather.4
  243.4 132.4 reduce-scatter.1

commit v3 on v1

--- a/solution.py
+++ b/solution.py
@@ -10,8 +10,425 @@
 L = 128
 HG = 4
 LOG2E = 1.4426950408889634
+BWD_TICKS = 44
+TAIL_TICKS = 22
 bf16, f32 = jnp.bfloat16, jnp.float32
 HIGHEST = lax.Precision.HIGHEST
+
+
+AXES = ("dp", "fsdp")
+MESH = pl.DeviceIdType.MESH
+
+
+class Place:
+    def __init__(self, nd, nf):
+        self.zn, self.nf = nd // 2, nf
+        d, f = lax.axis_index("dp"), lax.axis_index("fsdp")
+        self.z, self.y = d // 2, d % 2
+        self.x, self.c = f // 2, f % 2
+
+    def dev(self, z, y, x, c):
+        return (z * 2 + y, x * 2 + c)
+
+    def idx(self, z, y, x, c):
+        return (z * 2 + y) * self.nf + x * 2 + c
+
+    def barrier(self):
+        z, y, x, c, zn = self.z, self.y, self.x, self.c, self.zn
+        sem = pltpu.get_barrier_semaphore()
+        for there in ((z, y, 1 - x, c), (z, 1 - y, x, c), (z, y, x, 1 - c)):
+            pl.semaphore_signal(sem, inc=1, device_id=self.dev(*there), device_id_type=MESH)
+
+        @pl.when(z > 0)
+        def _():
+            pl.semaphore_signal(sem, inc=1, device_id=self.dev(z - 1, y, x, c), device_id_type=MESH)
+
+        @pl.when(z < zn - 1)
+        def _():
+            pl.semaphore_signal(sem, inc=1, device_id=self.dev(z + 1, y, x, c), device_id_type=MESH)
+
+        pl.semaphore_wait(sem, 3 + (z + zn - 1) // zn + (2 * zn - 2 - z) // zn)
+
+
+def gather_kernel(nd, nf, src_ref, out_ref, own_sem, z_send, z_recv, x_send, x_recv, y_send, y_recv, dx_send, dx_recv, dy_send, dy_recv, c_send, c_recv):
+    at = Place(nd, nf)
+    z, y, x, c, zn = at.z, at.y, at.x, at.c, at.zn
+    half = out_ref.shape[2] // 256 * 128
+    lo, hi = pl.ds(0, half), pl.ds(half, out_ref.shape[2] - half)
+    at.barrier()
+
+    def copy(block, to, send, recv, cols=None, src=None):
+        ref = out_ref.at[block] if cols is None else out_ref.at[block, :, cols]
+        return pltpu.make_async_remote_copy(src_ref=ref if src is None else src, dst_ref=ref, send_sem=send, recv_sem=recv,
+                                            device_id=at.dev(*to), device_id_type=MESH)
+
+    def block(zs, col):
+        return at.idx(zs, 1 - y if col & 2 else y, 1 - x if col & 1 else x, c)
+
+    def up(zs, src=None):
+        return copy(block(zs, 0), (z + 1, y, x, c), z_send.at[0, zs], z_recv.at[zs], src=src)
+
+    def down(zs, src=None):
+        return copy(block(zs, 0), (z - 1, y, x, c), z_send.at[1, zs], z_recv.at[zs], src=src)
+
+    def to_x(zs, src=None):
+        return copy(block(zs, 0), (z, y, 1 - x, c), x_send.at[zs], x_recv.at[zs], src=src)
+
+    def to_y(zs, src=None):
+        return copy(block(zs, 0), (z, 1 - y, x, c), y_send.at[zs], y_recv.at[zs], src=src)
+
+    def diag_y(zs):
+        return copy(block(zs, 1), (z, 1 - y, x, c), dy_send.at[zs], dy_recv.at[zs], lo)
+
+    def diag_x(zs):
+        return copy(block(zs, 2), (z, y, 1 - x, c), dx_send.at[zs], dx_recv.at[zs], hi)
+
+    def to_core(zs, col, src=None):
+        return copy(block(zs, col), (z, y, x, 1 - c), c_send.at[zs, col], c_recv.at[zs, col], src=src)
+
+    own = pltpu.make_async_copy(src_ref, out_ref.at[block(z, 0)], own_sem)
+    own.start()
+
+    @pl.when(z < zn - 1)
+    def _():
+        up(z, src_ref).start()
+
+    @pl.when(z > 0)
+    def _():
+        down(z, src_ref).start()
+
+    to_x(z, src_ref).start()
+    to_y(z, src_ref).start()
+    to_core(z, 0, src_ref).start()
+
+    def each(dist, fn):
+        if dist == 0:
+            fn(z, 0)
+            return
+
+        @pl.when(z - dist >= 0)
+        def _():
+            fn(z - dist, 1)
+
+        @pl.when(z + dist < zn)
+        def _():
+            fn(z + dist, -1)
+
+    def from_z(zs, way):
+        copy(block(zs, 0), (z, y, x, c), z_send.at[0, zs], z_recv.at[zs]).wait_recv()
+        if way > 0:
+            @pl.when(z < zn - 1)
+            def _():
+                up(zs).start()
+        else:
+            @pl.when(z > 0)
+            def _():
+                down(zs).start()
+        to_x(zs).start()
+        to_y(zs).start()
+        to_core(zs, 0).start()
+
+    def from_xy(zs, way):
+        to_x(zs).wait_recv()
+        diag_y(zs).start()
+        to_core(zs, 1).start()
+        to_y(zs).wait_recv()
+        diag_x(zs).start()
+        to_core(zs, 2).start()
+
+    def from_diag(zs, way):
+        diag_y(zs).wait_recv()
+        diag_x(zs).wait_recv()
+        to_core(zs, 3).start()
+
+    for dist in range(zn):
+        if dist:
+            each(dist, from_z)
+        each(dist, from_xy)
+    for dist in range(zn):
+        each(dist, from_diag)
+    own.wait()
+
+    def sent(zs, way):
+        for col in range(4):
+            to_core(zs, col).wait_recv()
+            to_core(zs, col).wait_send()
+        to_x(zs).wait_send()
+        to_y(zs).wait_send()
+        diag_x(zs).wait_send()
+        diag_y(zs).wait_send()
+        if way >= 0:
+            @pl.when(z < zn - 1)
+            def _():
+                up(zs).wait_send()
+        if way <= 0:
+            @pl.when(z > 0)
+            def _():
+                down(zs).wait_send()
+
+    for dist in range(zn):
+        each(dist, sent)
+
+
+def gather_rows(shard, nd, nf, cid):
+    zn = nd // 2
+    D = pltpu.SemaphoreType.DMA
+    return pl.pallas_call(
+        functools.partial(gather_kernel, nd, nf),
+        out_shape=jax.ShapeDtypeStruct((nd * nf,) + shard.shape, shard.dtype),
+        in_specs=[pl.BlockSpec(memory_space=pl.ANY)],
+        out_specs=pl.BlockSpec(memory_space=pl.ANY),
+        scratch_shapes=[D(()), D((2, zn)), D((zn,)), D((zn,)), D((zn,)), D((zn,)), D((zn,)), D((zn,)), D((zn,)), D((zn,)), D((zn,)),
+                        D((zn, 4)), D((zn, 4))],
+        compiler_params=pltpu.CompilerParams(collective_id=cid, has_side_effects=True),
+    )(shard)
+
+
+class Scatter:
+    def __init__(self, nd, nf, g_refs, out_ref, acc, c_in, d_in, xy_in, z_in,
+                 load_sem, c_send, c_recv, dx_send, dx_recv, dy_send, dy_recv, x_send, x_recv, y_send, y_recv, z_send, z_recv):
+        at = Place(nd, nf)
+        z, y, x, c, zn = at.z, at.y, at.x, at.c, at.zn
+        cols = out_ref.shape[1]
+        offs = [sum(r.shape[2] for r in g_refs[:k]) for k in range(len(g_refs))]
+        half = cols // 256 * 128
+        lo, hi = pl.ds(0, half), pl.ds(half, cols - half)
+
+        def idx(zs, col, core):
+            return at.idx(zs, 1 - y if col & 2 else y, 1 - x if col & 1 else x, core)
+
+        def remote(src, dst, to, send, recv):
+            return pltpu.make_async_remote_copy(src_ref=src, dst_ref=dst, send_sem=send, recv_sem=recv, device_id=at.dev(*to), device_id_type=MESH)
+
+        def load(zs, col):
+            return [pltpu.make_async_copy(r.at[idx(zs, col, c)], acc.at[zs, col, :, pl.ds(o, r.shape[2])], load_sem.at[zs, col, k])
+                    for k, (r, o) in enumerate(zip(g_refs, offs))]
+
+        def core(zs, col):
+            return [remote(r.at[idx(zs, col, 1 - c)], c_in.at[zs, col, :, pl.ds(o, r.shape[2])], (z, y, x, 1 - c),
+                           c_send.at[zs, col, k], c_recv.at[zs, col, k])
+                    for k, (r, o) in enumerate(zip(g_refs, offs))]
+
+        def diag_x(zs):
+            return remote(acc.at[zs, 3, :, lo], d_in.at[zs, :, lo], (z, y, 1 - x, c), dx_send.at[zs], dx_recv.at[zs])
+
+        def diag_y(zs):
+            return remote(acc.at[zs, 3, :, hi], d_in.at[zs, :, hi], (z, 1 - y, x, c), dy_send.at[zs], dy_recv.at[zs])
+
+        def to_x(zs):
+            return remote(acc.at[zs, 1], xy_in.at[0, zs], (z, y, 1 - x, c), x_send.at[zs], x_recv.at[zs])
+
+        def to_y(zs):
+            return remote(acc.at[zs, 2], xy_in.at[1, zs], (z, 1 - y, x, c), y_send.at[zs], y_recv.at[zs])
+
+        def up(zs):
+            return remote(acc.at[zs, 0], z_in.at[0, zs], (z + 1, y, x, c), z_send.at[zs], z_recv.at[0, zs])
+
+        def down(zs):
+            return remote(acc.at[zs, 0], z_in.at[1, zs], (z - 1, y, x, c), z_send.at[zs], z_recv.at[1, zs])
+
+        def each(dist, fn):
+            if dist == 0:
+                fn(z)
+                return
+
+            @pl.when(z - dist >= 0)
+            def _():
+                fn(z - dist)
+
+            @pl.when(z + dist < zn)
+            def _():
+                fn(z + dist)
+
+        order = list(range(zn - 1, -1, -1))
+
+        def begin():
+            at.barrier()
+            for col in (3, 1, 2, 0):
+                for dist in order:
+                    def one(zs):
+                        for cp in core(zs, col) + load(zs, col):
+                            cp.start()
+                    each(dist, one)
+
+        def ready(zs, col):
+            for cp in load(zs, col):
+                cp.wait()
+            for cp in core(zs, col):
+                cp.wait_recv()
+
+        def wide(*terms):
+            total = terms[0].astype(f32)
+            for t in terms[1:]:
+                total = total + t.astype(f32)
+            return total
+
+        def diag(zs):
+            ready(zs, 3)
+            acc[zs, 3] = wide(acc[zs, 3], c_in[zs, 3]).astype(bf16)
+            diag_x(zs).start()
+            diag_y(zs).start()
+
+        def sides(zs):
+            ready(zs, 1)
+            diag_y(zs).wait_recv()
+            acc[zs, 1, :, lo] = wide(acc[zs, 1, :, lo], c_in[zs, 1, :, lo]).astype(bf16)
+            acc[zs, 1, :, hi] = wide(acc[zs, 1, :, hi], c_in[zs, 1, :, hi], d_in[zs, :, hi]).astype(bf16)
+            to_x(zs).start()
+            ready(zs, 2)
+            diag_x(zs).wait_recv()
+            acc[zs, 2, :, lo] = wide(acc[zs, 2, :, lo], c_in[zs, 2, :, lo], d_in[zs, :, lo]).astype(bf16)
+            acc[zs, 2, :, hi] = wide(acc[zs, 2, :, hi], c_in[zs, 2, :, hi]).astype(bf16)
+            to_y(zs).start()
+
+        def column(zs):
+            ready(zs, 0)
+            to_x(zs).wait_recv()
+            to_y(zs).wait_recv()
+            return wide(acc[zs, 0], c_in[zs, 0]) + wide(xy_in[0, zs], xy_in[1, zs])
+
+        def pass_on(zs):
+            total = column(zs)
+
+            @pl.when(zs > z)
+            def _():
+                @pl.when(z > 0)
+                def _():
+                    up(zs).wait_recv()
+                    acc[zs, 0] = (total + z_in[0, zs].astype(f32)).astype(bf16)
+
+                @pl.when(z == 0)
+                def _():
+                    acc[zs, 0] = total.astype(bf16)
+                up(zs).start()
+
+            @pl.when(zs < z)
+            def _():
+                @pl.when(z < zn - 1)
+                def _():
+                    down(zs).wait_recv()
+                    acc[zs, 0] = (total + z_in[1, zs].astype(f32)).astype(bf16)
+
+                @pl.when(z == zn - 1)
+                def _():
+                    acc[zs, 0] = total.astype(bf16)
+                down(zs).start()
+
+        def finish():
+            out_ref[...] = column(z)
+
+            @pl.when(z > 0)
+            def _():
+                up(z).wait_recv()
+                out_ref[...] += z_in[0, z].astype(f32)
+
+            @pl.when(z < zn - 1)
+            def _():
+                down(z).wait_recv()
+                out_ref[...] += z_in[1, z].astype(f32)
+
+            def sent(zs):
+                for col in range(4):
+                    for cp in core(zs, col):
+                        cp.wait_send()
+                diag_x(zs).wait_send()
+                diag_y(zs).wait_send()
+                to_x(zs).wait_send()
+                to_y(zs).wait_send()
+
+            for dist in order:
+                each(dist, sent)
+                if dist:
+                    each(dist, lambda zs: up(zs).wait_send())
+
+        self.begin, self.finish = begin, finish
+        self.diag = [functools.partial(each, dist, diag) for dist in order]
+        self.sides = [functools.partial(each, dist, sides) for dist in order]
+        self.pass_on = [functools.partial(each, dist, pass_on) for dist in order[:-1]]
+
+    def plan(self, diag, sides, side_gap, pass_on, pass_gap):
+        ticks = {0: [self.begin], diag: list(self.diag)}
+        for k, fn in enumerate(self.sides):
+            ticks.setdefault(sides + k * side_gap, []).append(fn)
+        for k, fn in enumerate(self.pass_on):
+            ticks.setdefault(pass_on + k * pass_gap, []).append(fn)
+        return ticks
+
+    @staticmethod
+    def scratch(nd, rows, cols, parts):
+        zn = nd // 2
+        D, V = pltpu.SemaphoreType.DMA, pltpu.VMEM
+        return [V((zn, 4, rows, cols), bf16), V((zn, 4, rows, cols), bf16), V((zn, rows, cols), bf16), V((2, zn, rows, cols), bf16),
+                V((2, zn, rows, cols), bf16), D((zn, 4, parts)), D((zn, 4, parts)), D((zn, 4, parts))] + [D((zn,))] * 9 + [D((2, zn))]
+
+
+def run_ticks(ticks, now, last):
+    for tick, fns in ticks.items():
+        if tick <= last:
+            @pl.when(now == tick)
+            def _(fns=fns):
+                for fn in fns:
+                    fn()
+
+
+def run_rest(ticks, last):
+    for tick, fns in sorted(ticks.items()):
+        if tick > last:
+            for fn in fns:
+                fn()
+
+
+def exchange_kernel(nd, nf, g_ref, out_ref, got, send, recv):
+    n = nd * nf
+    me = lax.axis_index("dp") * nf + lax.axis_index("fsdp")
+    sem = pltpu.get_barrier_semaphore()
+
+    def peer(k):
+        return lax.rem(me + k, n)
+
+    def greet(k, carry):
+        pl.semaphore_signal(sem, inc=1, device_id=(peer(k) // nf, peer(k) % nf), device_id_type=MESH)
+        return carry
+
+    lax.fori_loop(1, n, greet, 0)
+    pl.semaphore_wait(sem, n - 1)
+
+    def copy(k):
+        p = peer(k)
+        return pltpu.make_async_remote_copy(src_ref=g_ref.at[p], dst_ref=got.at[k], send_sem=send.at[k], recv_sem=recv.at[k],
+                                            device_id=(p // nf, p % nf), device_id_type=MESH)
+
+    def begin(k, carry):
+        copy(k).start()
+        return carry
+
+    lax.fori_loop(1, n, begin, 0)
+
+    def add(k, total):
+        copy(k).wait_recv()
+        return total + got[k]
+
+    out_ref[...] = lax.fori_loop(1, n, add, g_ref[me])
+
+    def end(k, carry):
+        copy(k).wait_send()
+        return carry
+
+    lax.fori_loop(1, n, end, 0)
+
+
+def exchange(g, nd, nf, cid):
+    n = nd * nf
+    D = pltpu.SemaphoreType.DMA
+    vm = pl.BlockSpec(memory_space=pltpu.VMEM)
+    return pl.pallas_call(
+        functools.partial(exchange_kernel, nd, nf),
+        out_shape=jax.ShapeDtypeStruct(g.shape[1:], g.dtype),
+        in_specs=[vm],
+        out_specs=vm,
+        scratch_shapes=[pltpu.VMEM(g.shape, g.dtype), D((n,)), D((n,))],
+        compiler_params=pltpu.CompilerParams(collective_id=cid, has_side_effects=True),
+    )(g)
 
 
 def dot(a, b, dims=((1,), (0,)), precision=None):
@@ -174,9 +591,8 @@
     lax.fori_loop(0, nc, chunk, 0)
 
 
-def fwd(zx, taps, masks, b, c, bt, gm, cum4, cumr, sc):
-    T = zx.shape[0]
-    E = zx.shape[1] // 2
+def fwd(u, gate, taps, masks, b, c, bt, gm, cum4, cumr, sc):
+    T, E = gate.shape
     N = b.shape[1]
     G = cum4.shape[0]
     W = E // G
@@ -188,18 +604,37 @@
     return pl.pallas_call(
         fwd_kernel,
         grid=(G,),
-        in_specs=[col(G), col(0), pl.BlockSpec((8, W), lambda g: (0, g)), full(masks), full(b), full(c), full(bt), full(gm),
+        in_specs=[col(0), col(0), pl.BlockSpec((8, W), lambda g: (0, g)), full(masks), full(b), full(c), full(bt), full(gm),
                   grp(cum4), grp(cumr), grp(sc)],
         out_specs=[col(0), pl.BlockSpec((T, 128), lambda g: (0, 0)), col(0), pl.BlockSpec((nc, N, W), lambda g: (0, 0, g))],
         out_shape=(S((T, E), bf16), S((T, 128), f32), S((T, E), bf16), S((nc, N, E), bf16)),
         scratch_shapes=[pltpu.VMEM((N, W), f32)],
         compiler_params=pltpu.CompilerParams(vmem_limit_bytes=60 << 20),
         cost_estimate=pl.CostEstimate(flops=T * E * (2 * L + 4 * N) * 2, bytes_accessed=T * E * 12, transcendentals=T * E * 4),
-    )(zx, zx, taps, masks, b, c, bt, gm, cum4, cumr, sc)
-
-
-def bwd_kernel(u_ref, gate_ref, pre_ref, dm_ref, rq_ref, taps_ref, m_ref, b_ref, c_ref, ct_ref, gm_ref, cum4_ref, cumr_ref, sc_ref, st_ref,
-               du_ref, dgate_ref, dg_ref, db_ref, dc_ref, rs_ref, small_ref, kk_ref, ds, nxt, acc):
+    )(u, gate, taps, masks, b, c, bt, gm, cum4, cumr, sc)
+
+
+def bwd_kernel(*refs):
+    bwd_body(lambda now: None, *refs)
+
+
+def bwd_scatter_kernel(nd, nf, parts, *refs):
+    g_refs, ins, outs = refs[:parts], refs[parts : parts + 15], refs[parts + 15 : parts + 23]
+    own, comm = refs[parts + 23 : parts + 26], refs[parts + 26 :]
+    sc = Scatter(nd, nf, g_refs, outs[7], *comm)
+    nc = ins[0].shape[0] // L
+    last = pl.num_programs(0) * nc - 1
+    ticks = sc.plan(7, 12, 3, 28, 6)
+    bwd_body(lambda now: run_ticks(ticks, now, BWD_TICKS), *ins, *outs[:7], *own)
+
+    @pl.when(pl.program_id(0) == pl.num_programs(0) - 1)
+    def _():
+        run_rest(ticks, BWD_TICKS)
+        sc.finish()
+
+
+def bwd_body(tick, u_ref, gate_ref, pre_ref, dm_ref, rq_ref, taps_ref, m_ref, b_ref, c_ref, ct_ref, gm_ref, cum4_ref, cumr_ref, sc_ref, st_ref,
+               dz_ref, dg_ref, db_ref, dc_ref, rs_ref, small_ref, kk_ref, ds, nxt, acc):
     T, W = u_ref.shape
     P = W // HG
     nc = T // L
@@ -229,6 +664,7 @@
         return jnp.sum(z.reshape(L // 8, 8, W), axis=0)
 
     def chunk(i, carry):
+        tick(step * nc + i)
         c = nc - 1 - i
         t0 = pl.multiple_of(c * L, L)
         here = pl.ds(t0, L)
@@ -268,7 +704,7 @@
         dgg = gain * dmr - g * q
         dyb = (dgg * silu_g).astype(bf16)
         dy = dyb.astype(f32)
-        dgate_ref[here, :] = (dgg * y * (sgate + silu_g * (1.0 - sgate))).astype(bf16)
+        dz_ref[0, here, :] = (dgg * y * (sgate + silu_g * (1.0 - sgate))).astype(bf16)
         dxi = []
         dgc = dg_ref[c]
         for p in range(HG // 2):
@@ -307,7 +743,7 @@
             sk = pltpu.roll(ext * mrows[:, k : k + 1], L + 8 - k, 0)[:L]
             du = du + taps[3 - k : 4 - k] * sk
             acc[24 + 8 * k : 32 + 8 * k, :] += eight(sk * u)
-        du_ref[here, :] = du.astype(bf16)
+        dz_ref[1, here, :] = du.astype(bf16)
         return carry
 
     lax.fori_loop(0, nc, chunk, 0)
@@ -316,35 +752,49 @@
     small_ref[7:8, :] = jnp.zeros((1, W), f32)
 
 
-def bwd(zx, pre, dm, rq, taps, masks, b, c, ct, gm, cum4, cumr, sc, st):
-    T = zx.shape[0]
-    E = zx.shape[1] // 2
+def bwd(half, halves, u, gate, pre, dm, rq, taps, masks, b, c, ct, gm, cum4, cumr, sc, st, comm=None):
+    T, E = gate.shape
     N = b.shape[1]
     G = cum4.shape[0]
     W = E // G
     nc = T // L
+    Gh = G // halves
+    Eh = E // halves
+    g0 = half * Gh
     S = jax.ShapeDtypeStruct
-    col = lambda off: pl.BlockSpec((T, W), lambda g: (0, g + off))
+    col = pl.BlockSpec((T, W), lambda g: (0, g + g0))
     full = lambda a: pl.BlockSpec(a.shape, lambda g: (0,) * a.ndim)
     whole = lambda s: pl.BlockSpec(s, lambda g: (0,) * len(s))
-    grp = lambda a: pl.BlockSpec((1,) + a.shape[1:], lambda g: (g, 0, 0))
-    masks = jnp.pad(masks, ((0, 8), (0, 0)))
+    grp = lambda a: pl.BlockSpec((1,) + a.shape[1:], lambda g: (g + g0, 0, 0))
+    in_specs = [col, col, col, col, full(rq), pl.BlockSpec((8, W), lambda g: (0, g + g0)), full(masks), full(b), full(c),
+                full(ct), full(gm), grp(cum4), grp(cumr), grp(sc), pl.BlockSpec((nc, N, W), lambda g: (0, 0, g + g0))]
+    out_specs = [pl.BlockSpec((2, T, W), lambda g: (0, 0, g)), whole((nc, L, L)), whole((T, N)), whole((T, N)),
+                 pl.BlockSpec((1, T, 16), lambda g: (g, 0, 0)), pl.BlockSpec((8, W), lambda g: (0, g)), pl.BlockSpec((nc, W), lambda g: (0, g))]
+    out_shape = [S((2, T, Eh), bf16), S((nc, L, L), f32), S((T, N), f32), S((T, N), f32), S((Gh, T, 16), f32), S((8, Eh), f32), S((nc, Eh), f32)]
+    scratch = [pltpu.VMEM((N, W), f32), pltpu.VMEM((8, W), f32), pltpu.VMEM((56, W), f32)]
+    kernel, first, params = bwd_kernel, (), {}
+    if comm:
+        nd, nf, cid, first = comm
+        rows, cols = first[0].shape[1], sum(g.shape[2] for g in first)
+        kernel = functools.partial(bwd_scatter_kernel, nd, nf, len(first))
+        in_specs = [pl.BlockSpec(memory_space=pl.ANY)] * len(first) + in_specs
+        out_specs.append(whole((rows, cols)))
+        out_shape.append(S((rows, cols), f32))
+        scratch += Scatter.scratch(nd, rows, cols, len(first))
+        params = dict(collective_id=cid, has_side_effects=True)
     return pl.pallas_call(
-        bwd_kernel,
-        grid=(G,),
-        in_specs=[col(G), col(0), col(0), col(0), full(rq), pl.BlockSpec((8, W), lambda g: (0, g)), full(masks), full(b), full(c),
-                  full(ct), full(gm), grp(cum4), grp(cumr), grp(sc), pl.BlockSpec((nc, N, W), lambda g: (0, 0, g))],
-        out_specs=[col(0), col(0), whole((nc, L, L)), whole((T, N)), whole((T, N)), pl.BlockSpec((1, T, 16), lambda g: (g, 0, 0)),
-                   pl.BlockSpec((8, W), lambda g: (0, g)), pl.BlockSpec((nc, W), lambda g: (0, g))],
-        out_shape=(S((T, E), bf16), S((T, E), bf16), S((nc, L, L), f32), S((T, N), f32), S((T, N), f32), S((G, T, 16), f32),
-                   S((8, E), f32), S((nc, E), f32)),
-        scratch_shapes=[pltpu.VMEM((N, W), f32), pltpu.VMEM((8, W), f32), pltpu.VMEM((56, W), f32)],
-        compiler_params=pltpu.CompilerParams(vmem_limit_bytes=60 << 20),
-        cost_estimate=pl.CostEstimate(flops=T * E * (8 * L + 12 * N), bytes_accessed=T * E * 16, transcendentals=T * E * 4),
-    )(zx, zx, pre, dm, rq, taps, masks, b, c, ct, gm, cum4, cumr, sc, st)
-
-
-def post_kernel(bcdt_ref, pre_ref, taps_ref, heads_ref, m_ref, segc_ref, segr_ref, b_ref, c_ref, dg_ref, db_ref, dc_ref, rs_ref, kk_ref, dt_ref,
+        kernel,
+        grid=(Gh,),
+        in_specs=in_specs,
+        out_specs=out_specs,
+        out_shape=out_shape,
+        scratch_shapes=scratch,
+        compiler_params=pltpu.CompilerParams(vmem_limit_bytes=60 << 20, **params),
+        cost_estimate=pl.CostEstimate(flops=T * Eh * (8 * L + 12 * N), bytes_accessed=T * Eh * 16, transcendentals=T * Eh * 4),
+    )(*first, u, gate, pre, dm, rq, taps, masks, b, c, ct, gm, cum4, cumr, sc, st)
+
+
+def post_kernel(bcdt_ref, pre_ref, taps_ref, heads_ref, m_ref, segc_ref, segr_ref, b_ref, c_ref, dg0_ref, db0_ref, dc0_ref, rs0_ref, dg1_ref, db1_ref, dc1_ref, rs1_ref, kk_ref, dt_ref,
                 out_ref, small_ref, hs_ref, nxt, acc, hacc):
     T = bcdt_ref.shape[0]
     nc = T // L
@@ -369,10 +819,10 @@
         t0 = pl.multiple_of(c * L, L)
         here = pl.ds(t0, L)
         same = segc_ref[here, 0:1] == segr_ref[:, here]
-        dg = jnp.where(tri & same, dg_ref[c], 0.0)
+        dg = jnp.where(tri & same, dg0_ref[c] + dg1_ref[c], 0.0)
         dgb = dg.astype(bf16)
-        dcv = dc_ref[here, :] + dot(dgb, b_ref[here, :])
-        dbv = db_ref[here, :] + dot(dg.T.astype(bf16), c_ref[here, :])
+        dcv = dc0_ref[here, :] + dc1_ref[here, :] + dot(dgb, b_ref[here, :])
+        dbv = db0_ref[here, :] + db1_ref[here, :] + dot(dg.T.astype(bf16), c_ref[here, :])
         pre = pre_ref[here, :]
         sig = sigmoid(pre)
         dpre = jnp.concatenate([dbv, dcv], axis=1) * (sig + pre * sig * (1.0 - sig))
@@ -388,9 +838,9 @@
             dv = dv + taps[3 - k : 4 - k] * sk
             acc[8 + 8 * k : 16 + 8 * k, :] += eight(sk * v)
         out_ref[here, : 2 * N] = dv.astype(bf16)
-        r1 = jnp.concatenate([rs_ref[k, here, 0:HG] for k in range(G)], axis=1)
-        r2 = jnp.concatenate([rs_ref[k, here, HG : 2 * HG] for k in range(G)], axis=1)
-        r3 = jnp.concatenate([rs_ref[k, here, 2 * HG : 3 * HG] for k in range(G)], axis=1)
+        r1 = jnp.concatenate([r[k, here, 0:HG] for r in (rs0_ref, rs1_ref) for k in range(G // 2)], axis=1)
+        r2 = jnp.concatenate([r[k, here, HG : 2 * HG] for r in (rs0_ref, rs1_ref) for k in range(G // 2)], axis=1)
+        r3 = jnp.concatenate([r[k, here, 2 * HG : 3 * HG] for r in (rs0_ref, rs1_ref) for k in range(G // 2)], axis=1)
         da = dot(upper, r1, precision=HIGHEST) + dot(strict, r2, precision=HIGHEST) + kk_ref[pl.ds(c, 1), :]
         dt = dt_ref[here, :]
         raw = bcdt_ref[here, 2 * N : 2 * N + 128].astype(f32)[:, :H] + bias
@@ -408,102 +858,217 @@
         hs_ref[j : j + 1, :] = jnp.sum(hacc[8 * j : 8 * j + 8, :], axis=0, keepdims=True)
 
 
-def post(bcdt, pre, taps, heads, masks, segc, segr, b, c, dg, db, dc, rs, kk, dt):
+def post(bcdt, pre, taps, heads, masks, segc, segr, b, c, first, second, kk, dt):
     T = bcdt.shape[0]
     N = b.shape[1]
     H = dt.shape[1]
     S = jax.ShapeDtypeStruct
-    masks = jnp.pad(masks, ((0, 8), (0, 0)))
     return pl.pallas_call(
         post_kernel,
         out_shape=(S(bcdt.shape, bf16), S((8, 2 * N), f32), S((2, H), f32)),
         scratch_shapes=[pltpu.VMEM((8, 2 * N), f32), pltpu.VMEM((40, 2 * N), f32), pltpu.VMEM((16, H), f32)],
         compiler_params=pltpu.CompilerParams(vmem_limit_bytes=60 << 20),
-    )(bcdt, pre, taps, heads, masks, segc, segr, b, c, dg, db, dc, rs, kk, dt)
-
-
-def layer(hidden, grad_out, seg, w_zx, w_bcdt, w_out, conv, norm_gain, gate_gain, heads):
+    )(bcdt, pre, taps, heads, masks, segc, segr, b, c, *first, *second, kk, dt)
+
+
+KT = 384
+
+
+def tail_kernel(nd, nf, parts, *refs):
+    g_refs, refs = refs[:parts], refs[parts:]
+    dz0_ref, dz1_ref, dbc_ref, wg_ref, wa_ref, gg_ref, wo_ref, hid_ref, go_ref, r_ref, gain_ref, sum_ref, gin_ref, out_ref, dn_ref = refs[:15]
+    lhs, rhs, acc, dn = refs[15:19]
+    sc = Scatter(nd, nf, g_refs, sum_ref, *refs[19:])
+    T, D = hid_ref.shape
+    step = pl.program_id(0)
+    steps = pl.num_programs(0)
+    nk = (steps - 1) // 3
+    q = nk // 2
+    ticks = sc.plan(3, 5, 2, 14, 3)
+    run_ticks(ticks, step, TAIL_TICKS)
+
+    def load(cond, ref, src):
+        @pl.when(cond)
+        def _():
+            ref[...] = src[0] if len(src.shape) == 3 else src[...]
+
+    gate_part = step < nk
+    u_part = (step >= nk) & (step < 2 * nk)
+    bc_part = step == 2 * nk
+    out_part = step > 2 * nk
+    load((step < 2 * nk) & (step % nk < q), lhs, dz0_ref)
+    load((step < 2 * nk) & (step % nk >= q), lhs, dz1_ref)
+    load(bc_part, lhs, dbc_ref)
+    load(out_part, lhs, gg_ref)
+    load(gate_part, rhs, wg_ref)
+    load(u_part | bc_part, rhs, wa_ref)
+
+    @pl.when((step == 0) | (step == 2 * nk + 1))
+    def _():
+        acc[...] = jnp.zeros_like(acc)
+
+    BN = 256
+
+    @pl.when(step <= 2 * nk)
+    def _():
+        def block(j, carry):
+            cols = pl.ds(pl.multiple_of(j * BN, BN), BN)
+            acc[:, cols] += dot(lhs[...], rhs[cols, :], ((1,), (1,)))
+            return carry
+        lax.fori_loop(0, D // BN, block, 0)
+
+    @pl.when(out_part)
+    def _():
+        def block(j, carry):
+            cols = pl.ds(pl.multiple_of(j * BN, BN), BN)
+            acc[:, cols] += dot(lhs[...], wo_ref[:, cols])
+            return carry
+        lax.fori_loop(0, D // BN, block, 0)
+
+    @pl.when(step == 2 * nk)
+    def _():
+        gain = gain_ref[...]
+        dn[...] = jnp.zeros_like(dn)
+
+        def rows_of(i, carry):
+            here = pl.ds(pl.multiple_of(i * 64, 64), 64)
+            rows = hid_ref[here, :].astype(f32)
+            rinv = lax.rsqrt(jnp.mean(rows * rows, axis=-1, keepdims=True) + EPS)
+            xhat = rows * rinv
+            bn = acc[here, :]
+            prod = bn * xhat
+            dn[...] += jnp.sum(prod.reshape(8, 8, D), axis=0)
+            mean = jnp.mean(prod * gain, axis=-1, keepdims=True)
+            gin_ref[here, :] = (go_ref[here, :].astype(f32) + rinv * (bn * gain - xhat * mean)).astype(bf16)
+            return carry
+        lax.fori_loop(0, T // 64, rows_of, 0)
+        dn_ref[...] = jnp.sum(dn[...], axis=0, keepdims=True)
+
+    @pl.when(step == steps - 1)
+    def _():
+        def rows_of(i, carry):
+            here = pl.ds(pl.multiple_of(i * 64, 64), 64)
+            out_ref[here, :] = (hid_ref[here, :].astype(f32) + r_ref[here, :] * acc[here, :]).astype(bf16)
+            return carry
+        lax.fori_loop(0, T // 64, rows_of, 0)
+        run_rest(ticks, TAIL_TICKS)
+        sc.finish()
+
+
+def tail(nd, nf, cid, gs, dz0, dz1, dbcdt, full_gate, full_a, gg, full_out, hidden, grad_out, r, norm_gain):
     T, D = hidden.shape
-    E = w_out.shape[0]
-    H = heads.shape[1]
-    N = (conv.shape[1] - E) // 2
+    E = full_out.shape[0]
+    nk, q = E // KT, E // KT // 2
+    rows, cols = gs[0].shape[1], sum(g.shape[2] for g in gs)
+    S = jax.ShapeDtypeStruct
+    any_ = pl.BlockSpec(memory_space=pl.ANY)
+    whole = lambda s: pl.BlockSpec(s, lambda k: (0,) * len(s), pipeline_mode=pl.Buffered(1))
+    clip = jnp.clip
+    first = pl.BlockSpec((1, T, KT), lambda k: (jnp.minimum(k // nk, 1), 0, clip(jnp.minimum(k, 2 * nk - 1) % nk, 0, q - 1)))
+    second = pl.BlockSpec((1, T, KT), lambda k: (jnp.minimum(k // nk, 1), 0, clip(jnp.minimum(k, 2 * nk - 1) % nk - q, 0, q - 1)))
+    return pl.pallas_call(
+        functools.partial(tail_kernel, nd, nf, len(gs)),
+        grid=(3 * nk + 1,),
+        in_specs=[any_] * len(gs) + [
+            first, second, whole((T, KT)),
+            pl.BlockSpec((D, KT), lambda k: (0, clip(k, 0, nk - 1))), pl.BlockSpec((D, KT), lambda k: (0, clip(k - nk, 0, nk))),
+            pl.BlockSpec((T, KT), lambda k: (0, clip(k - 2 * nk - 1, 0, nk - 1))), pl.BlockSpec((KT, D), lambda k: (clip(k - 2 * nk - 1, 0, nk - 1), 0)),
+            whole((T, D)), whole((T, D)), whole((T, 1)), whole((1, D))],
+        out_specs=[whole((rows, cols)), whole((T, D)), whole((T, D)), whole((1, D))],
+        out_shape=(S((rows, cols), f32), S((T, D), bf16), S((T, D), bf16), S((1, D), f32)),
+        scratch_shapes=[pltpu.VMEM((T, KT), bf16), pltpu.VMEM((D, KT), bf16), pltpu.VMEM((T, D), f32), pltpu.VMEM((8, D), f32)]
+        + Scatter.scratch(nd, rows, cols, len(gs)),
+        compiler_params=pltpu.CompilerParams(collective_id=cid, has_side_effects=True, vmem_limit_bytes=63 << 20),
+        cost_estimate=pl.CostEstimate(flops=2 * T * D * 3 * E, bytes_accessed=8 * D * E, transcendentals=0),
+    )(*gs, dz0, dz1, dbcdt, full_gate, full_a, gg, full_out, hidden, grad_out, r, norm_gain)
+
+
+def layer(nd, nf, hidden, grad_out, seg, shard_a, shard_gate, shard_out, head_params, sizes):
+    n = nd * nf
+    E, N, H, K1, S = sizes
+    T, D = hidden.shape
+    wide = 2 * N + 128
+    full_gate = lax.all_gather(shard_gate, AXES, axis=0, tiled=True)
+    full_out = lax.all_gather(shard_out, AXES, axis=0, tiled=True)
+    full_a = gather_rows(shard_a, nd, nf, 0)
+    off = E + 2 * N + H
+    flat = full_a[:, :, off : off + S].reshape(n, -1)
+    ncol, nrow, ngate = (E + 2 * N) // n, D // n, E // n
+    conv = flat[:, : K1 * ncol].reshape(n, K1, ncol).transpose(1, 0, 2).reshape(K1, n * ncol).astype(f32)
+    norm_gain = flat[:, K1 * ncol : K1 * ncol + nrow].reshape(-1).astype(f32)
+    gate_gain = flat[:, K1 * ncol + nrow : K1 * ncol + nrow + ngate].reshape(-1).astype(f32)
+    full_a = full_a.reshape(D, E + wide)
     rows = hidden.astype(f32)
     rinv = lax.rsqrt(jnp.mean(rows * rows, axis=-1, keepdims=True) + EPS)
     xhat = rows * rinv
     normed = (xhat * norm_gain).astype(bf16)
-    zx = dot(normed, w_zx).astype(bf16)
-    bcdt = dot(normed, w_bcdt).astype(bf16)
+    ubc = dot(normed, full_a).astype(bf16)
+    gate = dot(normed, full_gate).astype(bf16)
+    bcdt = ubc[:, E:]
     pos = jnp.arange(T, dtype=jnp.int32)
     masks = jnp.stack([jnp.ones((T,), f32)] + [((jnp.roll(seg, k) == seg) & (pos >= k)).astype(f32) for k in range(1, 4)], axis=1)
     lastid = seg[L - 1 :: L]
     previd = jnp.concatenate([jnp.full((1,), -1, jnp.int32), lastid[:-1]])
     segc = jnp.stack([seg, jnp.repeat(previd, L), jnp.repeat(lastid, L)], axis=1)
     segr = seg[None, :]
-    taps_u = jnp.concatenate([conv[:, :E], gate_gain[None], jnp.repeat(heads[2], E // H)[None], jnp.zeros((1, E), f32)], axis=0)
+    taps_u = jnp.concatenate([conv[:, :E], gate_gain[None], jnp.repeat(head_params[2], E // H)[None], jnp.zeros((1, E), f32)], axis=0)
     taps_bc = jnp.concatenate([conv[:, E:], jnp.zeros((3, 2 * N), f32)], axis=0)
-    heads_p = jnp.pad(heads, ((0, 5), (0, 128 - H)))
+    heads_p = jnp.pad(head_params, ((0, 5), (0, 128 - H)))
     b, c, bt, ct, pre_bc, gm, cum4, cumr, sc, dt = prep(bcdt, taps_bc, heads_p, masks, segc, segr, N, H)
-    gg, ssq, pre, st = fwd(zx, taps_u, masks, b, c, bt, gm, cum4, cumr, sc)
+    gg, ssq, pre, st = fwd(ubc, gate, taps_u, masks, b, c, bt, gm, cum4, cumr, sc)
     r = lax.rsqrt(jnp.sum(ssq, axis=1, keepdims=True) / E + EPS)
-    output = (rows + r * dot(gg, w_out)).astype(bf16)
-    dm = dot(grad_out, w_out, ((1,), (1,))).astype(bf16)
     gos = (grad_out.astype(f32) * r).astype(bf16)
     g_out = dot(gg, gos, ((0,), (0,))).astype(bf16)
+    s_out = lax.psum_scatter(g_out, AXES, scatter_dimension=0, tiled=True).astype(f32)
+    dm = dot(grad_out, full_out, ((1,), (1,))).astype(bf16)
     s = jnp.sum(gg.astype(f32) * dm.astype(f32), axis=1, keepdims=True)
     rq = jnp.concatenate([r, r * r * r * s / E], axis=1)
-    du, dgate, dg, db, dc, rs, small, kk = bwd(zx, pre, dm, rq, taps_u, masks, b, c, ct, gm, cum4, cumr, sc, st)
+    masks8 = jnp.pad(masks, ((0, 8), (0, 0)))
+    shape = lambda g: g.reshape(n, D // n, -1)
+    grad = lambda dz: shape(dot(normed, dz, ((0,), (0,))).astype(bf16))
+    back = functools.partial(bwd, u=ubc, gate=gate, pre=pre, dm=dm, rq=rq, taps=taps_u, masks=masks8, b=b, c=c, ct=ct, gm=gm, cum4=cum4,
+                             cumr=cumr, sc=sc, st=st)
+    dz0, dg0, db0, dc0, rs0, small0, kk0 = back(0, 2)
+    dz1, dg1, db1, dc1, rs1, small1, kk1, sum0 = back(1, 2, comm=(nd, nf, 3, (grad(dz0[0]), grad(dz0[1]))))
+    small = jnp.concatenate([small0, small1], axis=1)
+    kk = jnp.concatenate([kk0, kk1], axis=1)
     kkh = jnp.sum(kk.reshape(kk.shape[0], H, E // H), axis=2)
-    dbcdt, small_bc, hs = post(bcdt, pre_bc, taps_bc, heads_p, masks, segc, segr, b, c, dg, db, dc, rs, kkh, dt)
-    g_gate = dot(normed, dgate, ((0,), (0,))).astype(bf16)
-    g_u = dot(normed, du, ((0,), (0,))).astype(bf16)
-    g_bcdt = dot(normed, dbcdt, ((0,), (0,))).astype(bf16)
-    bn = dot(dgate, w_zx[:, :E], ((1,), (1,))) + dot(du, w_zx[:, E:], ((1,), (1,))) + dot(dbcdt, w_bcdt, ((1,), (1,)))
-    gb = bn * norm_gain
-    d_rows = rinv * (gb - xhat * jnp.mean(gb * xhat, axis=-1, keepdims=True))
-    grad_in = (grad_out.astype(f32) + d_rows).astype(bf16)
-    d_norm = jnp.sum(bn * xhat, axis=0)
-    d_conv_u = jnp.stack([small[6], small[5], small[4], small[3], small[2]])
-    d_conv_bc = jnp.stack([small_bc[4], small_bc[3], small_bc[2], small_bc[1], small_bc[0]])
-    d_conv = jnp.concatenate([d_conv_u, d_conv_bc], axis=1)
+    dbcdt, small_bc, hs = post(bcdt, pre_bc, taps_bc, heads_p, masks8, segc, segr, b, c, (dg0, db0, dc0, rs0), (dg1, db1, dc1, rs1), kkh, dt)
+    sum1, grad_in, output, d_norm = tail(nd, nf, 1, (grad(dz1[0]), grad(dz1[1]), grad(dbcdt)), dz0, dz1, dbcdt, full_gate, full_a, gg, full_out,
+                                         hidden, grad_out, r, norm_gain[None])
+    d_conv = jnp.concatenate([jnp.stack([small[6], small[5], small[4], small[3], small[2]]),
+                              jnp.stack([small_bc[4], small_bc[3], small_bc[2], small_bc[1], small_bc[0]])], axis=1)
     d_heads = jnp.concatenate([hs, jnp.sum(small[1].reshape(1, H, E // H), axis=2)], axis=0)
-    return output, grad_in, g_gate, g_u, g_bcdt, g_out, d_conv, d_norm, small[0], d_heads
-
-
-AXES = ("dp", "fsdp")
-
-
-def per_device(hidden, grad_out, segment_ids, w_zx, w_bc, w_dt, w_out, conv_params, norm_gain, gate_gain, head_params):
-    n = lax.axis_size(AXES)
-    E = w_out.shape[0] * n
-    H = w_dt.shape[1]
-    gather = lambda w, axis=0: lax.all_gather(w, AXES, axis=axis, tiled=True)
-    scatter = lambda w, axis=0: lax.psum_scatter(w, AXES, scatter_dimension=axis, tiled=True)
-    pad = 128 - H
-    full_zx = gather(w_zx)
-    full_bcdt = gather(jnp.concatenate([w_bc, w_dt, jnp.zeros((w_dt.shape[0], pad), bf16)], axis=1))
-    full_out = gather(w_out)
+    mine = jnp.concatenate([d_conv.reshape(K1, n, ncol).transpose(1, 0, 2).reshape(n, -1), d_norm.reshape(n, -1), small[0].reshape(n, -1),
+                            jnp.broadcast_to(d_heads.reshape(1, -1), (n, d_heads.size))], axis=1)
+    tiles = -(-mine.shape[1] // 1024)
+    mine = jnp.pad(mine, ((0, 0), (0, tiles * 1024 - mine.shape[1]))).reshape(n, tiles * 8, 128)
+    tot = exchange(mine, nd, nf, 2).reshape(-1)
+    cut = [0, K1 * ncol, nrow, ngate, d_heads.size]
+    ends = [sum(cut[: k + 1]) for k in range(5)]
+    t_conv, t_norm, t_gate, t_heads = (tot[ends[k] : ends[k + 1]] for k in range(4))
+    Eh = E // 2
+    s_zx = jnp.concatenate([sum0[:, :Eh], sum1[:, :Eh], sum0[:, Eh:], sum1[:, Eh : 2 * Eh]], axis=1)
+    return (output, grad_in, s_zx, sum1[:, 2 * Eh : 2 * Eh + 2 * N], sum1[:, 2 * Eh + 2 * N : 2 * Eh + 2 * N + H], s_out,
+            t_conv.reshape(K1, ncol), t_norm, t_gate, t_heads.reshape(d_heads.shape))
+
+
+def per_device(nd, nf, hidden, grad_out, segment_ids, w_zx, w_bc, w_dt, w_out, conv_params, norm_gain, gate_gain, head_params):
+    n = nd * nf
+    E, N2, H = w_out.shape[0] * n, w_bc.shape[1], w_dt.shape[1]
+    rows = w_zx.shape[0]
     small = jnp.concatenate([conv_params.reshape(-1), norm_gain, gate_gain])
-    smalls = gather(small[None])
-    nc_, k1 = conv_params.shape[1], conv_params.shape[0]
-    conv = smalls[:, : k1 * nc_].reshape(n, k1, nc_).transpose(1, 0, 2).reshape(k1, n * nc_).astype(f32)
-    ng = smalls[:, k1 * nc_ : k1 * nc_ + norm_gain.shape[0]].reshape(-1).astype(f32)
-    gg = smalls[:, k1 * nc_ + norm_gain.shape[0] :].reshape(-1).astype(f32)
-    output, grad_in, g_gate, g_u, g_bcdt, g_out, d_conv, d_norm, d_gg, d_heads = layer(
-        hidden, grad_out, segment_ids, full_zx, full_bcdt, full_out, conv, ng, gg, head_params)
-    s_out = scatter(g_out).astype(f32)
-    s_zx = scatter(jnp.concatenate([g_gate, g_u], axis=1)).astype(f32)
-    s_bcdt = scatter(g_bcdt).astype(f32)
-    rows = jnp.concatenate([d_conv.reshape(k1, n, nc_).transpose(1, 0, 2).reshape(n, -1), d_norm.reshape(n, -1), d_gg.reshape(n, -1)], axis=1)
-    s_small = scatter(rows)[0]
-    N2 = w_bc.shape[1]
-    return (output, grad_in, s_zx, s_bcdt[:, :N2], s_bcdt[:, N2 : N2 + H], s_out, s_small[: k1 * nc_].reshape(k1, nc_),
-            s_small[k1 * nc_ : k1 * nc_ + norm_gain.shape[0]], s_small[k1 * nc_ + norm_gain.shape[0] :], lax.psum(d_heads, AXES))
+    S = -(-small.shape[0] // rows)
+    assert S + H <= 128
+    small = jnp.pad(small, (0, S * rows - small.shape[0])).reshape(rows, S)
+    shard_a = jnp.concatenate([w_zx[:, E:], w_bc, w_dt, small, jnp.zeros((rows, 128 - H - S), bf16)], axis=1)
+    return layer(nd, nf, hidden, grad_out, segment_ids, shard_a, w_zx[:, :E], w_out, head_params, (E, N2 // 2, H, conv_params.shape[0], S))
 
 
 def solution(mesh):
     row, col, vec, rep = P(AXES, None), P(None, AXES), P(AXES), P()
     return jax.shard_map(
-        per_device,
+        functools.partial(per_device, mesh.shape["dp"], mesh.shape["fsdp"]),
         mesh=mesh,
         in_specs=(row, row, vec, row, row, row, row, col, vec, vec, rep),
         out_specs=(row, row, row, row, row, row, col, vec, vec, rep),

time: 1050 us -> 568 us (0.54)
  waiting for transfers between devices: 564 us -> 0.75 us
  Pallas kernels: 179 us -> 392 us
  blocking collectives: 81.7 us -> 0 us
  matrix products: 149 us -> 99.2 us
  other arithmetic: 31.6 us -> 12.7 us
  local copies, waits for them, and re-layouts: 23.2 us -> 39.6 us
    reduce_scatter x3 -> x1, waiting for transfers between devices: 448 us -> 0.01 us  [layer(): lax.psum_scatter(g_out, AXES, scatter_dimension=0, tiled=True).astype(f32)]
    pallas_call x2 -> x6, Pallas kernels: 149 us -> 361 us  [the longest x2 123 us: bwd(): pl.pallas_call(kernel, grid=(Gh,), in_specs=in_specs, out_specs=out_specs...]
    all_gather x3 -> x2, waiting for transfers between devices: 112 us -> 0.02 us  [the longest x1 0.02 us: layer(): full_out = lax.all_gather(shard_out, AXES, axis=0, tiled=True)]
    dot_general x11 -> x9, matrix products: 149 us -> 99.2 us  [dot(): lax.dot_general(a, b, (dims, ((), ())), preferred_element_type=f32, preci...]
    unnamed x1 -> x0, blocking collectives: 42.5 us -> none
    psum x1 -> x0, blocking collectives: 39.2 us -> none  [per_device(): lax.psum(d_heads, AXES)]
    concatenate x5, other arithmetic: 15.6 us -> 2.71 us  [the longest x1 1.09 us: layer(): jnp.concatenate([sum0[:, :Eh], sum1[:, :Eh], sum0[:, Eh:], sum1[:, Eh:2 *...]
  transfers between devices with their start and end apart: 7 -> 3, of which waited for: 6 -> 0; matrix products, arithmetic and copies ran while one was open for 13% -> 25% of each run, Pallas kernels for 6% -> 70%
where the time goes in v3:
time: 568 us; the launch traced here: 559 us
  Pallas kernels  392 us (69%)
  matrix products  99.2 us (17%)
  local copies, waits for them, and re-layouts  39.6 us (7%)
  between operations  14.5 us (3%)
  other arithmetic  12.7 us (2%)
    pallas_call x2, Pallas kernels, bwd(): pl.pallas_call(kernel, grid=(Gh,), in_specs=in_specs, out_specs=out_specs...  123 us
    pallas_call x1, Pallas kernels, tail(): pl.pallas_call(functools.partial(tail_kernel, nd, nf, len(gs)), grid=(3 *...  103 us
    dot_general x9, matrix products, dot(): lax.dot_general(a, b, (dims, ((), ())), preferred_element_type=f32, preci...  99.2 us
    pallas_call x1, Pallas kernels, gather_rows(): pl.pallas_call(functools.partial(gather_kernel, nd, nf), out_shape=jax.Sh...  78.1 us
    pallas_call x1, Pallas kernels, fwd(): pl.pallas_call(fwd_kernel, grid=(G,), in_specs=[col(0), col(0), pl.BlockS...  47.3 us
    pallas_call x1, Pallas kernels, prep(): pl.pallas_call(prep_kernel, out_shape=(S((T, N), bf16), S((T, N), bf16),...  17.4 us
    pallas_call x1, Pallas kernels, post(): pl.pallas_call(post_kernel, out_shape=(S(bcdt.shape, bf16), S((8, 2 * N),...  13 us
  transfers between devices with their start and end apart: 3, of which 0 were waited for; matrix products, arithmetic and copies ran while one was open for 25% of the time, Pallas kernels for 70%

profile of v3, /device:TPU:0, one launch (start us, length us, event | category | flops | bytes accessed | tf_op | source)
XLA Modules:
  0.0 558.8 jit_solution(1486442192349310844)
XLA Ops:
  7.2 1.8 fusion.34
  15.1 1.6 concatenate.49.src_ref
  16.6 78.1 %shard_map.186 = bf16[32,48,3456]{2,1,0:T(8,128)(2,1)} custom-call(bf16[48,3456]{1,0:T(8,128)(2,1)} %concatenate.49.src_ref), custom_call_target="tpu_custom_call" | custom-call | tf_op jit(solution)/shard_map/pallas_call | solution.py:176
  100.2 14.4 %convolution_convert_fusion.5.u_ref.refs_0_.refs_2_ = bf16[1024,3456]{1,0:T(8,128)(2,1)S(1)} fusion(bf16[1536,3456]{1,0:T(8,128)(2,1)} %bitcast.51, bf16[1024,1536]{1,0:T(8,128)(2,1)S(1)} %copy-done.2, f32[1536]{0:T(1024)S(1)} %reshape.179, f32[1024]{0:T(1024)S(1)} %add_rsqrt_fusion.1), kind=kOutput, calls=%fused_computation.8 | convolution fusion | flops 10881466368 | bytes 20850688 | tf_op jit(solution)/shard_map/dot_general | solution.py:435
  114.6 2.9 copy-done
  124.0 17.4 %shard_map.187 = (bf16[1024,128]{1,0:T(8,128)(2,1)}, bf16[1024,128]{1,0:T(8,128)(2,1)}, bf16[128,1024]{1,0:T(8,128)(2,1)}, bf16[128,1024]{1,0:T(8,128)(2,1)}, f3...) custom-call(bf16[1024,384]{1,0:T(8,128)(2,1)} %slice.186.bcdt_ref, ...), custom_call_target="tpu_custom_call" | custom-call | tf_op jit(solution)/shard_map/pallas_call | solution.py:516
  142.1 15.2 %convolution_convert_fusion.7.gate_ref.refs_1_.refs_3_ = bf16[1024,3072]{1,0:T(8,128)(2,1)} fusion(bf16[1536,3072]{1,0:T(8,128)(2,1)} %all-gather.3.cloned.1.call-done.refs_6_, bf16[1024,1536]{1,0:T(8,128)(2,1)} %refs_10_.1, f32[1536]{0:T(1024)S(1)} %reshape.179, f32[1024]{0:T(1024)S(1)} %add_rsqrt_fusion.1), kind=kOutput, calls=%fused_computation.14 | convolution fusion | flops 9673113600 | bytes 18884608 | tf_op jit(solution)/shard_map/dot_general | solution.py:435
  157.4 47.3 %shard_map.188 = (bf16[1024,3072]{1,0:T(8,128)(2,1)}, f32[1024,128]{1,0:T(8,128)}, bf16[1024,3072]{1,0:T(8,128)(2,1)}, bf16[8,128,3072]{2,1,0:T(8,128)(2,1)}) custom-call(bf16[1024,3456]{1,0:T(8,128)(2,1)} %copy-done, bf16[1024,3072]{1,0:T(8,128)(2,1)} %convolution_convert_fusion.7.gate_ref.refs_1_.refs_3_, ...), custom_call_target="tpu_custom_call" | custom-call | flops 4831838208 | bytes 37748736 | tf_op jit(solution)/shard_map/pallas_call | solution.py:604
  205.9 15.7 %convolution_convert_fusion = bf16[3072,1536]{1,0:T(8,128)(2,1)} fusion(bf16[1024,3072]{1,0:T(8,128)(2,1)} %get-tuple-element.55.refs_8_, bf16[1024,1536]{1,0:T(8,128)(2,1)S(1)} %copy-done.9, f32[1024]{0:T(1024)S(1)} %add_rsqrt_fusion), kind=kOutput, calls=%fused_computation.1 | convolution fusion | flops 9673113600 | bytes 18878464 | tf_op jit(solution)/shard_map/dot_general | solution.py:435
  221.7 16.3 %multiply_reduce_fusion = (f32[1024]{0:T(1024)S(1)}, bf16[1024,3072]{1,0:T(8,128)(2,1)}) fusion(bf16[1024,3072]{1,0:T(8,128)(2,1)} %get-tuple-element.55.refs_8_, bf16[1024,1536]{1,0:T(8,128)(2,1)S(1)} %copy-done.9, bf16[3072,1536]{1,0:T(8,128)(2,1)} %all-gather.5.cloned.1.call-done.refs_9_), kind=kOutput, calls=%fused_computation | convolution fusion | flops 9679404032 | bytes 25169920 | tf_op jit(solution)/shard_map/dot_general | solution.py:435
  240.1 53.1 %shard_map.189 = (bf16[2,1024,1536]{2,1,0:T(8,128)(2,1)}, f32[8,128,128]{2,1,0:T(8,128)}, f32[1024,128]{1,0:T(8,128)}, f32[1024,128]{1,0:T(8,128)}, f32[6,1024,1...) custom-call(bf16[1024,3456]{1,0:T(8,128)(2,1)} %copy-done, ...), custom_call_target="tpu_custom_call" | custom-call | flops 4026531840 | bytes 25165824 | tf_op jit(solution)/shard_map/pallas_call | solution.py:785
  294.0 9.3 %convolution_convert_fusion.3 = bf16[1536,1536]{1,0:T(8,128)(2,1)} fusion(bf16[2,1024,1536]{2,1,0:T(8,128)(2,1)} %get-tuple-element.58.refs_3_, bf16[1024,1536]{1,0:T(8,128)(2,1)S(1)} %copy-done.3, f32[1536]{0:T(1024)S(1)} %reshape.179, f32[1024]{0:T(1024)S(1)} %add_rsqrt_fusion.1), kind=kOutput, calls=%fused_computation.6 | convolution fusion | flops 4840488960 | bytes 11020288 | tf_op jit(solution)/shard_map/dot_general | solution.py:435
  303.3 7.5 %convolution_convert_fusion.4 = bf16[1536,1536]{1,0:T(8,128)(2,1)} fusion(bf16[2,1024,1536]{2,1,0:T(8,128)(2,1)S(1)} %copy-done.8, bf16[1024,1536]{1,0:T(8,128)(2,1)S(1)} %copy-done.3, f32[1536]{0:T(1024)S(1)} %reshape.179, f32[1024]{0:T(1024)S(1)} %add_rsqrt_fusion.1), kind=kOutput, calls=%fused_computation.7 | convolution fusion | flops 4840488960 | bytes 11022336 | tf_op jit(solution)/shard_map/dot_general | solution.py:435
  310.8 69.7 %shard_map.190 = (bf16[2,1024,1536]{2,1,0:T(8,128)(2,1)}, f32[8,128,128]{2,1,0:T(8,128)}, f32[1024,128]{1,0:T(8,128)}, f32[1024,128]{1,0:T(8,128)}, f32[6,1024,1...) custom-call(bf16[32,48,1536]{2,1,0:T(8,128)(2,1)} %bitcast.54, ...), custom_call_target="tpu_custom_call" | custom-call | flops 4026531840 | bytes 25165824 | tf_op jit(solution)/shard_map/pallas_call | solution.py:785
  383.2 13.0 %shard_map.191 = (bf16[1024,384]{1,0:T(8,128)(2,1)}, f32[8,256]{1,0:T(8,128)}, f32[2,48]{1,0:T(2,128)}) custom-call(bf16[1024,384]{1,0:T(8,128)(2,1)} %slice.186.bcdt_ref, f32[1024,256]{1,0:T(8,128)} %get-tuple-element.60.pre_ref, f32[8,256]{1,0:T(8,128)} %concatenate.54.taps_ref, f32[8,128]{1,0:T(8,128)} %pad.18.heads_ref, ...), custom_call_target="tpu_custom_call" | custom-call | tf_op jit(solution)/shard_map/pallas_call | solution.py:866
  398.5 4.2 convolution_convert_fusion.8
  402.7 9.1 %convolution_convert_fusion.1 = bf16[1536,1536]{1,0:T(8,128)(2,1)} fusion(bf16[2,1024,1536]{2,1,0:T(8,128)(2,1)} %get-tuple-element.59.refs_4_, bf16[1024,1536]{1,0:T(8,128)(2,1)S(1)} %copy-done.3, f32[1536]{0:T(1024)S(1)} %reshape.179, f32[1024]{0:T(1024)S(1)} %add_rsqrt_fusion.1), kind=kOutput, calls=%fused_computation.4 | convolution fusion | flops 4840488960 | bytes 11020288 | tf_op jit(solution)/shard_map/dot_general | solution.py:435
  411.9 7.4 %convolution_convert_fusion.2 = bf16[1536,1536]{1,0:T(8,128)(2,1)} fusion(bf16[2,1024,1536]{2,1,0:T(8,128)(2,1)S(1)} %bitcast.80, bf16[1024,1536]{1,0:T(8,128)(2,1)S(1)} %copy-done.3, f32[1536]{0:T(1024)S(1)} %reshape.179, f32[1024]{0:T(1024)S(1)} %add_rsqrt_fusion.1), kind=kOutput, calls=%fused_computation.5 | convolution fusion | flops 4840488960 | bytes 11022336 | tf_op jit(solution)/shard_map/dot_general | solution.py:435
  419.2 102.5 %shard_map.192 = (f32[48,3456]{1,0:T(8,128)}, bf16[1024,1536]{1,0:T(8,128)(2,1)}, bf16[1024,1536]{1,0:T(8,128)(2,1)}, f32[1,1536]{1,0:T(1,128)}) custom-call(bf16[32,48,1536]{2,1,0:T(8,128)(2,1)} %bitcast.82, bf16[32,48,1536]{2,1,0:T(8,128)(2,1)} %bitcast.81, bf16[32,48,384]{2,1,0:T(8,128)(2,1)} %bitcast.83, ...), custom_call_target="tpu_custom_call" | custom-call | flops 28991029248 | bytes 37748736 | tf_op jit(solution)/shard_map/pallas_call | solution.py:969
  523.4 10.7 %shard_map.193 = f32[8,128]{1,0:T(8,128)} custom-call(f32[32,8,128]{2,1,0:T(8,128)} %bitcast.55), custom_call_target="tpu_custom_call" | custom-call | tf_op jit(solution)/shard_map/pallas_call | solution.py:424
  537.4 1.4 slice.164
  544.5 1.8 convert_element_type.128
  546.4 3.8 copy.96
  550.1 1.7 copy.97
  (112 shorter events, 38.3 us)
Async XLA Ops:
  7.2 135.0 %all-gather.3.cloned.1.call-start = ((), (), s32[]{:S(2)}) async-start(), calls=%async_computation.1 | async-start | bytes 9732096 | tf_op jit(solution)/shard_map/all_gather | solution.py:991
  9.1 212.6 %all-gather.5.cloned.1.call-start = ((), (), s32[]{:S(2)}) async-start(), calls=%async_computation.2 | async-start | bytes 9732096 | tf_op jit(solution)/shard_map/all_gather | solution.py:992
  9.8 534.7 %reduce-scatter.2.cloned.1.call-start = ((), (), s32[]{:S(2)}) async-start(), calls=%async_computation.3 | async-start | bytes 9732096 | tf_op jit(solution)/shard_map/reduce_scatter | solution.py:1022
  16.6 82.8 %copy-start.2 = (bf16[1024,1536]{1,0:T(8,128)(2,1)S(1)}, bf16[1024,1536]{1,0:T(8,128)(2,1)}, u32[]{:S(2)}) copy-start(bf16[1024,1536]{1,0:T(8,128)(2,1)} %refs_10_.1) | copy-start | bytes 9437188
  100.2 18.3 %copy-start.5 = (s32[1024]{0:T(1024)S(1)}, s32[1024]{0:T(1024)}, u32[]{:S(2)}) copy-start(s32[1024]{0:T(1024)} %param.13) | copy-start | bytes 12292
  100.2 21.3 %copy-start.7 = (f32[3,48]{1,0:T(4,128)S(1)}, f32[3,48]{1,0:T(4,128)}, u32[]{:S(2)}) copy-start(f32[3,48]{1,0:T(4,128)} %param.21) | copy-start | bytes 1732
  114.6 2.9 copy-start
  119.5 4.5 copy-start.1
  157.4 48.6 %copy-start.9 = (bf16[1024,1536]{1,0:T(8,128)(2,1)S(1)}, bf16[1024,1536]{1,0:T(8,128)(2,1)}, u32[]{:S(2)}) copy-start(bf16[1024,1536]{1,0:T(8,128)(2,1)} %refs_11_.1) | copy-start | bytes 9437188
  240.1 53.9 %copy-start.3 = (bf16[1024,1536]{1,0:T(8,128)(2,1)S(1)}, bf16[1024,1536]{1,0:T(8,128)(2,1)}, u32[]{:S(2)}) copy-start(bf16[1024,1536]{1,0:T(8,128)(2,1)} %refs_10_.1) | copy-start | bytes 9437188
  294.0 9.3 %copy-start.8 = (bf16[2,1024,1536]{2,1,0:T(8,128)(2,1)S(1)}, bf16[2,1024,1536]{2,1,0:T(8,128)(2,1)}, u32[]{:S(2)}) copy-start(bf16[2,1024,1536]{2,1,0:T(8,128)(2,1)} %get-tuple-element.58.refs_3_) | copy-start | bytes 18874372
  310.8 70.8 %copy-start.6 = (f32[8,1536]{1,0:T(8,128)S(1)}, f32[8,1536]{1,0:T(8,128)}, u32[]{:S(2)}) copy-start(f32[8,1536]{1,0:T(8,128)} %get-tuple-element.69) | copy-start | bytes 147460
  398.5 13.4 %slice-start = ((s8[6291456]{0:T(1024)(128)(4,1)}), s8[4194304]{0:T(1024)(128)(4,1)S(1)}, s32[]{:S(2)}) async-start(s8[6291456]{0:T(1024)(128)(4,1)} %bitcast.79), calls=%async_computation.4 | async-start | bytes 8388608
  402.7 9.1 %slice-start.1 = ((s8[6291456]{0:T(1024)(128)(4,1)}), s8[2097152]{0:T(1024)(128)(4,1)S(1)}, s32[]{:S(2)}) async-start(s8[6291456]{0:T(1024)(128)(4,1)} %bitcast.79), calls=%async_computation.5 | async-start | bytes 4194304
  522.7 27.4 %copy-start.4 = (bf16[1024,1536]{1,0:T(8,128)(2,1)S(1)}, bf16[1024,1536]{1,0:T(8,128)(2,1)}, u32[]{:S(2)}) copy-start(bf16[1024,1536]{1,0:T(8,128)(2,1)} %get-tuple-element.118) | copy-start | bytes 9437188
Sparse Core Ops, SparseCore 0:
  10.9 97.3 all-gather.2
  111.2 82.2 all-gather.4
  221.8 141.6 reduce-scatter.1

commit v4 on v3

--- a/solution.py
+++ b/solution.py
@@ -11,7 +11,8 @@
 HG = 4
 LOG2E = 1.4426950408889634
 BWD_TICKS = 44
-TAIL_TICKS = 22
+TAIL_TICKS = 44
+TAIL_PLAN = (8, 14, 4, 28, 4)
 bf16, f32 = jnp.bfloat16, jnp.float32
 HIGHEST = lax.Precision.HIGHEST
 
@@ -222,10 +223,10 @@
             return remote(acc.at[zs, 2], xy_in.at[1, zs], (z, 1 - y, x, c), y_send.at[zs], y_recv.at[zs])
 
         def up(zs):
-            return remote(acc.at[zs, 0], z_in.at[0, zs], (z + 1, y, x, c), z_send.at[zs], z_recv.at[0, zs])
+            return remote(acc.at[zs, 0], z_in.at[zs + 1], (z + 1, y, x, c), z_send.at[zs], z_recv.at[0, zs])
 
         def down(zs):
-            return remote(acc.at[zs, 0], z_in.at[1, zs], (z - 1, y, x, c), z_send.at[zs], z_recv.at[1, zs])
+            return remote(acc.at[zs, 0], z_in.at[zs], (z - 1, y, x, c), z_send.at[zs], z_recv.at[1, zs])
 
         def each(dist, fn):
             if dist == 0:
@@ -295,7 +296,7 @@
                 @pl.when(z > 0)
                 def _():
                     up(zs).wait_recv()
-                    acc[zs, 0] = (total + z_in[0, zs].astype(f32)).astype(bf16)
+                    acc[zs, 0] = (total + z_in[zs + 1].astype(f32)).astype(bf16)
 
                 @pl.when(z == 0)
                 def _():
@@ -307,7 +308,7 @@
                 @pl.when(z < zn - 1)
                 def _():
                     down(zs).wait_recv()
-                    acc[zs, 0] = (total + z_in[1, zs].astype(f32)).astype(bf16)
+                    acc[zs, 0] = (total + z_in[zs].astype(f32)).astype(bf16)
 
                 @pl.when(z == zn - 1)
                 def _():
@@ -320,12 +321,12 @@
             @pl.when(z > 0)
             def _():
                 up(z).wait_recv()
-                out_ref[...] += z_in[0, z].astype(f32)
+                out_ref[...] += z_in[z + 1].astype(f32)
 
             @pl.when(z < zn - 1)
             def _():
                 down(z).wait_recv()
-                out_ref[...] += z_in[1, z].astype(f32)
+                out_ref[...] += z_in[z].astype(f32)
 
             def sent(zs):
                 for col in range(4):
@@ -359,7 +360,7 @@
         zn = nd // 2
         D, V = pltpu.SemaphoreType.DMA, pltpu.VMEM
         return [V((zn, 4, rows, cols), bf16), V((zn, 4, rows, cols), bf16), V((zn, rows, cols), bf16), V((2, zn, rows, cols), bf16),
-                V((2, zn, rows, cols), bf16), D((zn, 4, parts)), D((zn, 4, parts)), D((zn, 4, parts))] + [D((zn,))] * 9 + [D((2, zn))]
+                V((zn + 1, rows, cols), bf16), D((zn, 4, parts)), D((zn, 4, parts)), D((zn, 4, parts))] + [D((zn,))] * 9 + [D((2, zn))]
 
 
 def run_ticks(ticks, now, last):
@@ -623,7 +624,6 @@
     own, comm = refs[parts + 23 : parts + 26], refs[parts + 26 :]
     sc = Scatter(nd, nf, g_refs, outs[7], *comm)
     nc = ins[0].shape[0] // L
-    last = pl.num_programs(0) * nc - 1
     ticks = sc.plan(7, 12, 3, 28, 6)
     bwd_body(lambda now: run_ticks(ticks, now, BWD_TICKS), *ins, *outs[:7], *own)
 
@@ -871,64 +871,57 @@
     )(bcdt, pre, taps, heads, masks, segc, segr, b, c, *first, *second, kk, dt)
 
 
-KT = 384
-
-
-def tail_kernel(nd, nf, parts, *refs):
+NT = 256
+
+
+def tail_kernel(nd, nf, parts, gg_tiles, *refs):
     g_refs, refs = refs[:parts], refs[parts:]
-    dz0_ref, dz1_ref, dbc_ref, wg_ref, wa_ref, gg_ref, wo_ref, hid_ref, go_ref, r_ref, gain_ref, sum_ref, gin_ref, out_ref, dn_ref = refs[:15]
-    lhs, rhs, acc, dn = refs[15:19]
-    sc = Scatter(nd, nf, g_refs, sum_ref, *refs[19:])
-    T, D = hid_ref.shape
+    wo_hbm, wg_hbm, wa_hbm, gg_ref, dz0_ref, dz1_ref, dbc_ref, hid_ref, go_ref, r_ref, gain_ref, sum_ref, out_ref, gin_ref, dn_ref = refs[:15]
+    wo, wg, wa, acc, dn, sem = refs[15:21]
+    sc = Scatter(nd, nf, g_refs, sum_ref, *refs[21:])
+    D, E = wg.shape
+    Eh = E // 2
     step = pl.program_id(0)
-    steps = pl.num_programs(0)
-    nk = (steps - 1) // 3
-    q = nk // 2
-    ticks = sc.plan(3, 5, 2, 14, 3)
-    run_ticks(ticks, step, TAIL_TICKS)
-
-    def load(cond, ref, src):
-        @pl.when(cond)
-        def _():
-            ref[...] = src[0] if len(src.shape) == 3 else src[...]
-
-    gate_part = step < nk
-    u_part = (step >= nk) & (step < 2 * nk)
-    bc_part = step == 2 * nk
-    out_part = step > 2 * nk
-    load((step < 2 * nk) & (step % nk < q), lhs, dz0_ref)
-    load((step < 2 * nk) & (step % nk >= q), lhs, dz1_ref)
-    load(bc_part, lhs, dbc_ref)
-    load(out_part, lhs, gg_ref)
-    load(gate_part, rhs, wg_ref)
-    load(u_part | bc_part, rhs, wa_ref)
-
-    @pl.when((step == 0) | (step == 2 * nk + 1))
+    tiles = gg_tiles
+    blocks = D // NT
+    ticks = sc.plan(*TAIL_PLAN)
+    fetch = [pltpu.make_async_copy(src, dst, sem.at[k]) for k, (src, dst) in enumerate(((wo_hbm, wo), (wg_hbm, wg), (wa_hbm, wa)))]
+
+    @pl.when(step == 0)
     def _():
-        acc[...] = jnp.zeros_like(acc)
-
-    BN = 256
-
-    @pl.when(step <= 2 * nk)
+        for cp in fetch:
+            cp.start()
+        dn[...] = jnp.zeros_like(dn)
+        run_ticks(ticks, 0, 0)
+        fetch[0].wait()
+
+    @pl.when(step == tiles)
+    def _():
+        fetch[1].wait()
+        fetch[2].wait()
+
+    @pl.when(step < tiles)
     def _():
         def block(j, carry):
-            cols = pl.ds(pl.multiple_of(j * BN, BN), BN)
-            acc[:, cols] += dot(lhs[...], rhs[cols, :], ((1,), (1,)))
+            now = step * blocks + j
+            run_ticks({t: f for t, f in ticks.items() if 0 < t}, now, min(TAIL_TICKS, tiles * blocks - 1))
+            cols = pl.ds(pl.multiple_of(j * NT, NT), NT)
+            out_ref[:, cols] = (hid_ref[:, cols].astype(f32) + r_ref[...] * dot(gg_ref[...], wo[:, cols])).astype(bf16)
             return carry
-        lax.fori_loop(0, D // BN, block, 0)
-
-    @pl.when(out_part)
+        lax.fori_loop(0, blocks, block, 0)
+
+    @pl.when(step >= tiles)
     def _():
         def block(j, carry):
-            cols = pl.ds(pl.multiple_of(j * BN, BN), BN)
-            acc[:, cols] += dot(lhs[...], wo_ref[:, cols])
+            now = step * blocks + j
+            run_ticks({t: f for t, f in ticks.items() if t >= tiles * blocks}, now, TAIL_TICKS)
+            cols = pl.ds(pl.multiple_of(j * NT, NT), NT)
+            part = dot(dz0_ref[0], wg[cols, :Eh], ((1,), (1,))) + dot(dz1_ref[0], wg[cols, Eh:], ((1,), (1,)))
+            part = part + dot(dz0_ref[1], wa[cols, :Eh], ((1,), (1,))) + dot(dz1_ref[1], wa[cols, Eh:E], ((1,), (1,)))
+            acc[:, cols] = part + dot(dbc_ref[...], wa[cols, E:], ((1,), (1,)))
             return carry
-        lax.fori_loop(0, D // BN, block, 0)
-
-    @pl.when(step == 2 * nk)
-    def _():
+        lax.fori_loop(0, blocks, block, 0)
         gain = gain_ref[...]
-        dn[...] = jnp.zeros_like(dn)
 
         def rows_of(i, carry):
             here = pl.ds(pl.multiple_of(i * 64, 64), 64)
@@ -941,16 +934,11 @@
             mean = jnp.mean(prod * gain, axis=-1, keepdims=True)
             gin_ref[here, :] = (go_ref[here, :].astype(f32) + rinv * (bn * gain - xhat * mean)).astype(bf16)
             return carry
-        lax.fori_loop(0, T // 64, rows_of, 0)
+        lax.fori_loop(0, hid_ref.shape[0] // 64, rows_of, 0)
+
+    @pl.when(step == 2 * tiles - 1)
+    def _():
         dn_ref[...] = jnp.sum(dn[...], axis=0, keepdims=True)
-
-    @pl.when(step == steps - 1)
-    def _():
-        def rows_of(i, carry):
-            here = pl.ds(pl.multiple_of(i * 64, 64), 64)
-            out_ref[here, :] = (hid_ref[here, :].astype(f32) + r_ref[here, :] * acc[here, :]).astype(bf16)
-            return carry
-        lax.fori_loop(0, T // 64, rows_of, 0)
         run_rest(ticks, TAIL_TICKS)
         sc.finish()
 
@@ -958,29 +946,28 @@
 def tail(nd, nf, cid, gs, dz0, dz1, dbcdt, full_gate, full_a, gg, full_out, hidden, grad_out, r, norm_gain):
     T, D = hidden.shape
     E = full_out.shape[0]
-    nk, q = E // KT, E // KT // 2
     rows, cols = gs[0].shape[1], sum(g.shape[2] for g in gs)
+    MT = 256 if rows % 16 == 0 else 128
+    tiles = T // MT
+    wide = dbcdt.shape[1]
     S = jax.ShapeDtypeStruct
     any_ = pl.BlockSpec(memory_space=pl.ANY)
     whole = lambda s: pl.BlockSpec(s, lambda k: (0,) * len(s), pipeline_mode=pl.Buffered(1))
-    clip = jnp.clip
-    first = pl.BlockSpec((1, T, KT), lambda k: (jnp.minimum(k // nk, 1), 0, clip(jnp.minimum(k, 2 * nk - 1) % nk, 0, q - 1)))
-    second = pl.BlockSpec((1, T, KT), lambda k: (jnp.minimum(k // nk, 1), 0, clip(jnp.minimum(k, 2 * nk - 1) % nk - q, 0, q - 1)))
+    early = lambda w: pl.BlockSpec((MT, w), lambda k: (jnp.minimum(k, tiles - 1), 0))
+    late = lambda w: pl.BlockSpec((MT, w), lambda k: (jnp.maximum(k - tiles, 0), 0))
+    both = lambda w: pl.BlockSpec((MT, w), lambda k: (lax.rem(k, tiles), 0))
+    half = pl.BlockSpec((2, MT, E // 2), lambda k: (0, jnp.maximum(k - tiles, 0), 0))
     return pl.pallas_call(
-        functools.partial(tail_kernel, nd, nf, len(gs)),
-        grid=(3 * nk + 1,),
-        in_specs=[any_] * len(gs) + [
-            first, second, whole((T, KT)),
-            pl.BlockSpec((D, KT), lambda k: (0, clip(k, 0, nk - 1))), pl.BlockSpec((D, KT), lambda k: (0, clip(k - nk, 0, nk))),
-            pl.BlockSpec((T, KT), lambda k: (0, clip(k - 2 * nk - 1, 0, nk - 1))), pl.BlockSpec((KT, D), lambda k: (clip(k - 2 * nk - 1, 0, nk - 1), 0)),
-            whole((T, D)), whole((T, D)), whole((T, 1)), whole((1, D))],
-        out_specs=[whole((rows, cols)), whole((T, D)), whole((T, D)), whole((1, D))],
+        functools.partial(tail_kernel, nd, nf, len(gs), tiles),
+        grid=(2 * tiles,),
+        in_specs=[any_] * (len(gs) + 3) + [early(E), half, half, late(wide), both(D), late(D), early(1), whole((1, D))],
+        out_specs=[whole((rows, cols)), early(D), late(D), whole((1, D))],
         out_shape=(S((rows, cols), f32), S((T, D), bf16), S((T, D), bf16), S((1, D), f32)),
-        scratch_shapes=[pltpu.VMEM((T, KT), bf16), pltpu.VMEM((D, KT), bf16), pltpu.VMEM((T, D), f32), pltpu.VMEM((8, D), f32)]
-        + Scatter.scratch(nd, rows, cols, len(gs)),
-        compiler_params=pltpu.CompilerParams(collective_id=cid, has_side_effects=True, vmem_limit_bytes=63 << 20),
+        scratch_shapes=[pltpu.VMEM((E, D), bf16), pltpu.VMEM((D, E), bf16), pltpu.VMEM((D, E + wide), bf16), pltpu.VMEM((MT, D), f32),
+                        pltpu.VMEM((8, D), f32), pltpu.SemaphoreType.DMA((3,))] + Scatter.scratch(nd, rows, cols, len(gs)),
+        compiler_params=pltpu.CompilerParams(collective_id=cid, has_side_effects=True, vmem_limit_bytes=67043328),
         cost_estimate=pl.CostEstimate(flops=2 * T * D * 3 * E, bytes_accessed=8 * D * E, transcendentals=0),
-    )(*gs, dz0, dz1, dbcdt, full_gate, full_a, gg, full_out, hidden, grad_out, r, norm_gain)
+    )(*gs, full_out, full_gate, full_a, gg, dz0, dz1, dbcdt, hidden, grad_out, r, norm_gain)
 
 
 def layer(nd, nf, hidden, grad_out, seg, shard_a, shard_gate, shard_out, head_params, sizes):
@@ -1019,7 +1006,6 @@
     r = lax.rsqrt(jnp.sum(ssq, axis=1, keepdims=True) / E + EPS)
     gos = (grad_out.astype(f32) * r).astype(bf16)
     g_out = dot(gg, gos, ((0,), (0,))).astype(bf16)
-    s_out = lax.psum_scatter(g_out, AXES, scatter_dimension=0, tiled=True).astype(f32)
     dm = dot(grad_out, full_out, ((1,), (1,))).astype(bf16)
     s = jnp.sum(gg.astype(f32) * dm.astype(f32), axis=1, keepdims=True)
     rq = jnp.concatenate([r, r * r * r * s / E], axis=1)
@@ -1028,13 +1014,13 @@
     grad = lambda dz: shape(dot(normed, dz, ((0,), (0,))).astype(bf16))
     back = functools.partial(bwd, u=ubc, gate=gate, pre=pre, dm=dm, rq=rq, taps=taps_u, masks=masks8, b=b, c=c, ct=ct, gm=gm, cum4=cum4,
                              cumr=cumr, sc=sc, st=st)
-    dz0, dg0, db0, dc0, rs0, small0, kk0 = back(0, 2)
+    dz0, dg0, db0, dc0, rs0, small0, kk0, s_out = back(0, 2, comm=(nd, nf, 4, (g_out.reshape(n, E // n, D),)))
     dz1, dg1, db1, dc1, rs1, small1, kk1, sum0 = back(1, 2, comm=(nd, nf, 3, (grad(dz0[0]), grad(dz0[1]))))
     small = jnp.concatenate([small0, small1], axis=1)
     kk = jnp.concatenate([kk0, kk1], axis=1)
     kkh = jnp.sum(kk.reshape(kk.shape[0], H, E // H), axis=2)
     dbcdt, small_bc, hs = post(bcdt, pre_bc, taps_bc, heads_p, masks8, segc, segr, b, c, (dg0, db0, dc0, rs0), (dg1, db1, dc1, rs1), kkh, dt)
-    sum1, grad_in, output, d_norm = tail(nd, nf, 1, (grad(dz1[0]), grad(dz1[1]), grad(dbcdt)), dz0, dz1, dbcdt, full_gate, full_a, gg, full_out,
+    sum1, output, grad_in, d_norm = tail(nd, nf, 1, (grad(dz1[0]), grad(dz1[1]), grad(dbcdt)), dz0, dz1, dbcdt, full_gate, full_a, gg, full_out,
                                          hidden, grad_out, r, norm_gain[None])
     d_conv = jnp.concatenate([jnp.stack([small[6], small[5], small[4], small[3], small[2]]),
                               jnp.stack([small_bc[4], small_bc[3], small_bc[2], small_bc[1], small_bc[0]])], axis=1)

time: 568 us -> 545 us (0.960)
  Pallas kernels: 392 us -> 367 us
    pallas_call x1, Pallas kernels: 103 us -> 71.3 us  [tail(): pl.pallas_call(functools.partial(tail_kernel, nd, nf, len(gs), tiles), gr...]
  transfers between devices with their start and end apart: 3 -> 2, of which waited for: 0 -> 0; matrix products, arithmetic and copies ran while one was open for 25% -> 13% of each run, Pallas kernels for 70% -> 27%
where the time goes in v4:
time: 545 us; the launch traced here: 536 us
  Pallas kernels  367 us (67%)
  matrix products  99.9 us (18%)
  local copies, waits for them, and re-layouts  41.8 us (8%)
  between operations  14.9 us (3%)
  other arithmetic  11.7 us (2%)
    pallas_call x2, Pallas kernels, bwd(): pl.pallas_call(kernel, grid=(Gh,), in_specs=in_specs, out_specs=out_specs...  125 us
    dot_general x9, matrix products, dot(): lax.dot_general(a, b, (dims, ((), ())), preferred_element_type=f32, preci...  99.9 us
    pallas_call x1, Pallas kernels, gather_rows(): pl.pallas_call(functools.partial(gather_kernel, nd, nf), out_shape=jax.Sh...  78.4 us
    pallas_call x1, Pallas kernels, tail(): pl.pallas_call(functools.partial(tail_kernel, nd, nf, len(gs), tiles), gr...  71.3 us
    pallas_call x1, Pallas kernels, fwd(): pl.pallas_call(fwd_kernel, grid=(G,), in_specs=[col(0), col(0), pl.BlockS...  47.2 us
    pallas_call x1, Pallas kernels, prep(): pl.pallas_call(prep_kernel, out_shape=(S((T, N), bf16), S((T, N), bf16),...  17.4 us
    pallas_call x1, Pallas kernels, exchange(): pl.pallas_call(functools.partial(exchange_kernel, nd, nf), out_shape=jax....  14.6 us
    pallas_call x1, Pallas kernels, post(): pl.pallas_call(post_kernel, out_shape=(S(bcdt.shape, bf16), S((8, 2 * N),...  13.1 us
  transfers between devices with their start and end apart: 2, of which 0 were waited for; matrix products, arithmetic and copies ran while one was open for 13% of the time, Pallas kernels for 27%

profile of v4, /device:TPU:0, one launch (start us, length us, event | category | flops | bytes accessed | tf_op | source)
XLA Modules:
  0.0 535.6 jit_solution(10711997078587023618)
XLA Ops:
  7.2 1.8 fusion.34
  15.5 1.6 concatenate.49.src_ref
  17.1 78.4 %shard_map.186 = bf16[32,48,3456]{2,1,0:T(8,128)(2,1)} custom-call(bf16[48,3456]{1,0:T(8,128)(2,1)} %concatenate.49.src_ref), custom_call_target="tpu_custom_call" | custom-call | tf_op jit(solution)/shard_map/pallas_call | solution.py:177
  101.0 14.4 %convolution_convert_fusion.5.u_ref.refs_1_.refs_2_ = bf16[1024,3456]{1,0:T(8,128)(2,1)S(1)} fusion(bf16[1536,3456]{1,0:T(8,128)(2,1)} %bitcast.52, bf16[1024,1536]{1,0:T(8,128)(2,1)S(1)} %copy-done.2, f32[1536]{0:T(1024)S(1)} %reshape.183, f32[1024]{0:T(1024)S(1)} %add_rsqrt_fusion.1), kind=kOutput, calls=%fused_computation.8 | convolution fusion | flops 10881466368 | bytes 20850688 | tf_op jit(solution)/shard_map/dot_general | solution.py:436
  115.4 2.9 copy-done
  124.8 17.4 %shard_map.187 = (bf16[1024,128]{1,0:T(8,128)(2,1)}, bf16[1024,128]{1,0:T(8,128)(2,1)}, bf16[128,1024]{1,0:T(8,128)(2,1)}, bf16[128,1024]{1,0:T(8,128)(2,1)}, f3...) custom-call(bf16[1024,384]{1,0:T(8,128)(2,1)} %slice.186.bcdt_ref, ...), custom_call_target="tpu_custom_call" | custom-call | tf_op jit(solution)/shard_map/pallas_call | solution.py:517
  142.9 15.3 %convolution_convert_fusion.7.gate_ref.refs_2_.refs_3_ = bf16[1024,3072]{1,0:T(8,128)(2,1)} fusion(bf16[1536,3072]{1,0:T(8,128)(2,1)} %all-gather.3.cloned.1.call-done.refs_4_, bf16[1024,1536]{1,0:T(8,128)(2,1)} %refs_10_.1, f32[1536]{0:T(1024)S(1)} %reshape.183, f32[1024]{0:T(1024)S(1)} %add_rsqrt_fusion.1), kind=kOutput, calls=%fused_computation.14 | convolution fusion | flops 9673113600 | bytes 18884608 | tf_op jit(solution)/shard_map/dot_general | solution.py:436
  158.1 47.2 %shard_map.188 = (bf16[1024,3072]{1,0:T(8,128)(2,1)}, f32[1024,128]{1,0:T(8,128)}, bf16[1024,3072]{1,0:T(8,128)(2,1)}, bf16[8,128,3072]{2,1,0:T(8,128)(2,1)}) custom-call(bf16[1024,3456]{1,0:T(8,128)(2,1)} %copy-done, bf16[1024,3072]{1,0:T(8,128)(2,1)} %convolution_convert_fusion.7.gate_ref.refs_2_.refs_3_, ...), custom_call_target="tpu_custom_call" | custom-call | flops 4831838208 | bytes 37748736 | tf_op jit(solution)/shard_map/pallas_call | solution.py:605
  206.6 16.6 %convolution_convert_fusion = bf16[3072,1536]{1,0:T(8,128)(2,1)} fusion(bf16[1024,3072]{1,0:T(8,128)(2,1)} %get-tuple-element.54.refs_6_, bf16[1024,1536]{1,0:T(8,128)(2,1)} %refs_11_.1, f32[1024]{0:T(1024)S(1)} %add_rsqrt_fusion), kind=kOutput, calls=%fused_computation.1 | convolution fusion | flops 9673113600 | bytes 18878464 | tf_op jit(solution)/shard_map/dot_general | solution.py:436
  223.2 16.1 %multiply_reduce_fusion = (f32[1024]{0:T(1024)S(1)}, bf16[1024,3072]{1,0:T(8,128)(2,1)}) fusion(bf16[1024,3072]{1,0:T(8,128)(2,1)} %get-tuple-element.54.refs_6_, bf16[1024,1536]{1,0:T(8,128)(2,1)S(1)} %copy-done.19, bf16[3072,1536]{1,0:T(8,128)(2,1)} %all-gather.5.cloned.1.call-done.refs_3_), kind=kOutput, calls=%fused_computation | convolution fusion | flops 9679404032 | bytes 25169920 | tf_op jit(solution)/shard_map/dot_general | solution.py:436
  240.4 61.2 %shard_map.189 = (bf16[2,1024,1536]{2,1,0:T(8,128)(2,1)}, f32[8,128,128]{2,1,0:T(8,128)}, f32[1024,128]{1,0:T(8,128)}, f32[1024,128]{1,0:T(8,128)}, f32[6,1024,1...) custom-call(bf16[32,96,1536]{2,1,0:T(8,128)(2,1)} %bitcast.54, ...), custom_call_target="tpu_custom_call" | custom-call | flops 4026531840 | bytes 25165824 | tf_op jit(solution)/shard_map/pallas_call | solution.py:785
  301.6 9.2 %convolution_convert_fusion.3 = bf16[1536,1536]{1,0:T(8,128)(2,1)} fusion(bf16[2,1024,1536]{2,1,0:T(8,128)(2,1)} %get-tuple-element.59.refs_7_, bf16[1024,1536]{1,0:T(8,128)(2,1)S(1)} %copy-done.3, f32[1536]{0:T(1024)S(1)} %reshape.183, f32[1024]{0:T(1024)S(1)} %add_rsqrt_fusion.1), kind=kOutput, calls=%fused_computation.6 | convolution fusion | flops 4840488960 | bytes 11020288 | tf_op jit(solution)/shard_map/dot_general | solution.py:436
  310.7 7.6 %convolution_convert_fusion.4 = bf16[1536,1536]{1,0:T(8,128)(2,1)} fusion(bf16[2,1024,1536]{2,1,0:T(8,128)(2,1)S(1)} %copy-done.17, bf16[1024,1536]{1,0:T(8,128)(2,1)S(1)} %copy-done.3, f32[1536]{0:T(1024)S(1)} %reshape.183, f32[1024]{0:T(1024)S(1)} %add_rsqrt_fusion.1), kind=kOutput, calls=%fused_computation.7 | convolution fusion | flops 4840488960 | bytes 11022336 | tf_op jit(solution)/shard_map/dot_general | solution.py:436
  318.4 63.5 %shard_map.190 = (bf16[2,1024,1536]{2,1,0:T(8,128)(2,1)}, f32[8,128,128]{2,1,0:T(8,128)}, f32[1024,128]{1,0:T(8,128)}, f32[1024,128]{1,0:T(8,128)}, f32[6,1024,1...) custom-call(bf16[32,48,1536]{2,1,0:T(8,128)(2,1)} %bitcast.56, ...), custom_call_target="tpu_custom_call" | custom-call | flops 4026531840 | bytes 25165824 | tf_op jit(solution)/shard_map/pallas_call | solution.py:785
  381.9 9.3 %convolution_convert_fusion.1 = bf16[1536,1536]{1,0:T(8,128)(2,1)} fusion(bf16[2,1024,1536]{2,1,0:T(8,128)(2,1)} %get-tuple-element.60.refs_8_, bf16[1024,1536]{1,0:T(8,128)(2,1)S(1)} %copy-done.3, f32[1536]{0:T(1024)S(1)} %reshape.183, f32[1024]{0:T(1024)S(1)} %add_rsqrt_fusion.1), kind=kOutput, calls=%fused_computation.4 | convolution fusion | flops 4840488960 | bytes 11020288 | tf_op jit(solution)/shard_map/dot_general | solution.py:436
  391.3 7.3 %convolution_convert_fusion.2 = bf16[1536,1536]{1,0:T(8,128)(2,1)} fusion(bf16[2,1024,1536]{2,1,0:T(8,128)(2,1)S(1)} %copy-done.18, bf16[1024,1536]{1,0:T(8,128)(2,1)S(1)} %copy-done.3, f32[1536]{0:T(1024)S(1)} %reshape.183, f32[1024]{0:T(1024)S(1)} %add_rsqrt_fusion.1), kind=kOutput, calls=%fused_computation.5 | convolution fusion | flops 4840488960 | bytes 11022336 | tf_op jit(solution)/shard_map/dot_general | solution.py:436
  401.8 13.1 %shard_map.191 = (bf16[1024,384]{1,0:T(8,128)(2,1)}, f32[8,256]{1,0:T(8,128)}, f32[2,48]{1,0:T(2,128)}) custom-call(bf16[1024,384]{1,0:T(8,128)(2,1)} %slice.186.bcdt_ref, f32[1024,256]{1,0:T(8,128)} %get-tuple-element.61.pre_ref, f32[8,256]{1,0:T(8,128)} %concatenate.54.taps_ref, f32[8,128]{1,0:T(8,128)} %pad.18.heads_ref, ...), custom_call_target="tpu_custom_call" | custom-call | tf_op jit(solution)/shard_map/pallas_call | solution.py:866
  419.0 4.1 convolution_convert_fusion.8
  423.1 71.3 %shard_map.192 = (f32[48,3456]{1,0:T(8,128)}, bf16[1024,1536]{1,0:T(8,128)(2,1)}, bf16[1024,1536]{1,0:T(8,128)(2,1)}, f32[1,1536]{1,0:T(1,128)}) custom-call(bf16[32,48,1536]{2,1,0:T(8,128)(2,1)} %bitcast.82, bf16[32,48,1536]{2,1,0:T(8,128)(2,1)} %bitcast.81, bf16[32,48,384]{2,1,0:T(8,128)(2,1)} %bitcast.83, ...), custom_call_target="tpu_custom_call" | custom-call | flops 28991029248 | bytes 37748736 | tf_op jit(solution)/shard_map/pallas_call | solution.py:960
  497.0 14.6 %shard_map.193 = f32[8,128]{1,0:T(8,128)} custom-call(f32[32,8,128]{2,1,0:T(8,128)} %bitcast.57), custom_call_target="tpu_custom_call" | custom-call | tf_op jit(solution)/shard_map/pallas_call | solution.py:425
  514.9 1.4 slice.164
  516.3 1.3 slice.165
  522.0 3.8 copy.97
  525.8 1.7 copy.98
  (124 shorter events, 39.7 us)
Async XLA Ops:
  7.2 135.7 %all-gather.3.cloned.1.call-start = ((), (), s32[]{:S(2)}) async-start(), calls=%async_computation | async-start | bytes 9732096 | tf_op jit(solution)/shard_map/all_gather | solution.py:978
  9.1 214.1 %all-gather.5.cloned.1.call-start = ((), (), s32[]{:S(2)}) async-start(), calls=%async_computation.1 | async-start | bytes 9732096 | tf_op jit(solution)/shard_map/all_gather | solution.py:979
  17.1 83.1 %copy-start.2 = (bf16[1024,1536]{1,0:T(8,128)(2,1)S(1)}, bf16[1024,1536]{1,0:T(8,128)(2,1)}, u32[]{:S(2)}) copy-start(bf16[1024,1536]{1,0:T(8,128)(2,1)} %refs_10_.1) | copy-start | bytes 9437188
  99.6 291.7 %copy-start.12 = (f32[1536]{0:T(1024)}, f32[1536]{0:T(1024)S(1)}, u32[]{:S(2)}) copy-start(f32[1536]{0:T(1024)S(1)} %reshape.183) | copy-start | bytes 18436
  100.9 18.3 %copy-start.6 = (s32[1024]{0:T(1024)S(1)}, s32[1024]{0:T(1024)}, u32[]{:S(2)}) copy-start(s32[1024]{0:T(1024)} %param.13) | copy-start | bytes 12292
  100.9 19.4 %copy-start.16 = (s32[8]{0:T(128)S(1)}, s32[8]{0:T(128)}, u32[]{:S(2)}) copy-start(s32[8]{0:T(128)} %slice.154) | copy-start | bytes 100
  100.9 21.2 %copy-start.15 = (f32[3,48]{1,0:T(4,128)S(1)}, f32[3,48]{1,0:T(4,128)}, u32[]{:S(2)}) copy-start(f32[3,48]{1,0:T(4,128)} %param.21) | copy-start | bytes 1732
  115.4 2.9 copy-start
  120.3 4.5 copy-start.1
  206.6 16.6 %copy-start.19 = (bf16[1024,1536]{1,0:T(8,128)(2,1)S(1)}, bf16[1024,1536]{1,0:T(8,128)(2,1)}, u32[]{:S(2)}) copy-start(bf16[1024,1536]{1,0:T(8,128)(2,1)} %refs_11_.1) | copy-start | bytes 9437188
  240.4 61.2 %copy-start.3 = (bf16[1024,1536]{1,0:T(8,128)(2,1)S(1)}, bf16[1024,1536]{1,0:T(8,128)(2,1)}, u32[]{:S(2)}) copy-start(bf16[1024,1536]{1,0:T(8,128)(2,1)} %refs_10_.1) | copy-start | bytes 9437188
  301.5 9.2 %copy-start.17 = (bf16[2,1024,1536]{2,1,0:T(8,128)(2,1)S(1)}, bf16[2,1024,1536]{2,1,0:T(8,128)(2,1)}, u32[]{:S(2)}) copy-start(bf16[2,1024,1536]{2,1,0:T(8,128)(2,1)} %get-tuple-element.59.refs_7_) | copy-start | bytes 18874372
  381.9 9.4 %copy-start.18 = (bf16[2,1024,1536]{2,1,0:T(8,128)(2,1)S(1)}, bf16[2,1024,1536]{2,1,0:T(8,128)(2,1)}, u32[]{:S(2)}) copy-start(bf16[2,1024,1536]{2,1,0:T(8,128)(2,1)} %get-tuple-element.60.refs_8_) | copy-start | bytes 18874372
  391.2 8.4 %copy-start.7 = (f32[8,1536]{1,0:T(8,128)S(1)}, f32[8,1536]{1,0:T(8,128)}, u32[]{:S(2)}) copy-start(f32[8,1536]{1,0:T(8,128)} %get-tuple-element.79) | copy-start | bytes 147460
  391.2 8.4 %copy-start.8 = (f32[8,1536]{1,0:T(8,128)S(1)}, f32[8,1536]{1,0:T(8,128)}, u32[]{:S(2)}) copy-start(f32[8,1536]{1,0:T(8,128)} %get-tuple-element.80) | copy-start | bytes 147460
  391.2 9.8 %copy-start.9 = (f32[8,1536]{1,0:T(8,128)S(1)}, f32[8,1536]{1,0:T(8,128)}, u32[]{:S(2)}) copy-start(f32[8,1536]{1,0:T(8,128)} %get-tuple-element.70) | copy-start | bytes 147460
  391.2 9.8 %copy-start.10 = (f32[8,1536]{1,0:T(8,128)S(1)}, f32[8,1536]{1,0:T(8,128)}, u32[]{:S(2)}) copy-start(f32[8,1536]{1,0:T(8,128)} %get-tuple-element.71) | copy-start | bytes 147460
  401.8 13.1 %copy-start.14 = (f32[48]{0:T(128)S(1)}, f32[48]{0:T(128)}, u32[]{:S(2)}) copy-start(f32[48]{0:T(128)} %reduce_sum.54) | copy-start | bytes 580
  401.8 15.4 %copy-start.11 = (f32[1,3072]{1,0:T(1,128)S(1)}, f32[1,3072]{1,0:T(1,128)}, u32[]{:S(2)}) copy-start(f32[1,3072]{1,0:T(1,128)} %get-tuple-element.96) | copy-start | bytes 36868
  401.8 17.1 %copy-start.13 = (f32[1536]{0:T(1024)S(1)}, f32[1536]{0:T(1024)}, u32[]{:S(2)}) copy-start(f32[1536]{0:T(1024)} %copy-done.12) | copy-start | bytes 18436
  494.3 31.5 %copy-start.4 = (bf16[1024,1536]{1,0:T(8,128)(2,1)S(1)}, bf16[1024,1536]{1,0:T(8,128)(2,1)}, u32[]{:S(2)}) copy-start(bf16[1024,1536]{1,0:T(8,128)(2,1)} %get-tuple-element.120) | copy-start | bytes 9437188
  522.0 5.5 %copy-start.5 = (f32[96,1536]{1,0:T(8,128)S(1)}, f32[96,1536]{1,0:T(8,128)}, u32[]{:S(2)}) copy-start(f32[96,1536]{1,0:T(8,128)} %get-tuple-element.124) | copy-start | bytes 1769476
Sparse Core Ops, SparseCore 0:
  10.9 97.8 all-gather.2
  111.7 82.6 all-gather.4

commit v5 on v4

--- a/solution.py
+++ b/solution.py
@@ -8,11 +8,12 @@
 
 EPS = 1e-05
 L = 128
-HG = 4
+HG = 8
 LOG2E = 1.4426950408889634
-BWD_TICKS = 44
-TAIL_TICKS = 44
-TAIL_PLAN = (8, 14, 4, 28, 4)
+BWD_PLAN = (2, 5, 2, 14, 2)
+BWD_TICKS = 23
+TAIL_PLAN = (6, 12, 4, 28, 4)
+TAIL_TICKS = 47
 bf16, f32 = jnp.bfloat16, jnp.float32
 HIGHEST = lax.Precision.HIGHEST
 
@@ -243,14 +244,12 @@
 
         order = list(range(zn - 1, -1, -1))
 
-        def begin():
-            at.barrier()
-            for col in (3, 1, 2, 0):
-                for dist in order:
-                    def one(zs):
-                        for cp in core(zs, col) + load(zs, col):
-                            cp.start()
-                    each(dist, one)
+        def start(col):
+            for dist in order:
+                def one(zs):
+                    for cp in core(zs, col) + load(zs, col):
+                        cp.start()
+                each(dist, one)
 
         def ready(zs, col):
             for cp in load(zs, col):
@@ -258,35 +257,29 @@
             for cp in core(zs, col):
                 cp.wait_recv()
 
-        def wide(*terms):
-            total = terms[0].astype(f32)
-            for t in terms[1:]:
-                total = total + t.astype(f32)
-            return total
-
         def diag(zs):
             ready(zs, 3)
-            acc[zs, 3] = wide(acc[zs, 3], c_in[zs, 3]).astype(bf16)
+            acc[zs, 3] = acc[zs, 3] + c_in[zs, 3]
             diag_x(zs).start()
             diag_y(zs).start()
 
         def sides(zs):
             ready(zs, 1)
             diag_y(zs).wait_recv()
-            acc[zs, 1, :, lo] = wide(acc[zs, 1, :, lo], c_in[zs, 1, :, lo]).astype(bf16)
-            acc[zs, 1, :, hi] = wide(acc[zs, 1, :, hi], c_in[zs, 1, :, hi], d_in[zs, :, hi]).astype(bf16)
+            acc[zs, 1, :, lo] = acc[zs, 1, :, lo] + c_in[zs, 1, :, lo]
+            acc[zs, 1, :, hi] = acc[zs, 1, :, hi] + c_in[zs, 1, :, hi] + d_in[zs, :, hi]
             to_x(zs).start()
             ready(zs, 2)
             diag_x(zs).wait_recv()
-            acc[zs, 2, :, lo] = wide(acc[zs, 2, :, lo], c_in[zs, 2, :, lo], d_in[zs, :, lo]).astype(bf16)
-            acc[zs, 2, :, hi] = wide(acc[zs, 2, :, hi], c_in[zs, 2, :, hi]).astype(bf16)
+            acc[zs, 2, :, lo] = acc[zs, 2, :, lo] + c_in[zs, 2, :, lo] + d_in[zs, :, lo]
+            acc[zs, 2, :, hi] = acc[zs, 2, :, hi] + c_in[zs, 2, :, hi]
             to_y(zs).start()
 
         def column(zs):
             ready(zs, 0)
             to_x(zs).wait_recv()
             to_y(zs).wait_recv()
-            return wide(acc[zs, 0], c_in[zs, 0]) + wide(xy_in[0, zs], xy_in[1, zs])
+            return (acc[zs, 0] + c_in[zs, 0]).astype(f32) + (xy_in[0, zs] + xy_in[1, zs]).astype(f32)
 
         def pass_on(zs):
             total = column(zs)
@@ -342,18 +335,10 @@
                 if dist:
                     each(dist, lambda zs: up(zs).wait_send())
 
-        self.begin, self.finish = begin, finish
+        self.start, self.finish, self.barrier = start, finish, at.barrier
         self.diag = [functools.partial(each, dist, diag) for dist in order]
         self.sides = [functools.partial(each, dist, sides) for dist in order]
         self.pass_on = [functools.partial(each, dist, pass_on) for dist in order[:-1]]
-
-    def plan(self, diag, sides, side_gap, pass_on, pass_gap):
-        ticks = {0: [self.begin], diag: list(self.diag)}
-        for k, fn in enumerate(self.sides):
-            ticks.setdefault(sides + k * side_gap, []).append(fn)
-        for k, fn in enumerate(self.pass_on):
-            ticks.setdefault(pass_on + k * pass_gap, []).append(fn)
-        return ticks
 
     @staticmethod
     def scratch(nd, rows, cols, parts):
@@ -361,6 +346,35 @@
         D, V = pltpu.SemaphoreType.DMA, pltpu.VMEM
         return [V((zn, 4, rows, cols), bf16), V((zn, 4, rows, cols), bf16), V((zn, rows, cols), bf16), V((2, zn, rows, cols), bf16),
                 V((zn + 1, rows, cols), bf16), D((zn, 4, parts)), D((zn, 4, parts)), D((zn, 4, parts))] + [D((zn,))] * 9 + [D((2, zn))]
+
+
+def plan(pipes, barrier, diag, sides, side_gap, pass_on, pass_gap):
+    ticks = {0: [barrier] + [functools.partial(p.start, col) for col in (3, 1, 2, 0) for p in pipes]}
+    for m, p in enumerate(pipes):
+        ticks.setdefault(diag + m, []).extend(p.diag)
+        for k, fn in enumerate(p.sides):
+            ticks.setdefault(sides + k * side_gap + m * (side_gap // 2), []).append(fn)
+        for k, fn in enumerate(p.pass_on):
+            ticks.setdefault(pass_on + k * pass_gap + m * (pass_gap // 2), []).append(fn)
+    return ticks
+
+
+def columns(refs, split):
+    return [[refs[a].at[:, :, pl.ds(o, w)] for a, o, w in pipe] for pipe in split]
+
+
+def pipes_of(nd, nf, g_refs, out_ref, split, scratch):
+    pipes, off = [], 0
+    per = len(scratch) // len(split)
+    for m, (views, pipe) in enumerate(zip(columns(g_refs, split), split)):
+        width = sum(w for _, _, w in pipe)
+        pipes.append(Scatter(nd, nf, views, out_ref.at[:, pl.ds(off, width)], *scratch[per * m : per * (m + 1)]))
+        off += width
+    return pipes
+
+
+def pipes_scratch(nd, rows, split):
+    return [x for pipe in split for x in Scatter.scratch(nd, rows, sum(w for _, _, w in pipe), len(pipe))]
 
 
 def run_ticks(ticks, now, last):
@@ -379,57 +393,52 @@
                 fn()
 
 
-def exchange_kernel(nd, nf, g_ref, out_ref, got, send, recv):
-    n = nd * nf
-    me = lax.axis_index("dp") * nf + lax.axis_index("fsdp")
-    sem = pltpu.get_barrier_semaphore()
-
-    def peer(k):
-        return lax.rem(me + k, n)
-
-    def greet(k, carry):
-        pl.semaphore_signal(sem, inc=1, device_id=(peer(k) // nf, peer(k) % nf), device_id_type=MESH)
-        return carry
-
-    lax.fori_loop(1, n, greet, 0)
-    pl.semaphore_wait(sem, n - 1)
-
-    def copy(k):
-        p = peer(k)
-        return pltpu.make_async_remote_copy(src_ref=g_ref.at[p], dst_ref=got.at[k], send_sem=send.at[k], recv_sem=recv.at[k],
-                                            device_id=(p // nf, p % nf), device_id_type=MESH)
-
-    def begin(k, carry):
-        copy(k).start()
-        return carry
-
-    lax.fori_loop(1, n, begin, 0)
-
-    def add(k, total):
-        copy(k).wait_recv()
-        return total + got[k]
-
-    out_ref[...] = lax.fori_loop(1, n, add, g_ref[me])
-
-    def end(k, carry):
-        copy(k).wait_send()
-        return carry
-
-    lax.fori_loop(1, n, end, 0)
-
-
-def exchange(g, nd, nf, cid):
-    n = nd * nf
-    D = pltpu.SemaphoreType.DMA
-    vm = pl.BlockSpec(memory_space=pltpu.VMEM)
-    return pl.pallas_call(
-        functools.partial(exchange_kernel, nd, nf),
-        out_shape=jax.ShapeDtypeStruct(g.shape[1:], g.dtype),
-        in_specs=[vm],
-        out_specs=vm,
-        scratch_shapes=[pltpu.VMEM(g.shape, g.dtype), D((n,)), D((n,))],
-        compiler_params=pltpu.CompilerParams(collective_id=cid, has_side_effects=True),
-    )(g)
+class Spread:
+    def __init__(self, nd, nf, src, got, send, recv):
+        self.n, self.nf = nd * nf, nf
+        self.me = lax.axis_index("dp") * nf + lax.axis_index("fsdp")
+        self.src, self.got, self.send, self.recv = src, got, send, recv
+
+    def peer(self, k):
+        return lax.rem(self.me + k, self.n)
+
+    def loop(self, fn):
+        def body(k, carry):
+            fn(k)
+            return carry
+        lax.fori_loop(1, self.n, body, 0)
+
+    def barrier(self):
+        sem = pltpu.get_barrier_semaphore()
+
+        def greet(k):
+            pl.semaphore_signal(sem, inc=1, device_id=(self.peer(k) // self.nf, self.peer(k) % self.nf), device_id_type=MESH)
+        self.loop(greet)
+        pl.semaphore_wait(sem, self.n - 1)
+
+    def copy(self, k):
+        p = self.peer(k)
+        src = self.src.at[p] if len(self.src.shape) == 3 else self.src
+        return pltpu.make_async_remote_copy(src_ref=src, dst_ref=self.got.at[k], send_sem=self.send.at[k], recv_sem=self.recv.at[k],
+                                            device_id=(p // self.nf, p % self.nf), device_id_type=MESH)
+
+    def begin(self):
+        self.loop(lambda k: self.copy(k).start())
+
+    def total(self):
+        own = self.src[self.me] if len(self.src.shape) == 3 else self.src[...]
+
+        def add(k, total):
+            self.copy(k).wait_recv()
+            return total + self.got[k]
+        total = lax.fori_loop(1, self.n, add, own)
+        self.loop(lambda k: self.copy(k).wait_send())
+        return total
+
+    @staticmethod
+    def scratch(n, tile):
+        D = pltpu.SemaphoreType.DMA
+        return [pltpu.VMEM((n,) + tile, f32), D((n,)), D((n,))]
 
 
 def dot(a, b, dims=((1,), (0,)), precision=None):
@@ -437,7 +446,7 @@
 
 
 def sigmoid(x):
-    return 1.0 / (1.0 + jnp.exp(-x))
+    return 0.5 * jnp.tanh(0.5 * x) + 0.5
 
 
 def conv_rows(ext, taps, masks, halo):
@@ -452,12 +461,12 @@
 
 
 def prep_kernel(bcdt_ref, taps_ref, heads_ref, m_ref, segc_ref, segr_ref,
-                b_ref, c_ref, bt_ref, ct_ref, pre_ref, gm_ref, cum4_ref, cumr_ref, sc_ref, dt_ref):
+                b_ref, c_ref, bt_ref, ct_ref, pre_ref, gm_ref, cum_ref, cumr_ref, sc_ref, dt_ref):
     T = bcdt_ref.shape[0]
     nc = T // L
     N = b_ref.shape[1]
     H = dt_ref.shape[1]
-    groups = cum4_ref.shape[0]
+    groups = cumr_ref.shape[0]
     taps = taps_ref[...]
     tri = (lax.broadcasted_iota(jnp.int32, (L, L), 0) >= lax.broadcasted_iota(jnp.int32, (L, L), 1))
     trif = tri.astype(f32)
@@ -495,15 +504,14 @@
         ein = jnp.where(segc == prev, jnp.exp2(cum), 0.0)
         lv = jnp.where(segc == last, jnp.exp2(end - cum), 0.0)
         dt_ref[here, :] = dt
-        cumt = cum.T
+        wide = jnp.concatenate([cum, jnp.zeros((L, 128 - H), f32)], axis=1)
+        cum_ref[here, :] = wide
+        cumt = wide.T
+        for k in range(groups):
+            cumr_ref[k, :, here] = cumt[HG * k : HG * (k + 1)]
         s0 = pl.multiple_of(c * (3 * L), L)
-        for k in range(groups):
-            cols = slice(HG * k, HG * (k + 1))
-            cum4_ref[k, here, :] = cum[:, cols]
-            cumr_ref[k, :, here] = cumt[cols]
-            sc_ref[k, pl.ds(s0, L), :] = dt[:, cols].astype(bf16)
-            sc_ref[k, pl.ds(s0 + L, L), :] = ein[:, cols].astype(bf16)
-            sc_ref[k, pl.ds(s0 + 2 * L, L), :] = lv[:, cols].astype(bf16)
+        for k, part in enumerate((dt, ein, lv)):
+            sc_ref[pl.ds(s0 + k * L, L), :] = jnp.concatenate([part, jnp.zeros((L, 128 - H), f32)], axis=1).astype(bf16)
         return carry
 
     lax.fori_loop(0, nc, chunk, 0)
@@ -514,16 +522,23 @@
     nc = T // L
     G = H // HG
     S = jax.ShapeDtypeStruct
+    full = lambda a: pl.BlockSpec(a.shape, lambda i: (0,) * a.ndim)
+    outs = (S((T, N), bf16), S((T, N), bf16), S((N, T), bf16), S((N, T), bf16), S((T, 2 * N), f32),
+            S((nc, L, L), f32), S((T, 128), f32), S((G, HG, T), f32), S((3 * T, 128), bf16), S((T, H), f32))
+    wide = 2 * N + 128
     return pl.pallas_call(
         prep_kernel,
-        out_shape=(S((T, N), bf16), S((T, N), bf16), S((N, T), bf16), S((N, T), bf16), S((T, 2 * N), f32),
-                   S((nc, L, L), f32), S((G, T, HG), f32), S((G, HG, T), f32), S((G, 3 * T, HG), bf16), S((T, H), f32)),
+        grid=(1,),
+        in_specs=[pl.BlockSpec((T, wide), lambda i: (0, bcdt.shape[1] // wide - 1))] + [full(a) for a in (taps, heads, masks, segc, segr)],
+        out_specs=[full(o) for o in outs],
+        out_shape=outs,
         compiler_params=pltpu.CompilerParams(vmem_limit_bytes=60 << 20),
     )(bcdt, taps, heads, masks, segc, segr)
 
 
-def lane_onehot(width, per):
-    return (lax.broadcasted_iota(jnp.int32, (HG, width), 1) // per == lax.broadcasted_iota(jnp.int32, (HG, width), 0)).astype(bf16)
+def lane_onehot(group, width, per):
+    shape = (128, width)
+    return (group * HG + lax.broadcasted_iota(jnp.int32, shape, 1) // per == lax.broadcasted_iota(jnp.int32, shape, 0)).astype(bf16)
 
 
 def half_masks(P):
@@ -536,7 +551,7 @@
     return jnp.exp2(jnp.minimum(cum4[:, k : k + 1] - cumr[k : k + 1, :], 0.0))
 
 
-def fwd_kernel(u_ref, gate_ref, taps_ref, m_ref, b_ref, c_ref, bt_ref, gm_ref, cum4_ref, cumr_ref, sc_ref,
+def fwd_kernel(u_ref, gate_ref, taps_ref, m_ref, b_ref, c_ref, bt_ref, gm_ref, cum_ref, cumr_ref, sc_ref,
                gg_ref, ssq_ref, pre_ref, st_ref, state):
     T, W = u_ref.shape
     P = W // HG
@@ -545,7 +560,7 @@
     taps = taps_ref[...]
     gain = taps[5:6]
     skip = taps[6:7]
-    onehot = lane_onehot(W, P)
+    onehot = lane_onehot(step, W, P)
     ma, mb = half_masks(P)
     state[...] = jnp.zeros_like(state)
 
@@ -562,12 +577,12 @@
         pre_ref[here, :] = pre.astype(bf16)
         x = pre * sigmoid(pre)
         s0 = pl.multiple_of(c * (3 * L), L)
-        exp = dot(sc_ref[0, pl.ds(s0, 3 * L), :], onehot)
+        exp = dot(sc_ref[pl.ds(s0, 3 * L), :], onehot)
         dtx, einx, lvx = exp[:L], exp[L : 2 * L], exp[2 * L :]
         xd = x * dtx
         xdb = xd.astype(bf16)
         gm = gm_ref[c]
-        cum4 = cum4_ref[0, here, :]
+        cum4 = pltpu.roll(cum_ref[here, :], 128 - step * HG, 1)
         cumr = cumr_ref[0, :, here]
         sb = state[...].astype(bf16)
         st_ref[c] = sb
@@ -592,10 +607,10 @@
     lax.fori_loop(0, nc, chunk, 0)
 
 
-def fwd(u, gate, taps, masks, b, c, bt, gm, cum4, cumr, sc):
+def fwd(u, gate, taps, masks, b, c, bt, gm, cum, cumr, sc):
     T, E = gate.shape
     N = b.shape[1]
-    G = cum4.shape[0]
+    G = cumr.shape[0]
     W = E // G
     nc = T // L
     S = jax.ShapeDtypeStruct
@@ -606,34 +621,30 @@
         fwd_kernel,
         grid=(G,),
         in_specs=[col(0), col(0), pl.BlockSpec((8, W), lambda g: (0, g)), full(masks), full(b), full(c), full(bt), full(gm),
-                  grp(cum4), grp(cumr), grp(sc)],
+                  full(cum), grp(cumr), full(sc)],
         out_specs=[col(0), pl.BlockSpec((T, 128), lambda g: (0, 0)), col(0), pl.BlockSpec((nc, N, W), lambda g: (0, 0, g))],
         out_shape=(S((T, E), bf16), S((T, 128), f32), S((T, E), bf16), S((nc, N, E), bf16)),
         scratch_shapes=[pltpu.VMEM((N, W), f32)],
         compiler_params=pltpu.CompilerParams(vmem_limit_bytes=60 << 20),
         cost_estimate=pl.CostEstimate(flops=T * E * (2 * L + 4 * N) * 2, bytes_accessed=T * E * 12, transcendentals=T * E * 4),
-    )(u, gate, taps, masks, b, c, bt, gm, cum4, cumr, sc)
-
-
-def bwd_kernel(*refs):
-    bwd_body(lambda now: None, *refs)
-
-
-def bwd_scatter_kernel(nd, nf, parts, *refs):
-    g_refs, ins, outs = refs[:parts], refs[parts : parts + 15], refs[parts + 15 : parts + 23]
-    own, comm = refs[parts + 23 : parts + 26], refs[parts + 26 :]
-    sc = Scatter(nd, nf, g_refs, outs[7], *comm)
-    nc = ins[0].shape[0] // L
-    ticks = sc.plan(7, 12, 3, 28, 6)
-    bwd_body(lambda now: run_ticks(ticks, now, BWD_TICKS), *ins, *outs[:7], *own)
+    )(u, gate, taps, masks, b, c, bt, gm, cum, cumr, sc)
+
+
+def bwd_scatter_kernel(nd, nf, g0, arrays, split, *refs):
+    g_refs, ins, outs = refs[:arrays], refs[arrays : arrays + 15], refs[arrays + 15 : arrays + 23]
+    own, comm = refs[arrays + 23 : arrays + 26], refs[arrays + 26 :]
+    pipes = pipes_of(nd, nf, g_refs, outs[7], split, comm)
+    ticks = plan(pipes, pipes[0].barrier, *BWD_PLAN)
+    bwd_body(lambda now: run_ticks(ticks, now, BWD_TICKS), g0, *ins, *outs[:7], *own)
 
     @pl.when(pl.program_id(0) == pl.num_programs(0) - 1)
     def _():
         run_rest(ticks, BWD_TICKS)
-        sc.finish()
-
-
-def bwd_body(tick, u_ref, gate_ref, pre_ref, dm_ref, rq_ref, taps_ref, m_ref, b_ref, c_ref, ct_ref, gm_ref, cum4_ref, cumr_ref, sc_ref, st_ref,
+        for p in pipes:
+            p.finish()
+
+
+def bwd_body(tick, g0, u_ref, gate_ref, pre_ref, dm_ref, rq_ref, taps_ref, m_ref, b_ref, c_ref, ct_ref, gm_ref, cum_ref, cumr_ref, sc_ref, st_ref,
                dz_ref, dg_ref, db_ref, dc_ref, rs_ref, small_ref, kk_ref, ds, nxt, acc):
     T, W = u_ref.shape
     P = W // HG
@@ -642,7 +653,7 @@
     taps = taps_ref[...]
     gain = taps[5:6]
     skip = taps[6:7]
-    onehot = lane_onehot(W, P)
+    onehot = lane_onehot(step + g0, W, P)
     ma, mb = half_masks(P)
     ds[...] = jnp.zeros_like(ds)
     nxt[...] = jnp.zeros_like(nxt)
@@ -653,11 +664,12 @@
         dg_ref[...] = jnp.zeros_like(dg_ref)
         db_ref[...] = jnp.zeros_like(db_ref)
         dc_ref[...] = jnp.zeros_like(dc_ref)
-
-    ri = lax.broadcasted_iota(jnp.int32, (4 * W, 16), 0)
-    ci = lax.broadcasted_iota(jnp.int32, (4 * W, 16), 1)
+        rs_ref[...] = jnp.zeros_like(rs_ref)
+
+    ri = lax.broadcasted_iota(jnp.int32, (4 * W, 128), 0)
+    ci = lax.broadcasted_iota(jnp.int32, (4 * W, 128), 1)
     part = ri // W
-    want = jnp.maximum(part - 1, 0) * HG + (ri % W) // P
+    want = (jnp.maximum(part - 1, 0) * pl.num_programs(0) + step) * HG + (ri % W) // P
     fold = (want == ci).astype(bf16)
 
     def eight(z):
@@ -674,12 +686,12 @@
         x = pre * sig
         dsilu = sig + x * (1.0 - sig)
         s0 = pl.multiple_of(c * (3 * L), L)
-        exp = dot(sc_ref[0, pl.ds(s0, 3 * L), :], onehot)
+        exp = dot(sc_ref[pl.ds(s0, 3 * L), :], onehot)
         dtx, einx, lvx = exp[:L], exp[L : 2 * L], exp[2 * L :]
         xdb = (x * dtx).astype(bf16)
         xd = xdb.astype(f32)
         gm = gm_ref[c]
-        cum4 = cum4_ref[0, here, :]
+        cum4 = pltpu.roll(cum_ref[here, :], 128 - (step + g0) * HG, 1)
         cumr = cumr_ref[0, :, here]
         sb = st_ref[c]
         es, ms, inner = [], [], []
@@ -729,7 +741,7 @@
         r1 = dy * yn - xd * dxi
         r1h = r1.astype(bf16)
         r1l = (r1 - r1h.astype(f32)).astype(bf16)
-        rs_ref[0, here, :] = dot(jnp.concatenate([r1h, r1l, (xd * dxe).astype(bf16), (x * dxd).astype(bf16)], axis=1), fold)
+        rs_ref[here, :] += dot(jnp.concatenate([r1h, r1l, (xd * dxe).astype(bf16), (x * dxd).astype(bf16)], axis=1), fold)
         dpre = (dxd * dtx + skip * dy) * dsilu
         ext = jnp.concatenate([dpre, nxt[...]], axis=0)
         nxt[...] = dpre[:8]
@@ -752,10 +764,10 @@
     small_ref[7:8, :] = jnp.zeros((1, W), f32)
 
 
-def bwd(half, halves, u, gate, pre, dm, rq, taps, masks, b, c, ct, gm, cum4, cumr, sc, st, comm=None):
+def bwd(half, halves, u, gate, pre, dm, rq, taps, masks, b, c, ct, gm, cum, cumr, sc, st, comm):
     T, E = gate.shape
     N = b.shape[1]
-    G = cum4.shape[0]
+    G = cumr.shape[0]
     W = E // G
     nc = T // L
     Gh = G // halves
@@ -767,31 +779,23 @@
     whole = lambda s: pl.BlockSpec(s, lambda g: (0,) * len(s))
     grp = lambda a: pl.BlockSpec((1,) + a.shape[1:], lambda g: (g + g0, 0, 0))
     in_specs = [col, col, col, col, full(rq), pl.BlockSpec((8, W), lambda g: (0, g + g0)), full(masks), full(b), full(c),
-                full(ct), full(gm), grp(cum4), grp(cumr), grp(sc), pl.BlockSpec((nc, N, W), lambda g: (0, 0, g + g0))]
+                full(ct), full(gm), full(cum), grp(cumr), full(sc), pl.BlockSpec((nc, N, W), lambda g: (0, 0, g + g0))]
     out_specs = [pl.BlockSpec((2, T, W), lambda g: (0, 0, g)), whole((nc, L, L)), whole((T, N)), whole((T, N)),
-                 pl.BlockSpec((1, T, 16), lambda g: (g, 0, 0)), pl.BlockSpec((8, W), lambda g: (0, g)), pl.BlockSpec((nc, W), lambda g: (0, g))]
-    out_shape = [S((2, T, Eh), bf16), S((nc, L, L), f32), S((T, N), f32), S((T, N), f32), S((Gh, T, 16), f32), S((8, Eh), f32), S((nc, Eh), f32)]
+                 whole((T, 128)), pl.BlockSpec((8, W), lambda g: (0, g)), pl.BlockSpec((nc, W), lambda g: (0, g))]
+    out_shape = [S((2, T, Eh), bf16), S((nc, L, L), f32), S((T, N), f32), S((T, N), f32), S((T, 128), f32), S((8, Eh), f32), S((nc, Eh), f32)]
     scratch = [pltpu.VMEM((N, W), f32), pltpu.VMEM((8, W), f32), pltpu.VMEM((56, W), f32)]
-    kernel, first, params = bwd_kernel, (), {}
-    if comm:
-        nd, nf, cid, first = comm
-        rows, cols = first[0].shape[1], sum(g.shape[2] for g in first)
-        kernel = functools.partial(bwd_scatter_kernel, nd, nf, len(first))
-        in_specs = [pl.BlockSpec(memory_space=pl.ANY)] * len(first) + in_specs
-        out_specs.append(whole((rows, cols)))
-        out_shape.append(S((rows, cols), f32))
-        scratch += Scatter.scratch(nd, rows, cols, len(first))
-        params = dict(collective_id=cid, has_side_effects=True)
+    nd, nf, cid, first, split = comm
+    rows, cols = first[0].shape[1], sum(w for pipe in split for _, _, w in pipe)
     return pl.pallas_call(
-        kernel,
+        functools.partial(bwd_scatter_kernel, nd, nf, g0, len(first), split),
         grid=(Gh,),
-        in_specs=in_specs,
-        out_specs=out_specs,
-        out_shape=out_shape,
-        scratch_shapes=scratch,
-        compiler_params=pltpu.CompilerParams(vmem_limit_bytes=60 << 20, **params),
+        in_specs=[pl.BlockSpec(memory_space=pl.ANY)] * len(first) + in_specs,
+        out_specs=out_specs + [whole((rows, cols))],
+        out_shape=out_shape + [S((rows, cols), f32)],
+        scratch_shapes=scratch + pipes_scratch(nd, rows, split),
+        compiler_params=pltpu.CompilerParams(vmem_limit_bytes=60 << 20, collective_id=cid, has_side_effects=True),
         cost_estimate=pl.CostEstimate(flops=T * Eh * (8 * L + 12 * N), bytes_accessed=T * Eh * 16, transcendentals=T * Eh * 4),
-    )(*first, u, gate, pre, dm, rq, taps, masks, b, c, ct, gm, cum4, cumr, sc, st)
+    )(*first, u, gate, pre, dm, rq, taps, masks, b, c, ct, gm, cum, cumr, sc, st)
 
 
 def post_kernel(bcdt_ref, pre_ref, taps_ref, heads_ref, m_ref, segc_ref, segr_ref, b_ref, c_ref, dg0_ref, db0_ref, dc0_ref, rs0_ref, dg1_ref, db1_ref, dc1_ref, rs1_ref, kk_ref, dt_ref,
@@ -800,7 +804,6 @@
     nc = T // L
     N = b_ref.shape[1]
     H = dt_ref.shape[1]
-    G = H // HG
     taps = taps_ref[...]
     tri = (lax.broadcasted_iota(jnp.int32, (L, L), 0) >= lax.broadcasted_iota(jnp.int32, (L, L), 1))
     upper = (lax.broadcasted_iota(jnp.int32, (L, L), 0) <= lax.broadcasted_iota(jnp.int32, (L, L), 1)).astype(f32)
@@ -838,9 +841,9 @@
             dv = dv + taps[3 - k : 4 - k] * sk
             acc[8 + 8 * k : 16 + 8 * k, :] += eight(sk * v)
         out_ref[here, : 2 * N] = dv.astype(bf16)
-        r1 = jnp.concatenate([r[k, here, 0:HG] for r in (rs0_ref, rs1_ref) for k in range(G // 2)], axis=1)
-        r2 = jnp.concatenate([r[k, here, HG : 2 * HG] for r in (rs0_ref, rs1_ref) for k in range(G // 2)], axis=1)
-        r3 = jnp.concatenate([r[k, here, 2 * HG : 3 * HG] for r in (rs0_ref, rs1_ref) for k in range(G // 2)], axis=1)
+        q = H // 2
+        r0, r1 = rs0_ref[here, :], rs1_ref[here, :]
+        r1, r2, r3 = (jnp.concatenate([r0[:, m * q : (m + 1) * q], r1[:, m * q : (m + 1) * q]], axis=1) for m in range(3))
         da = dot(upper, r1, precision=HIGHEST) + dot(strict, r2, precision=HIGHEST) + kk_ref[pl.ds(c, 1), :]
         dt = dt_ref[here, :]
         raw = bcdt_ref[here, 2 * N : 2 * N + 128].astype(f32)[:, :H] + bias
@@ -863,28 +866,40 @@
     N = b.shape[1]
     H = dt.shape[1]
     S = jax.ShapeDtypeStruct
+    wide = 2 * N + 128
+    full = lambda a: pl.BlockSpec(a.shape, lambda i: (0,) * a.ndim)
+    ins = (bcdt, pre, taps, heads, masks, segc, segr, b, c, *first, *second, kk, dt)
+    outs = (S((T, wide), bf16), S((8, 2 * N), f32), S((2, H), f32))
     return pl.pallas_call(
         post_kernel,
-        out_shape=(S(bcdt.shape, bf16), S((8, 2 * N), f32), S((2, H), f32)),
+        grid=(1,),
+        in_specs=[pl.BlockSpec((T, wide), lambda i: (0, bcdt.shape[1] // wide - 1))] + [full(a) for a in ins[1:]],
+        out_specs=[full(o) for o in outs],
+        out_shape=outs,
         scratch_shapes=[pltpu.VMEM((8, 2 * N), f32), pltpu.VMEM((40, 2 * N), f32), pltpu.VMEM((16, H), f32)],
         compiler_params=pltpu.CompilerParams(vmem_limit_bytes=60 << 20),
-    )(bcdt, pre, taps, heads, masks, segc, segr, b, c, *first, *second, kk, dt)
+    )(*ins)
 
 
 NT = 256
 
 
-def tail_kernel(nd, nf, parts, gg_tiles, *refs):
-    g_refs, refs = refs[:parts], refs[parts:]
-    wo_hbm, wg_hbm, wa_hbm, gg_ref, dz0_ref, dz1_ref, dbc_ref, hid_ref, go_ref, r_ref, gain_ref, sum_ref, out_ref, gin_ref, dn_ref = refs[:15]
-    wo, wg, wa, acc, dn, sem = refs[15:21]
-    sc = Scatter(nd, nf, g_refs, sum_ref, *refs[21:])
+def tail_kernel(nd, nf, arrays, split, tiles, *refs):
+    g_refs, refs = refs[:arrays], refs[arrays:]
+    (wo_hbm, wg_hbm, wa_hbm, gg_ref, dz0_ref, dz1_ref, dbc_ref, hid_ref, go_ref, r_ref, gain_ref, mine_ref,
+     sum_ref, out_ref, gin_ref, small_ref, dnorm_ref) = refs[:17]
+    wo, wg, wa, acc, dn, flat, sem = refs[17:24]
+    mine = Spread(nd, nf, mine_ref, *refs[24:27])
+    norm = Spread(nd, nf, flat, *refs[27:30])
+    pipes = pipes_of(nd, nf, g_refs, sum_ref, split, refs[30:])
     D, E = wg.shape
     Eh = E // 2
     step = pl.program_id(0)
-    tiles = gg_tiles
+    early = tiles // 2
     blocks = D // NT
-    ticks = sc.plan(*TAIL_PLAN)
+    ticks = plan(pipes, mine.barrier, *TAIL_PLAN)
+    ticks[0].append(mine.begin)
+    ticks.setdefault((early + tiles) * blocks + 2, []).append(norm.begin)
     fetch = [pltpu.make_async_copy(src, dst, sem.at[k]) for k, (src, dst) in enumerate(((wo_hbm, wo), (wg_hbm, wg), (wa_hbm, wa)))]
 
     @pl.when(step == 0)
@@ -895,26 +910,27 @@
         run_ticks(ticks, 0, 0)
         fetch[0].wait()
 
-    @pl.when(step == tiles)
+    @pl.when(step == early)
     def _():
         fetch[1].wait()
         fetch[2].wait()
 
-    @pl.when(step < tiles)
+    back = (step >= early) & (step < early + tiles)
+    in_back = lambda t: early * blocks <= t < (early + tiles) * blocks
+
+    @pl.when(jnp.logical_not(back))
     def _():
         def block(j, carry):
-            now = step * blocks + j
-            run_ticks({t: f for t, f in ticks.items() if 0 < t}, now, min(TAIL_TICKS, tiles * blocks - 1))
+            run_ticks({t: f for t, f in ticks.items() if t and not in_back(t)}, step * blocks + j, TAIL_TICKS)
             cols = pl.ds(pl.multiple_of(j * NT, NT), NT)
             out_ref[:, cols] = (hid_ref[:, cols].astype(f32) + r_ref[...] * dot(gg_ref[...], wo[:, cols])).astype(bf16)
             return carry
         lax.fori_loop(0, blocks, block, 0)
 
-    @pl.when(step >= tiles)
+    @pl.when(back)
     def _():
         def block(j, carry):
-            now = step * blocks + j
-            run_ticks({t: f for t, f in ticks.items() if t >= tiles * blocks}, now, TAIL_TICKS)
+            run_ticks({t: f for t, f in ticks.items() if in_back(t)}, step * blocks + j, TAIL_TICKS)
             cols = pl.ds(pl.multiple_of(j * NT, NT), NT)
             part = dot(dz0_ref[0], wg[cols, :Eh], ((1,), (1,))) + dot(dz1_ref[0], wg[cols, Eh:], ((1,), (1,)))
             part = part + dot(dz0_ref[1], wa[cols, :Eh], ((1,), (1,))) + dot(dz1_ref[1], wa[cols, Eh:E], ((1,), (1,)))
@@ -936,38 +952,53 @@
             return carry
         lax.fori_loop(0, hid_ref.shape[0] // 64, rows_of, 0)
 
+    @pl.when(step == early + tiles - 1)
+    def _():
+        flat[...] = jnp.zeros_like(flat)
+        for j in range(D // 128):
+            flat[j : j + 1, :] = jnp.sum(dn[:, 128 * j : 128 * (j + 1)], axis=0, keepdims=True)
+
     @pl.when(step == 2 * tiles - 1)
     def _():
-        dn_ref[...] = jnp.sum(dn[...], axis=0, keepdims=True)
         run_rest(ticks, TAIL_TICKS)
-        sc.finish()
-
-
-def tail(nd, nf, cid, gs, dz0, dz1, dbcdt, full_gate, full_a, gg, full_out, hidden, grad_out, r, norm_gain):
+        for p in pipes:
+            p.finish()
+        small_ref[...] = mine.total()
+        dnorm_ref[...] = norm.total()
+
+
+def tail(nd, nf, cid, gs, split, dz0, dz1, dbcdt, full_gate, full_a, gg, full_out, hidden, grad_out, r, norm_gain, mine):
     T, D = hidden.shape
     E = full_out.shape[0]
-    rows, cols = gs[0].shape[1], sum(g.shape[2] for g in gs)
+    n = nd * nf
+    rows, cols = gs[0].shape[1], sum(w for pipe in split for _, _, w in pipe)
     MT = 256 if rows % 16 == 0 else 128
     tiles = T // MT
+    early = tiles // 2
     wide = dbcdt.shape[1]
     S = jax.ShapeDtypeStruct
     any_ = pl.BlockSpec(memory_space=pl.ANY)
     whole = lambda s: pl.BlockSpec(s, lambda k: (0,) * len(s), pipeline_mode=pl.Buffered(1))
-    early = lambda w: pl.BlockSpec((MT, w), lambda k: (jnp.minimum(k, tiles - 1), 0))
-    late = lambda w: pl.BlockSpec((MT, w), lambda k: (jnp.maximum(k - tiles, 0), 0))
-    both = lambda w: pl.BlockSpec((MT, w), lambda k: (lax.rem(k, tiles), 0))
-    half = pl.BlockSpec((2, MT, E // 2), lambda k: (0, jnp.maximum(k - tiles, 0), 0))
+    at_out = lambda k: jnp.minimum(k, early - 1) + jnp.clip(k - tiles - early + 1, 0, tiles - early)
+    at_back = lambda k: jnp.clip(k - early, 0, tiles - 1)
+    at_row = lambda k: k - early * jnp.clip(k - early + 1, 0, 1) - (tiles - early) * jnp.clip(k - early - tiles + 1, 0, 1)
+    out_tile = lambda w: pl.BlockSpec((MT, w), lambda k: (at_out(k), 0))
+    back_tile = lambda w: pl.BlockSpec((MT, w), lambda k: (at_back(k), 0))
+    half = pl.BlockSpec((2, MT, E // 2), lambda k: (0, at_back(k), 0))
+    tile, ntile = mine.shape[1:], (-(-D // 1024) * 8, 128)
     return pl.pallas_call(
-        functools.partial(tail_kernel, nd, nf, len(gs), tiles),
+        functools.partial(tail_kernel, nd, nf, len(gs), split, tiles),
         grid=(2 * tiles,),
-        in_specs=[any_] * (len(gs) + 3) + [early(E), half, half, late(wide), both(D), late(D), early(1), whole((1, D))],
-        out_specs=[whole((rows, cols)), early(D), late(D), whole((1, D))],
-        out_shape=(S((rows, cols), f32), S((T, D), bf16), S((T, D), bf16), S((1, D), f32)),
+        in_specs=[any_] * (len(gs) + 3) + [out_tile(E), half, half, back_tile(wide), pl.BlockSpec((MT, D), lambda k: (at_row(k), 0)), back_tile(D),
+                                           out_tile(1), whole((1, D)), whole(mine.shape)],
+        out_specs=[whole((rows, cols)), out_tile(D), back_tile(D), whole(tile), whole(ntile)],
+        out_shape=(S((rows, cols), f32), S((T, D), bf16), S((T, D), bf16), S(tile, f32), S(ntile, f32)),
         scratch_shapes=[pltpu.VMEM((E, D), bf16), pltpu.VMEM((D, E), bf16), pltpu.VMEM((D, E + wide), bf16), pltpu.VMEM((MT, D), f32),
-                        pltpu.VMEM((8, D), f32), pltpu.SemaphoreType.DMA((3,))] + Scatter.scratch(nd, rows, cols, len(gs)),
+                        pltpu.VMEM((8, D), f32), pltpu.VMEM(ntile, f32), pltpu.SemaphoreType.DMA((3,))]
+        + Spread.scratch(n, tile) + Spread.scratch(n, ntile) + pipes_scratch(nd, rows, split),
         compiler_params=pltpu.CompilerParams(collective_id=cid, has_side_effects=True, vmem_limit_bytes=67043328),
         cost_estimate=pl.CostEstimate(flops=2 * T * D * 3 * E, bytes_accessed=8 * D * E, transcendentals=0),
-    )(*gs, full_out, full_gate, full_a, gg, dz0, dz1, dbcdt, hidden, grad_out, r, norm_gain)
+    )(*gs, full_out, full_gate, full_a, gg, dz0, dz1, dbcdt, hidden, grad_out, r, norm_gain, mine)
 
 
 def layer(nd, nf, hidden, grad_out, seg, shard_a, shard_gate, shard_out, head_params, sizes):
@@ -991,7 +1022,6 @@
     normed = (xhat * norm_gain).astype(bf16)
     ubc = dot(normed, full_a).astype(bf16)
     gate = dot(normed, full_gate).astype(bf16)
-    bcdt = ubc[:, E:]
     pos = jnp.arange(T, dtype=jnp.int32)
     masks = jnp.stack([jnp.ones((T,), f32)] + [((jnp.roll(seg, k) == seg) & (pos >= k)).astype(f32) for k in range(1, 4)], axis=1)
     lastid = seg[L - 1 :: L]
@@ -1001,8 +1031,8 @@
     taps_u = jnp.concatenate([conv[:, :E], gate_gain[None], jnp.repeat(head_params[2], E // H)[None], jnp.zeros((1, E), f32)], axis=0)
     taps_bc = jnp.concatenate([conv[:, E:], jnp.zeros((3, 2 * N), f32)], axis=0)
     heads_p = jnp.pad(head_params, ((0, 5), (0, 128 - H)))
-    b, c, bt, ct, pre_bc, gm, cum4, cumr, sc, dt = prep(bcdt, taps_bc, heads_p, masks, segc, segr, N, H)
-    gg, ssq, pre, st = fwd(ubc, gate, taps_u, masks, b, c, bt, gm, cum4, cumr, sc)
+    b, c, bt, ct, pre_bc, gm, cum, cumr, sc, dt = prep(ubc, taps_bc, heads_p, masks, segc, segr, N, H)
+    gg, ssq, pre, st = fwd(ubc, gate, taps_u, masks, b, c, bt, gm, cum, cumr, sc)
     r = lax.rsqrt(jnp.sum(ssq, axis=1, keepdims=True) / E + EPS)
     gos = (grad_out.astype(f32) * r).astype(bf16)
     g_out = dot(gg, gos, ((0,), (0,))).astype(bf16)
@@ -1012,27 +1042,30 @@
     masks8 = jnp.pad(masks, ((0, 8), (0, 0)))
     shape = lambda g: g.reshape(n, D // n, -1)
     grad = lambda dz: shape(dot(normed, dz, ((0,), (0,))).astype(bf16))
-    back = functools.partial(bwd, u=ubc, gate=gate, pre=pre, dm=dm, rq=rq, taps=taps_u, masks=masks8, b=b, c=c, ct=ct, gm=gm, cum4=cum4,
+    back = functools.partial(bwd, u=ubc, gate=gate, pre=pre, dm=dm, rq=rq, taps=taps_u, masks=masks8, b=b, c=c, ct=ct, gm=gm, cum=cum,
                              cumr=cumr, sc=sc, st=st)
-    dz0, dg0, db0, dc0, rs0, small0, kk0, s_out = back(0, 2, comm=(nd, nf, 4, (g_out.reshape(n, E // n, D),)))
-    dz1, dg1, db1, dc1, rs1, small1, kk1, sum0 = back(1, 2, comm=(nd, nf, 3, (grad(dz0[0]), grad(dz0[1]))))
+    dz0, dg0, db0, dc0, rs0, small0, kk0, s_out = back(0, 2, comm=(nd, nf, 4, (g_out.reshape(n, E // n, D),), (((0, 0, D // 2),), ((0, D // 2, D // 2),))))
+    dz1, dg1, db1, dc1, rs1, small1, kk1, sum0 = back(1, 2, comm=(nd, nf, 3, (grad(dz0[0]), grad(dz0[1])), (((0, 0, E // 2),), ((1, 0, E // 2),))))
     small = jnp.concatenate([small0, small1], axis=1)
     kk = jnp.concatenate([kk0, kk1], axis=1)
     kkh = jnp.sum(kk.reshape(kk.shape[0], H, E // H), axis=2)
-    dbcdt, small_bc, hs = post(bcdt, pre_bc, taps_bc, heads_p, masks8, segc, segr, b, c, (dg0, db0, dc0, rs0), (dg1, db1, dc1, rs1), kkh, dt)
-    sum1, output, grad_in, d_norm = tail(nd, nf, 1, (grad(dz1[0]), grad(dz1[1]), grad(dbcdt)), dz0, dz1, dbcdt, full_gate, full_a, gg, full_out,
-                                         hidden, grad_out, r, norm_gain[None])
+    dbcdt, small_bc, hs = post(ubc, pre_bc, taps_bc, heads_p, masks8, segc, segr, b, c, (dg0, db0, dc0, rs0), (dg1, db1, dc1, rs1), kkh, dt)
     d_conv = jnp.concatenate([jnp.stack([small[6], small[5], small[4], small[3], small[2]]),
                               jnp.stack([small_bc[4], small_bc[3], small_bc[2], small_bc[1], small_bc[0]])], axis=1)
     d_heads = jnp.concatenate([hs, jnp.sum(small[1].reshape(1, H, E // H), axis=2)], axis=0)
-    mine = jnp.concatenate([d_conv.reshape(K1, n, ncol).transpose(1, 0, 2).reshape(n, -1), d_norm.reshape(n, -1), small[0].reshape(n, -1),
+    mine = jnp.concatenate([d_conv.reshape(K1, n, ncol).transpose(1, 0, 2).reshape(n, -1), small[0].reshape(n, -1),
                             jnp.broadcast_to(d_heads.reshape(1, -1), (n, d_heads.size))], axis=1)
     tiles = -(-mine.shape[1] // 1024)
     mine = jnp.pad(mine, ((0, 0), (0, tiles * 1024 - mine.shape[1]))).reshape(n, tiles * 8, 128)
-    tot = exchange(mine, nd, nf, 2).reshape(-1)
-    cut = [0, K1 * ncol, nrow, ngate, d_heads.size]
-    ends = [sum(cut[: k + 1]) for k in range(5)]
-    t_conv, t_norm, t_gate, t_heads = (tot[ends[k] : ends[k + 1]] for k in range(4))
+    split = (((0, 0, E // 2),), ((1, 0, E // 2), (2, 0, wide)))
+    sum1, output, grad_in, tot, d_norm = tail(nd, nf, 1, (grad(dz1[0]), grad(dz1[1]), grad(dbcdt)), split, dz0, dz1, dbcdt, full_gate, full_a, gg,
+                                              full_out, hidden, grad_out, r, norm_gain[None], mine)
+    tot = tot.reshape(-1)
+    me = lax.axis_index("dp") * nf + lax.axis_index("fsdp")
+    t_norm = lax.dynamic_slice(d_norm.reshape(-1), (me * nrow,), (nrow,))
+    cut = [0, K1 * ncol, ngate, d_heads.size]
+    ends = [sum(cut[: k + 1]) for k in range(4)]
+    t_conv, t_gate, t_heads = (tot[ends[k] : ends[k + 1]] for k in range(3))
     Eh = E // 2
     s_zx = jnp.concatenate([sum0[:, :Eh], sum1[:, :Eh], sum0[:, Eh:], sum1[:, Eh : 2 * Eh]], axis=1)
     return (output, grad_in, s_zx, sum1[:, 2 * Eh : 2 * Eh + 2 * N], sum1[:, 2 * Eh + 2 * N : 2 * Eh + 2 * N + H], s_out,

time: 545 us -> 501 us (0.919)
  Pallas kernels: 367 us -> 328 us
  local copies, waits for them, and re-layouts: 41.8 us -> 35.9 us
    pallas_call x6 -> x5, Pallas kernels: 241 us -> 210 us  [the longest x2 117 us: bwd(): pl.pallas_call(functools.partial(bwd_scatter_kernel, nd, nf, g0, len(firs...]
    pallas_call x1, Pallas kernels: 47.2 us -> 39.8 us  [fwd(): pl.pallas_call(fwd_kernel, grid=(G,), in_specs=[col(0), col(0), pl.BlockS...]
  transfers between devices with their start and end apart: 2 -> 2, of which waited for: 0 -> 0; matrix products, arithmetic and copies ran while one was open for 13% -> 14% of each run, Pallas kernels for 27% -> 25%
where the time goes in v5:
time: 501 us; the launch traced here: 493 us
  Pallas kernels  328 us (65%)
  matrix products  102 us (20%)
  local copies, waits for them, and re-layouts  35.9 us (7%)
  between operations  14.8 us (3%)
  other arithmetic  10.9 us (2%)
    pallas_call x2, Pallas kernels, bwd(): pl.pallas_call(functools.partial(bwd_scatter_kernel, nd, nf, g0, len(firs...  117 us
    dot_general x9, matrix products, dot(): lax.dot_general(a, b, (dims, ((), ())), preferred_element_type=f32, preci...  102 us
    pallas_call x1, Pallas kernels, gather_rows(): pl.pallas_call(functools.partial(gather_kernel, nd, nf), out_shape=jax.Sh...  77.9 us
    pallas_call x1, Pallas kernels, tail(): pl.pallas_call(functools.partial(tail_kernel, nd, nf, len(gs), split, til...  77.8 us
    pallas_call x1, Pallas kernels, fwd(): pl.pallas_call(fwd_kernel, grid=(G,), in_specs=[col(0), col(0), pl.BlockS...  39.8 us
  transfers between devices with their start and end apart: 2, of which 0 were waited for; matrix products, arithmetic and copies ran while one was open for 14% of the time, Pallas kernels for 25%

profile of v5, /device:TPU:0, one launch (start us, length us, event | category | flops | bytes accessed | tf_op | source)
XLA Modules:
  0.0 492.6 jit_solution(411486324269280395)
XLA Ops:
  7.2 1.8 fusion.34
  15.0 1.6 concatenate.49.src_ref
  16.6 77.9 %shard_map.186 = bf16[32,48,3456]{2,1,0:T(8,128)(2,1)} custom-call(bf16[48,3456]{1,0:T(8,128)(2,1)} %concatenate.49.src_ref), custom_call_target="tpu_custom_call" | custom-call | tf_op jit(solution)/shard_map/pallas_call | solution.py:178
  101.9 2.7 fusion
  104.6 17.5 %convolution_convert_fusion.5.bcdt_ref.u_ref.refs_1_.refs_2_ = bf16[1024,3456]{1,0:T(8,128)(2,1)} fusion(bf16[1536,3456]{1,0:T(8,128)(2,1)} %bitcast.53, bf16[1024,1536]{1,0:T(8,128)(2,1)} %refs_10_.1, f32[1536]{0:T(1024)S(1)} %reshape.183, f32[1024]{0:T(1024)S(1)} %add_rsqrt_fusion.1), kind=kOutput, calls=%fused_computation.8 | convolution fusion | flops 10881466368 | bytes 20850688 | tf_op jit(solution)/shard_map/dot_general | solution.py:445
  122.1 7.2 %shard_map.187 = (bf16[1024,128]{1,0:T(8,128)(2,1)}, bf16[1024,128]{1,0:T(8,128)(2,1)}, bf16[128,1024]{1,0:T(8,128)(2,1)}, bf16[128,1024]{1,0:T(8,128)(2,1)}, f3...) custom-call(bf16[1024,3456]{1,0:T(8,128)(2,1)} %convolution_convert_, ...), custom_call_target="tpu_custom_call" | custom-call | tf_op jit(solution)/shard_map/pallas_call | solution.py:529
  130.0 14.3 %convolution_convert_fusion.7.gate_ref.refs_2_.refs_3_ = bf16[1024,3072]{1,0:T(8,128)(2,1)} fusion(bf16[1536,3072]{1,0:T(8,128)(2,1)} %all-gather.3.cloned.1.call-done.refs_4_, bf16[1024,1536]{1,0:T(8,128)(2,1)S(1)} %copy-done.1, f32[1536]{0:T(1024)S(1)} %reshape.183, f32[1024]{0:T(1024)S(1)} %add_rsqrt_fusion.1), kind=kOutput, calls=%fused_computation.14 | convolution fusion | flops 9673113600 | bytes 18884608 | tf_op jit(solution)/shard_map/dot_general | solution.py:445
  144.3 39.8 %shard_map.188 = (bf16[1024,3072]{1,0:T(8,128)(2,1)}, f32[1024,128]{1,0:T(8,128)}, bf16[1024,3072]{1,0:T(8,128)(2,1)}, bf16[8,128,3072]{2,1,0:T(8,128)(2,1)}) custom-call(bf16[1024,3456]{1,0:T(8,128)(2,1)} %convolution_convert_fusion.5.bcdt_ref.u_ref.refs_1_.refs_2_, bf16[1024,3072]{1,0:T(8,128)(2,1)} %convolution_convert_fusion.7.gate_ref.refs_2_.refs_3_, ...), custom_call_target="tpu_custom_call" | custom-call | flops 4831838208 | bytes 37748736 | tf_op jit(solution)/shard_map/pallas_call | solution.py:620
  185.4 16.0 %convolution_convert_fusion = bf16[3072,1536]{1,0:T(8,128)(2,1)} fusion(bf16[1024,3072]{1,0:T(8,128)(2,1)} %get-tuple-element.55.refs_6_, bf16[1024,1536]{1,0:T(8,128)(2,1)} %refs_11_.1, f32[1024]{0:T(1024)S(1)} %add_rsqrt_fusion), kind=kOutput, calls=%fused_computation.1 | convolution fusion | flops 9673113600 | bytes 18878464 | tf_op jit(solution)/shard_map/dot_general | solution.py:445
  201.4 17.0 %multiply_reduce_fusion = (f32[1024]{0:T(1024)S(1)}, bf16[1024,3072]{1,0:T(8,128)(2,1)}) fusion(bf16[1024,3072]{1,0:T(8,128)(2,1)} %get-tuple-element.55.refs_6_, bf16[1024,1536]{1,0:T(8,128)(2,1)} %refs_11_.1, bf16[3072,1536]{1,0:T(8,128)(2,1)} %all-gather.5.cloned.1.call-done.refs_3_), kind=kOutput, calls=%fused_computation | convolution fusion | flops 9679404032 | bytes 25169920 | tf_op jit(solution)/shard_map/dot_general | solution.py:445
  219.4 56.6 %shard_map.189 = (bf16[2,1024,1536]{2,1,0:T(8,128)(2,1)}, f32[8,128,128]{2,1,0:T(8,128)}, f32[1024,128]{1,0:T(8,128)}, f32[1024,128]{1,0:T(8,128)}, f32[1024,128...) custom-call(bf16[32,96,1536]{2,1,0:T(8,128)(2,1)} %bitcast.55, ...), custom_call_target="tpu_custom_call" | custom-call | flops 4026531840 | bytes 25165824 | tf_op jit(solution)/shard_map/pallas_call | solution.py:789
  276.0 9.2 %convolution_convert_fusion.3 = bf16[1536,1536]{1,0:T(8,128)(2,1)} fusion(bf16[2,1024,1536]{2,1,0:T(8,128)(2,1)} %get-tuple-element.60.refs_7_, bf16[1024,1536]{1,0:T(8,128)(2,1)S(1)} %copy-done.1, f32[1536]{0:T(1024)S(1)} %reshape.183, f32[1024]{0:T(1024)S(1)} %add_rsqrt_fusion.1), kind=kOutput, calls=%fused_computation.6 | convolution fusion | flops 4840488960 | bytes 11020288 | tf_op jit(solution)/shard_map/dot_general | solution.py:445
  285.2 7.6 %convolution_convert_fusion.4 = bf16[1536,1536]{1,0:T(8,128)(2,1)} fusion(bf16[2,1024,1536]{2,1,0:T(8,128)(2,1)S(1)} %copy-done.15, bf16[1024,1536]{1,0:T(8,128)(2,1)S(1)} %copy-done.1, f32[1536]{0:T(1024)S(1)} %reshape.183, f32[1024]{0:T(1024)S(1)} %add_rsqrt_fusion.1), kind=kOutput, calls=%fused_computation.7 | convolution fusion | flops 4840488960 | bytes 11022336 | tf_op jit(solution)/shard_map/dot_general | solution.py:445
  292.8 60.8 %shard_map.190 = (bf16[2,1024,1536]{2,1,0:T(8,128)(2,1)}, f32[8,128,128]{2,1,0:T(8,128)}, f32[1024,128]{1,0:T(8,128)}, f32[1024,128]{1,0:T(8,128)}, f32[1024,128...) custom-call(bf16[32,48,1536]{2,1,0:T(8,128)(2,1)} %bitcast.57, ...), custom_call_target="tpu_custom_call" | custom-call | flops 4026531840 | bytes 25165824 | tf_op jit(solution)/shard_map/pallas_call | solution.py:789
  353.6 9.3 %convolution_convert_fusion.1 = bf16[1536,1536]{1,0:T(8,128)(2,1)} fusion(bf16[2,1024,1536]{2,1,0:T(8,128)(2,1)} %get-tuple-element.61.refs_8_, bf16[1024,1536]{1,0:T(8,128)(2,1)S(1)} %copy-done.1, f32[1536]{0:T(1024)S(1)} %reshape.183, f32[1024]{0:T(1024)S(1)} %add_rsqrt_fusion.1), kind=kOutput, calls=%fused_computation.4 | convolution fusion | flops 4840488960 | bytes 11020288 | tf_op jit(solution)/shard_map/dot_general | solution.py:445
  363.0 7.3 %convolution_convert_fusion.2 = bf16[1536,1536]{1,0:T(8,128)(2,1)} fusion(bf16[2,1024,1536]{2,1,0:T(8,128)(2,1)S(1)} %copy-done.16, bf16[1024,1536]{1,0:T(8,128)(2,1)S(1)} %copy-done.1, f32[1536]{0:T(1024)S(1)} %reshape.183, f32[1024]{0:T(1024)S(1)} %add_rsqrt_fusion.1), kind=kOutput, calls=%fused_computation.5 | convolution fusion | flops 4840488960 | bytes 11022336 | tf_op jit(solution)/shard_map/dot_general | solution.py:445
  373.6 7.9 %shard_map.191 = (bf16[1024,384]{1,0:T(8,128)(2,1)}, f32[8,256]{1,0:T(8,128)}, f32[2,48]{1,0:T(2,128)}) custom-call(bf16[1024,3456]{1,0:T(8,128)(2,1)} %convolution_convert_fusion.5.bcdt_ref.u_ref.refs_1_.refs_2_, f32[1024,256]{1,0:T(8,128)} %get-tuple-element.62.pre_ref, f32[8,256]{1,0:T(8,128)} %concatenate.54.taps_ref, f32[8,128]{1,0:T(8,128)} %pad.18.heads_ref, ...), custom_call_target="tpu_custom_call" | custom-call | tf_op jit(solution)/shard_map/pallas_call | solution.py:873
  384.5 4.1 convolution_convert_fusion.8
  388.6 77.8 %shard_map.192 = (f32[48,3456]{1,0:T(8,128)}, bf16[1024,1536]{1,0:T(8,128)(2,1)}, bf16[1024,1536]{1,0:T(8,128)(2,1)}, f32[8,128]{1,0:T(8,128)}, f32[16,128]{1,0:T(8,128)}) custom-call(bf16[32,48,1536]{2,1,0:T(8,128)(2,1)} %bitcast.82, bf16[32,48,1536]{2,1,0:T(8,128)(2,1)} %bitcast.81, bf16[32,48,384]{2,1,0:T(8,128)(2,1)} %bitcast.83, ...), custom_call_target="tpu_custom_call" | custom-call | flops 28991029248 | bytes 37748736 | tf_op jit(solution)/shard_map/pallas_call | solution.py:989
  466.4 1.6 slice.169
  471.4 2.2 fusion.32
  476.8 2.2 pad_maximum_fusion
  479.0 3.8 copy.97
  482.8 1.7 copy.98
  (115 shorter events, 30.0 us)
Async XLA Ops:
  7.2 122.8 %all-gather.3.cloned.1.call-start = ((), (), s32[]{:S(2)}) async-start(), calls=%async_computation | async-start | bytes 9732096 | tf_op jit(solution)/shard_map/all_gather | solution.py:1009
  9.1 192.3 %all-gather.5.cloned.1.call-start = ((), (), s32[]{:S(2)}) async-start(), calls=%async_computation.1 | async-start | bytes 9732096 | tf_op jit(solution)/shard_map/all_gather | solution.py:1010
  16.6 80.5 %copy-start.5 = (s32[1024]{0:T(1024)S(1)}, s32[1024]{0:T(1024)}, u32[]{:S(2)}) copy-start(s32[1024]{0:T(1024)} %param.13) | copy-start | bytes 12292
  16.6 83.4 %copy-start.14 = (f32[3,48]{1,0:T(4,128)S(1)}, f32[3,48]{1,0:T(4,128)}, u32[]{:S(2)}) copy-start(f32[3,48]{1,0:T(4,128)} %param.21) | copy-start | bytes 1732
  96.2 25.8 %copy-start.4 = (f32[5,3328]{1,0:T(8,128)}, f32[5,3328]{1,0:T(8,128)S(1)}, u32[]{:S(2)}) copy-start(f32[5,3328]{1,0:T(8,128)S(1)} %reshape.184) | copy-start | bytes 199684
  96.4 266.5 %copy-start.11 = (f32[1536]{0:T(1024)}, f32[1536]{0:T(1024)S(1)}, u32[]{:S(2)}) copy-start(f32[1536]{0:T(1024)S(1)} %reshape.183) | copy-start | bytes 18436
  98.1 24.0 %copy-start = (f32[1024,4]{1,0:T(8,128)}, f32[1024,4]{1,0:T(8,128)S(1)}, u32[]{:S(2)}) copy-start(f32[1024,4]{1,0:T(8,128)S(1)} %copy.82.m_ref) | copy-start | bytes 49156
  122.1 7.2 %slice-start = ((f32[5,3328]{1,0:T(8,128)}), f32[5,3072]{1,0:T(8,128)S(1)}, s32[]{:S(2)}) async-start(f32[5,3328]{1,0:T(8,128)} %copy-done.4), calls=%async_computation.2 | async-start | bytes 196608 | tf_op jit(solution)/shard_map/slice | solution.py:1031
  122.1 7.9 %copy-start.1 = (bf16[1024,1536]{1,0:T(8,128)(2,1)S(1)}, bf16[1024,1536]{1,0:T(8,128)(2,1)}, u32[]{:S(2)}) copy-start(bf16[1024,1536]{1,0:T(8,128)(2,1)} %refs_10_.1) | copy-start | bytes 9437188
  276.0 9.2 %copy-start.15 = (bf16[2,1024,1536]{2,1,0:T(8,128)(2,1)S(1)}, bf16[2,1024,1536]{2,1,0:T(8,128)(2,1)}, u32[]{:S(2)}) copy-start(bf16[2,1024,1536]{2,1,0:T(8,128)(2,1)} %get-tuple-element.60.refs_7_) | copy-start | bytes 18874372
  353.6 9.3 %copy-start.16 = (bf16[2,1024,1536]{2,1,0:T(8,128)(2,1)S(1)}, bf16[2,1024,1536]{2,1,0:T(8,128)(2,1)}, u32[]{:S(2)}) copy-start(bf16[2,1024,1536]{2,1,0:T(8,128)(2,1)} %get-tuple-element.61.refs_8_) | copy-start | bytes 18874372
  362.9 8.4 %copy-start.6 = (f32[8,1536]{1,0:T(8,128)S(1)}, f32[8,1536]{1,0:T(8,128)}, u32[]{:S(2)}) copy-start(f32[8,1536]{1,0:T(8,128)} %get-tuple-element.75) | copy-start | bytes 147460
  362.9 8.4 %copy-start.7 = (f32[8,1536]{1,0:T(8,128)S(1)}, f32[8,1536]{1,0:T(8,128)}, u32[]{:S(2)}) copy-start(f32[8,1536]{1,0:T(8,128)} %get-tuple-element.76) | copy-start | bytes 147460
  363.0 9.8 %copy-start.8 = (f32[8,1536]{1,0:T(8,128)S(1)}, f32[8,1536]{1,0:T(8,128)}, u32[]{:S(2)}) copy-start(f32[8,1536]{1,0:T(8,128)} %get-tuple-element.71) | copy-start | bytes 147460
  363.0 9.8 %copy-start.9 = (f32[8,1536]{1,0:T(8,128)S(1)}, f32[8,1536]{1,0:T(8,128)}, u32[]{:S(2)}) copy-start(f32[8,1536]{1,0:T(8,128)} %get-tuple-element.72) | copy-start | bytes 147460
  373.6 8.0 %copy-start.13 = (f32[48]{0:T(128)S(1)}, f32[48]{0:T(128)}, u32[]{:S(2)}) copy-start(f32[48]{0:T(128)} %reduce_sum.54) | copy-start | bytes 580
  373.6 9.7 %copy-start.10 = (f32[1,3072]{1,0:T(1,128)S(1)}, f32[1,3072]{1,0:T(1,128)}, u32[]{:S(2)}) copy-start(f32[1,3072]{1,0:T(1,128)} %get-tuple-element.98) | copy-start | bytes 36868
  373.6 11.0 %copy-start.12 = (f32[1536]{0:T(1024)S(1)}, f32[1536]{0:T(1024)}, u32[]{:S(2)}) copy-start(f32[1536]{0:T(1024)} %copy-done.11) | copy-start | bytes 18436
  466.4 16.4 %copy-start.2 = (bf16[1024,1536]{1,0:T(8,128)(2,1)S(1)}, bf16[1024,1536]{1,0:T(8,128)(2,1)}, u32[]{:S(2)}) copy-start(bf16[1024,1536]{1,0:T(8,128)(2,1)} %get-tuple-element.122) | copy-start | bytes 9437188
  479.0 5.5 %copy-start.3 = (f32[96,1536]{1,0:T(8,128)S(1)}, f32[96,1536]{1,0:T(8,128)}, u32[]{:S(2)}) copy-start(f32[96,1536]{1,0:T(8,128)} %get-tuple-element.126) | copy-start | bytes 1769476
Sparse Core Ops, SparseCore 0:
  10.9 97.3 all-gather.2
  111.2 82.3 all-gather.4

commit v6 on v5

--- a/solution.py
+++ b/solution.py
@@ -10,10 +10,9 @@
 L = 128
 HG = 8
 LOG2E = 1.4426950408889634
-BWD_PLAN = (2, 5, 2, 14, 2)
-BWD_TICKS = 23
-TAIL_PLAN = (6, 12, 4, 28, 4)
-TAIL_TICKS = 47
+MB = 512
+BWD_SPOTS = ((5.0, 10.0, 2.0, 26.0, 3.2), (7.0, 16.5, 2.0, 39.0, 3.2))
+TAIL_SPOTS = ((7.0, 13.0, 3.0, 30.0, 4.0), (9.0, 22.0, 3.0, 46.0, 3.0))
 bf16, f32 = jnp.bfloat16, jnp.float32
 HIGHEST = lax.Precision.HIGHEST
 
@@ -192,42 +191,42 @@
         at = Place(nd, nf)
         z, y, x, c, zn = at.z, at.y, at.x, at.c, at.zn
         cols = out_ref.shape[1]
-        offs = [sum(r.shape[2] for r in g_refs[:k]) for k in range(len(g_refs))]
+        wids = [r.shape[3] for r in g_refs]
+        offs = [sum(wids[:k]) for k in range(len(wids))]
         half = cols // 256 * 128
         lo, hi = pl.ds(0, half), pl.ds(half, cols - half)
 
-        def idx(zs, col, core):
-            return at.idx(zs, 1 - y if col & 2 else y, 1 - x if col & 1 else x, core)
+        def inner(col, core):
+            return at.idx(0, 1 - y if col & 2 else y, 1 - x if col & 1 else x, core)
 
         def remote(src, dst, to, send, recv):
             return pltpu.make_async_remote_copy(src_ref=src, dst_ref=dst, send_sem=send, recv_sem=recv, device_id=at.dev(*to), device_id_type=MESH)
 
-        def load(zs, col):
-            return [pltpu.make_async_copy(r.at[idx(zs, col, c)], acc.at[zs, col, :, pl.ds(o, r.shape[2])], load_sem.at[zs, col, k])
-                    for k, (r, o) in enumerate(zip(g_refs, offs))]
-
-        def core(zs, col):
-            return [remote(r.at[idx(zs, col, 1 - c)], c_in.at[zs, col, :, pl.ds(o, r.shape[2])], (z, y, x, 1 - c),
-                           c_send.at[zs, col, k], c_recv.at[zs, col, k])
-                    for k, (r, o) in enumerate(zip(g_refs, offs))]
+        def load(col):
+            return [pltpu.make_async_copy(r.at[:, inner(col, c)], acc.at[col, :, :, pl.ds(o, w)], load_sem.at[col, k])
+                    for k, (r, o, w) in enumerate(zip(g_refs, offs, wids))]
+
+        def core(col):
+            return [remote(r.at[:, inner(col, 1 - c)], c_in.at[col, :, :, pl.ds(o, w)], (z, y, x, 1 - c), c_send.at[col, k], c_recv.at[col, k])
+                    for k, (r, o, w) in enumerate(zip(g_refs, offs, wids))]
 
         def diag_x(zs):
-            return remote(acc.at[zs, 3, :, lo], d_in.at[zs, :, lo], (z, y, 1 - x, c), dx_send.at[zs], dx_recv.at[zs])
+            return remote(acc.at[3, zs, :, lo], d_in.at[zs, :, lo], (z, y, 1 - x, c), dx_send.at[zs], dx_recv.at[zs])
 
         def diag_y(zs):
-            return remote(acc.at[zs, 3, :, hi], d_in.at[zs, :, hi], (z, 1 - y, x, c), dy_send.at[zs], dy_recv.at[zs])
+            return remote(acc.at[3, zs, :, hi], d_in.at[zs, :, hi], (z, 1 - y, x, c), dy_send.at[zs], dy_recv.at[zs])
 
         def to_x(zs):
-            return remote(acc.at[zs, 1], xy_in.at[0, zs], (z, y, 1 - x, c), x_send.at[zs], x_recv.at[zs])
+            return remote(acc.at[1, zs], xy_in.at[0, zs], (z, y, 1 - x, c), x_send.at[zs], x_recv.at[zs])
 
         def to_y(zs):
-            return remote(acc.at[zs, 2], xy_in.at[1, zs], (z, 1 - y, x, c), y_send.at[zs], y_recv.at[zs])
+            return remote(acc.at[2, zs], xy_in.at[1, zs], (z, 1 - y, x, c), y_send.at[zs], y_recv.at[zs])
 
         def up(zs):
-            return remote(acc.at[zs, 0], z_in.at[zs + 1], (z + 1, y, x, c), z_send.at[zs], z_recv.at[0, zs])
+            return remote(acc.at[0, zs], z_in.at[zs + 1], (z + 1, y, x, c), z_send.at[zs], z_recv.at[0, zs])
 
         def down(zs):
-            return remote(acc.at[zs, 0], z_in.at[zs], (z - 1, y, x, c), z_send.at[zs], z_recv.at[1, zs])
+            return remote(acc.at[0, zs], z_in.at[zs], (z - 1, y, x, c), z_send.at[zs], z_recv.at[1, zs])
 
         def each(dist, fn):
             if dist == 0:
@@ -245,41 +244,34 @@
         order = list(range(zn - 1, -1, -1))
 
         def start(col):
-            for dist in order:
-                def one(zs):
-                    for cp in core(zs, col) + load(zs, col):
-                        cp.start()
-                each(dist, one)
-
-        def ready(zs, col):
-            for cp in load(zs, col):
+            for cp in core(col) + load(col):
+                cp.start()
+
+        def ready(col):
+            for cp in load(col):
                 cp.wait()
-            for cp in core(zs, col):
+            for cp in core(col):
                 cp.wait_recv()
 
         def diag(zs):
-            ready(zs, 3)
-            acc[zs, 3] = acc[zs, 3] + c_in[zs, 3]
+            acc[3, zs] = acc[3, zs] + c_in[3, zs]
             diag_x(zs).start()
             diag_y(zs).start()
 
         def sides(zs):
-            ready(zs, 1)
             diag_y(zs).wait_recv()
-            acc[zs, 1, :, lo] = acc[zs, 1, :, lo] + c_in[zs, 1, :, lo]
-            acc[zs, 1, :, hi] = acc[zs, 1, :, hi] + c_in[zs, 1, :, hi] + d_in[zs, :, hi]
+            acc[1, zs, :, lo] = acc[1, zs, :, lo] + c_in[1, zs, :, lo]
+            acc[1, zs, :, hi] = acc[1, zs, :, hi] + c_in[1, zs, :, hi] + d_in[zs, :, hi]
             to_x(zs).start()
-            ready(zs, 2)
             diag_x(zs).wait_recv()
-            acc[zs, 2, :, lo] = acc[zs, 2, :, lo] + c_in[zs, 2, :, lo] + d_in[zs, :, lo]
-            acc[zs, 2, :, hi] = acc[zs, 2, :, hi] + c_in[zs, 2, :, hi]
+            acc[2, zs, :, lo] = acc[2, zs, :, lo] + c_in[2, zs, :, lo] + d_in[zs, :, lo]
+            acc[2, zs, :, hi] = acc[2, zs, :, hi] + c_in[2, zs, :, hi]
             to_y(zs).start()
 
         def column(zs):
-            ready(zs, 0)
             to_x(zs).wait_recv()
             to_y(zs).wait_recv()
-            return (acc[zs, 0] + c_in[zs, 0]).astype(f32) + (xy_in[0, zs] + xy_in[1, zs]).astype(f32)
+            return (acc[0, zs] + c_in[0, zs]).astype(f32) + (xy_in[0, zs] + xy_in[1, zs]).astype(f32)
 
         def pass_on(zs):
             total = column(zs)
@@ -289,11 +281,11 @@
                 @pl.when(z > 0)
                 def _():
                     up(zs).wait_recv()
-                    acc[zs, 0] = (total + z_in[zs + 1].astype(f32)).astype(bf16)
+                    acc[0, zs] = (total + z_in[zs + 1].astype(f32)).astype(bf16)
 
                 @pl.when(z == 0)
                 def _():
-                    acc[zs, 0] = total.astype(bf16)
+                    acc[0, zs] = total.astype(bf16)
                 up(zs).start()
 
             @pl.when(zs < z)
@@ -301,11 +293,11 @@
                 @pl.when(z < zn - 1)
                 def _():
                     down(zs).wait_recv()
-                    acc[zs, 0] = (total + z_in[zs].astype(f32)).astype(bf16)
+                    acc[0, zs] = (total + z_in[zs].astype(f32)).astype(bf16)
 
                 @pl.when(z == zn - 1)
                 def _():
-                    acc[zs, 0] = total.astype(bf16)
+                    acc[0, zs] = total.astype(bf16)
                 down(zs).start()
 
         def finish():
@@ -322,68 +314,83 @@
                 out_ref[...] += z_in[z].astype(f32)
 
             def sent(zs):
-                for col in range(4):
-                    for cp in core(zs, col):
-                        cp.wait_send()
                 diag_x(zs).wait_send()
                 diag_y(zs).wait_send()
                 to_x(zs).wait_send()
                 to_y(zs).wait_send()
 
+            for col in range(4):
+                for cp in core(col):
+                    cp.wait_send()
             for dist in order:
                 each(dist, sent)
                 if dist:
                     each(dist, lambda zs: up(zs).wait_send())
 
         self.start, self.finish, self.barrier = start, finish, at.barrier
-        self.diag = [functools.partial(each, dist, diag) for dist in order]
+        self.diag = [functools.partial(ready, 3)] + [functools.partial(each, dist, diag) for dist in order]
         self.sides = [functools.partial(each, dist, sides) for dist in order]
         self.pass_on = [functools.partial(each, dist, pass_on) for dist in order[:-1]]
+        self.ready = lambda: (ready(1), ready(2), ready(0))
 
     @staticmethod
     def scratch(nd, rows, cols, parts):
         zn = nd // 2
         D, V = pltpu.SemaphoreType.DMA, pltpu.VMEM
-        return [V((zn, 4, rows, cols), bf16), V((zn, 4, rows, cols), bf16), V((zn, rows, cols), bf16), V((2, zn, rows, cols), bf16),
-                V((zn + 1, rows, cols), bf16), D((zn, 4, parts)), D((zn, 4, parts)), D((zn, 4, parts))] + [D((zn,))] * 9 + [D((2, zn))]
-
-
-def plan(pipes, barrier, diag, sides, side_gap, pass_on, pass_gap):
+        return [V((4, zn, rows, cols), bf16), V((4, zn, rows, cols), bf16), V((zn, rows, cols), bf16), V((2, zn, rows, cols), bf16),
+                V((zn + 1, rows, cols), bf16), D((4, parts)), D((4, parts)), D((4, parts))] + [D((zn,))] * 9 + [D((2, zn))]
+
+
+def plan(pipes, barrier, time_of, spots):
     ticks = {0: [barrier] + [functools.partial(p.start, col) for col in (3, 1, 2, 0) for p in pipes]}
-    for m, p in enumerate(pipes):
-        ticks.setdefault(diag + m, []).extend(p.diag)
-        for k, fn in enumerate(p.sides):
-            ticks.setdefault(sides + k * side_gap + m * (side_gap // 2), []).append(fn)
-        for k, fn in enumerate(p.pass_on):
-            ticks.setdefault(pass_on + k * pass_gap + m * (pass_gap // 2), []).append(fn)
+
+    def put(when, fn):
+        tick = next((t for t, us in enumerate(time_of) if us >= when), len(time_of))
+        ticks.setdefault(tick, []).append(fn)
+
+    todo = []
+    for p, (diag, sides, side_gap, pass_on, pass_gap) in zip(pipes, spots):
+        todo += [(diag, fn) for fn in p.diag] + [(sides, p.ready)]
+        todo += [(sides + k * side_gap * 4 / len(p.sides), fn) for k, fn in enumerate(p.sides)]
+        todo += [(pass_on + k * pass_gap * 4 / len(p.sides), fn) for k, fn in enumerate(p.pass_on)]
+    for when, fn in sorted(todo, key=lambda e: e[0]):
+        put(when, fn)
     return ticks
 
 
-def columns(refs, split):
-    return [[refs[a].at[:, :, pl.ds(o, w)] for a, o, w in pipe] for pipe in split]
-
-
-def pipes_of(nd, nf, g_refs, out_ref, split, scratch):
-    pipes, off = [], 0
+def pipes_of(nd, nf, g_refs, out_refs, split, scratch):
+    def view(a, lead, o, w):
+        return g_refs[a].at[:, :, :, pl.ds(o, w)] if lead is None else g_refs[a].at[lead, :, :, :, pl.ds(o, w)]
     per = len(scratch) // len(split)
-    for m, (views, pipe) in enumerate(zip(columns(g_refs, split), split)):
-        width = sum(w for _, _, w in pipe)
-        pipes.append(Scatter(nd, nf, views, out_ref.at[:, pl.ds(off, width)], *scratch[per * m : per * (m + 1)]))
-        off += width
-    return pipes
+    return [Scatter(nd, nf, [view(*v) for v in pipe], out_ref, *scratch[per * m : per * (m + 1)])
+            for m, (pipe, out_ref) in enumerate(zip(split, out_refs))]
+
+
+def widths(split):
+    return [sum(v[3] for v in pipe) for pipe in split]
 
 
 def pipes_scratch(nd, rows, split):
-    return [x for pipe in split for x in Scatter.scratch(nd, rows, sum(w for _, _, w in pipe), len(pipe))]
+    return [x for pipe, w in zip(split, widths(split)) for x in Scatter.scratch(nd, rows, w, len(pipe))]
 
 
 def run_ticks(ticks, now, last):
-    for tick, fns in ticks.items():
-        if tick <= last:
+    planned = sorted((t, fns) for t, fns in ticks.items() if t <= last)
+
+    def search(items):
+        if len(items) == 1:
+            tick, fns = items[0]
+
             @pl.when(now == tick)
-            def _(fns=fns):
+            def _():
                 for fn in fns:
                     fn()
+            return
+        mid = len(items) // 2
+        lax.cond(now < items[mid][0], lambda: search(items[:mid]), lambda: search(items[mid:]))
+
+    if planned:
+        search(planned)
 
 
 def run_rest(ticks, last):
@@ -460,8 +467,8 @@
     return out
 
 
-def prep_kernel(bcdt_ref, taps_ref, heads_ref, m_ref, segc_ref, segr_ref,
-                b_ref, c_ref, bt_ref, ct_ref, pre_ref, gm_ref, cum_ref, cumr_ref, sc_ref, dt_ref):
+def prep_kernel(bcdt_ref, taps_ref, heads_ref, segc_ref, segr_ref,
+                m_ref, b_ref, c_ref, bt_ref, ct_ref, pre_ref, gm_ref, cum_ref, cumr_ref, sc_ref, dt_ref):
     T = bcdt_ref.shape[0]
     nc = T // L
     N = b_ref.shape[1]
@@ -471,6 +478,7 @@
     tri = (lax.broadcasted_iota(jnp.int32, (L, L), 0) >= lax.broadcasted_iota(jnp.int32, (L, L), 1))
     trif = tri.astype(f32)
     neg_rate = -jnp.exp(heads_ref[0:1, :H]) * LOG2E
+    m_ref[T : T + 8, :] = jnp.zeros((8, 4), f32)
     bias = heads_ref[1:2, :H]
 
     def chunk(c, carry):
@@ -479,7 +487,15 @@
         h0 = pl.multiple_of(jnp.maximum(t0 - 16, 0), 16)
         before = bcdt_ref[pl.ds(h0, 16), : 2 * N].astype(f32)
         v = bcdt_ref[here, : 2 * N].astype(f32)
-        pre = conv_rows(jnp.concatenate([before, v], axis=0), taps, m_ref[here, :], 16)
+        segc = segc_ref[here, :].astype(f32)
+        seg_ext = jnp.concatenate([segc_ref[pl.ds(h0, 16), :].astype(f32), segc], axis=0)
+        at = t0 + lax.broadcasted_iota(jnp.int32, (L, 1), 0)
+        masks = [jnp.ones((L, 1), f32)]
+        for k in range(1, 4):
+            masks.append(((pltpu.roll(seg_ext, k, 0)[16:] == segc) & (at >= k)).astype(f32))
+        masks = jnp.concatenate(masks, axis=1)
+        m_ref[here, :] = masks
+        pre = conv_rows(jnp.concatenate([before, v], axis=0), taps, masks, 16)
         pre_ref[here, :] = pre
         act = pre * sigmoid(pre)
         b = act[:, :N]
@@ -490,10 +506,9 @@
         c_ref[here, :] = cb
         bt_ref[:, here] = b.T.astype(bf16)
         ct_ref[:, here] = cc.T.astype(bf16)
-        segc = segc_ref[here, 0:1]
-        prev = segc_ref[here, 1:2]
-        last = segc_ref[here, 2:3]
-        same = segc == segr_ref[:, here]
+        prev = jnp.where(c > 0, seg_ext[15:16], -1.0)
+        last = segc[L - 1 : L]
+        same = segc == segr_ref[:, here].astype(f32)
         g = dot(cb, bb, ((1,), (1,)))
         gm_ref[pl.ds(c, 1)] = jnp.where(tri & same, g, 0.0)[None]
         raw = bcdt_ref[here, 2 * N : 2 * N + 128].astype(f32)[:, :H] + bias
@@ -517,23 +532,23 @@
     lax.fori_loop(0, nc, chunk, 0)
 
 
-def prep(bcdt, taps, heads, masks, segc, segr, N, H):
+def prep(bcdt, taps, heads, segc, segr, N, H):
     T = bcdt.shape[0]
     nc = T // L
     G = H // HG
     S = jax.ShapeDtypeStruct
     full = lambda a: pl.BlockSpec(a.shape, lambda i: (0,) * a.ndim)
-    outs = (S((T, N), bf16), S((T, N), bf16), S((N, T), bf16), S((N, T), bf16), S((T, 2 * N), f32),
+    outs = (S((T + 8, 4), f32), S((T, N), bf16), S((T, N), bf16), S((N, T), bf16), S((N, T), bf16), S((T, 2 * N), f32),
             S((nc, L, L), f32), S((T, 128), f32), S((G, HG, T), f32), S((3 * T, 128), bf16), S((T, H), f32))
     wide = 2 * N + 128
     return pl.pallas_call(
         prep_kernel,
         grid=(1,),
-        in_specs=[pl.BlockSpec((T, wide), lambda i: (0, bcdt.shape[1] // wide - 1))] + [full(a) for a in (taps, heads, masks, segc, segr)],
+        in_specs=[pl.BlockSpec((T, wide), lambda i: (0, bcdt.shape[1] // wide - 1))] + [full(a) for a in (taps, heads, segc, segr)],
         out_specs=[full(o) for o in outs],
         out_shape=outs,
         compiler_params=pltpu.CompilerParams(vmem_limit_bytes=60 << 20),
-    )(bcdt, taps, heads, masks, segc, segr)
+    )(bcdt, taps, heads, segc, segr)
 
 
 def lane_onehot(group, width, per):
@@ -630,22 +645,26 @@
     )(u, gate, taps, masks, b, c, bt, gm, cum, cumr, sc)
 
 
-def bwd_scatter_kernel(nd, nf, g0, arrays, split, *refs):
-    g_refs, ins, outs = refs[:arrays], refs[arrays : arrays + 15], refs[arrays + 15 : arrays + 23]
-    own, comm = refs[arrays + 23 : arrays + 26], refs[arrays + 26 :]
-    pipes = pipes_of(nd, nf, g_refs, outs[7], split, comm)
-    ticks = plan(pipes, pipes[0].barrier, *BWD_PLAN)
-    bwd_body(lambda now: run_ticks(ticks, now, BWD_TICKS), g0, *ins, *outs[:7], *own)
+def bwd_scatter_kernel(nd, nf, g0, Gh, nc, arrays, split, *refs):
+    g_refs, ins, outs = refs[:arrays], refs[arrays : arrays + 16], refs[arrays + 16 : arrays + 24]
+    refs = refs[arrays + 24 :]
+    sums, own, comm = refs[: len(split)], refs[len(split) : len(split) + 3], refs[len(split) + 3 :]
+    pipes = pipes_of(nd, nf, g_refs, sums, split, comm)
+    nb = ins[15].shape[0] // MB
+    time_of = [21.0 * g + (1.9 * i if i < nc else 1.9 * nc + 1.9 * (i - nc)) for g in range(Gh) for i in range(nc + nb)]
+    ticks = plan(pipes, pipes[0].barrier, time_of, BWD_SPOTS)
+    last = len(time_of) - 1
+    bwd_body(lambda i: run_ticks(ticks, pl.program_id(0) * (nc + nb) + i, last), g0, *ins, *outs, *own)
 
     @pl.when(pl.program_id(0) == pl.num_programs(0) - 1)
     def _():
-        run_rest(ticks, BWD_TICKS)
+        run_rest(ticks, last)
         for p in pipes:
             p.finish()
 
 
-def bwd_body(tick, g0, u_ref, gate_ref, pre_ref, dm_ref, rq_ref, taps_ref, m_ref, b_ref, c_ref, ct_ref, gm_ref, cum_ref, cumr_ref, sc_ref, st_ref,
-               dz_ref, dg_ref, db_ref, dc_ref, rs_ref, small_ref, kk_ref, ds, nxt, acc):
+def bwd_body(tick, g0, u_ref, gate_ref, pre_ref, dm_ref, rq_ref, taps_ref, m_ref, b_ref, c_ref, ct_ref, gm_ref, cum_ref, cumr_ref, sc_ref, st_ref, normt_ref,
+             dz_ref, gw_ref, dg_ref, db_ref, dc_ref, rs_ref, small_ref, kk_ref, ds, nxt, acc):
     T, W = u_ref.shape
     P = W // HG
     nc = T // L
@@ -676,7 +695,7 @@
         return jnp.sum(z.reshape(L // 8, 8, W), axis=0)
 
     def chunk(i, carry):
-        tick(step * nc + i)
+        tick(i)
         c = nc - 1 - i
         t0 = pl.multiple_of(c * L, L)
         here = pl.ds(t0, L)
@@ -763,8 +782,17 @@
         small_ref[j : j + 1, :] = jnp.sum(acc[8 * j : 8 * j + 8, :], axis=0, keepdims=True)
     small_ref[7:8, :] = jnp.zeros((1, W), f32)
 
-
-def bwd(half, halves, u, gate, pre, dm, rq, taps, masks, b, c, ct, gm, cum, cumr, sc, st, comm):
+    def weights(i, carry):
+        tick(nc + i)
+        rows = pl.ds(pl.multiple_of(i * MB, MB), MB)
+        for kind in range(2):
+            gw_ref[kind, rows, :] = dot(normt_ref[rows, :], dz_ref[kind]).astype(bf16)
+        return carry
+
+    lax.fori_loop(0, normt_ref.shape[0] // MB, weights, 0)
+
+
+def bwd(half, halves, u, gate, pre, dm, rq, taps, masks, b, c, ct, gm, cum, cumr, sc, st, normt, comm):
     T, E = gate.shape
     N = b.shape[1]
     G = cumr.shape[0]
@@ -779,23 +807,24 @@
     whole = lambda s: pl.BlockSpec(s, lambda g: (0,) * len(s))
     grp = lambda a: pl.BlockSpec((1,) + a.shape[1:], lambda g: (g + g0, 0, 0))
     in_specs = [col, col, col, col, full(rq), pl.BlockSpec((8, W), lambda g: (0, g + g0)), full(masks), full(b), full(c),
-                full(ct), full(gm), full(cum), grp(cumr), full(sc), pl.BlockSpec((nc, N, W), lambda g: (0, 0, g + g0))]
-    out_specs = [pl.BlockSpec((2, T, W), lambda g: (0, 0, g)), whole((nc, L, L)), whole((T, N)), whole((T, N)),
+                full(ct), full(gm), full(cum), grp(cumr), full(sc), pl.BlockSpec((nc, N, W), lambda g: (0, 0, g + g0)), full(normt)]
+    D = normt.shape[0]
+    out_specs = [pl.BlockSpec((2, T, W), lambda g: (0, 0, g)), pl.BlockSpec((2, D, W), lambda g: (0, 0, g)), whole((nc, L, L)), whole((T, N)), whole((T, N)),
                  whole((T, 128)), pl.BlockSpec((8, W), lambda g: (0, g)), pl.BlockSpec((nc, W), lambda g: (0, g))]
-    out_shape = [S((2, T, Eh), bf16), S((nc, L, L), f32), S((T, N), f32), S((T, N), f32), S((T, 128), f32), S((8, Eh), f32), S((nc, Eh), f32)]
+    out_shape = [S((2, T, Eh), bf16), S((2, D, Eh), bf16), S((nc, L, L), f32), S((T, N), f32), S((T, N), f32), S((T, 128), f32), S((8, Eh), f32), S((nc, Eh), f32)]
     scratch = [pltpu.VMEM((N, W), f32), pltpu.VMEM((8, W), f32), pltpu.VMEM((56, W), f32)]
     nd, nf, cid, first, split = comm
-    rows, cols = first[0].shape[1], sum(w for pipe in split for _, _, w in pipe)
+    rows = first[0].shape[-2]
     return pl.pallas_call(
-        functools.partial(bwd_scatter_kernel, nd, nf, g0, len(first), split),
+        functools.partial(bwd_scatter_kernel, nd, nf, g0, Gh, nc, len(first), split),
         grid=(Gh,),
         in_specs=[pl.BlockSpec(memory_space=pl.ANY)] * len(first) + in_specs,
-        out_specs=out_specs + [whole((rows, cols))],
-        out_shape=out_shape + [S((rows, cols), f32)],
+        out_specs=out_specs + [whole((rows, w)) for w in widths(split)],
+        out_shape=out_shape + [S((rows, w), f32) for w in widths(split)],
         scratch_shapes=scratch + pipes_scratch(nd, rows, split),
         compiler_params=pltpu.CompilerParams(vmem_limit_bytes=60 << 20, collective_id=cid, has_side_effects=True),
-        cost_estimate=pl.CostEstimate(flops=T * Eh * (8 * L + 12 * N), bytes_accessed=T * Eh * 16, transcendentals=T * Eh * 4),
-    )(*first, u, gate, pre, dm, rq, taps, masks, b, c, ct, gm, cum, cumr, sc, st)
+        cost_estimate=pl.CostEstimate(flops=T * Eh * (8 * L + 12 * N + 4 * D), bytes_accessed=T * Eh * 16, transcendentals=T * Eh * 4),
+    )(*first, u, gate, pre, dm, rq, taps, masks, b, c, ct, gm, cum, cumr, sc, st, normt)
 
 
 def post_kernel(bcdt_ref, pre_ref, taps_ref, heads_ref, m_ref, segc_ref, segr_ref, b_ref, c_ref, dg0_ref, db0_ref, dc0_ref, rs0_ref, dg1_ref, db1_ref, dc1_ref, rs1_ref, kk_ref, dt_ref,
@@ -821,7 +850,7 @@
         c = nc - 1 - i
         t0 = pl.multiple_of(c * L, L)
         here = pl.ds(t0, L)
-        same = segc_ref[here, 0:1] == segr_ref[:, here]
+        same = segc_ref[here, :] == segr_ref[:, here]
         dg = jnp.where(tri & same, dg0_ref[c] + dg1_ref[c], 0.0)
         dgb = dg.astype(bf16)
         dcv = dc0_ref[here, :] + dc1_ref[here, :] + dot(dgb, b_ref[here, :])
@@ -887,17 +916,23 @@
 def tail_kernel(nd, nf, arrays, split, tiles, *refs):
     g_refs, refs = refs[:arrays], refs[arrays:]
     (wo_hbm, wg_hbm, wa_hbm, gg_ref, dz0_ref, dz1_ref, dbc_ref, hid_ref, go_ref, r_ref, gain_ref, mine_ref,
-     sum_ref, out_ref, gin_ref, small_ref, dnorm_ref) = refs[:17]
+     suma_ref, sumb_ref, out_ref, gin_ref, small_ref, dnorm_ref) = refs[:18]
+    refs = refs[1:]
     wo, wg, wa, acc, dn, flat, sem = refs[17:24]
     mine = Spread(nd, nf, mine_ref, *refs[24:27])
     norm = Spread(nd, nf, flat, *refs[27:30])
-    pipes = pipes_of(nd, nf, g_refs, sum_ref, split, refs[30:])
+    pipes = pipes_of(nd, nf, g_refs, (suma_ref, sumb_ref), split, refs[30:])
     D, E = wg.shape
     Eh = E // 2
     step = pl.program_id(0)
     early = tiles // 2
     blocks = D // NT
-    ticks = plan(pipes, mine.barrier, *TAIL_PLAN)
+    mid = (early + tiles) * blocks
+    scale = 4 / tiles
+    time_of = [4 + 0.75 * scale * t if t < early * blocks else
+               (13 + 1.65 * scale * (t - early * blocks) if t < mid else 52.6 + 0.65 * scale * (t - mid)) for t in range(2 * tiles * blocks)]
+    ticks = plan(pipes, mine.barrier, time_of, TAIL_SPOTS)
+    last = len(time_of) - 1
     ticks[0].append(mine.begin)
     ticks.setdefault((early + tiles) * blocks + 2, []).append(norm.begin)
     fetch = [pltpu.make_async_copy(src, dst, sem.at[k]) for k, (src, dst) in enumerate(((wo_hbm, wo), (wg_hbm, wg), (wa_hbm, wa)))]
@@ -921,7 +956,7 @@
     @pl.when(jnp.logical_not(back))
     def _():
         def block(j, carry):
-            run_ticks({t: f for t, f in ticks.items() if t and not in_back(t)}, step * blocks + j, TAIL_TICKS)
+            run_ticks({t: f for t, f in ticks.items() if t and not in_back(t)}, step * blocks + j, last)
             cols = pl.ds(pl.multiple_of(j * NT, NT), NT)
             out_ref[:, cols] = (hid_ref[:, cols].astype(f32) + r_ref[...] * dot(gg_ref[...], wo[:, cols])).astype(bf16)
             return carry
@@ -930,7 +965,7 @@
     @pl.when(back)
     def _():
         def block(j, carry):
-            run_ticks({t: f for t, f in ticks.items() if in_back(t)}, step * blocks + j, TAIL_TICKS)
+            run_ticks({t: f for t, f in ticks.items() if in_back(t)}, step * blocks + j, last)
             cols = pl.ds(pl.multiple_of(j * NT, NT), NT)
             part = dot(dz0_ref[0], wg[cols, :Eh], ((1,), (1,))) + dot(dz1_ref[0], wg[cols, Eh:], ((1,), (1,)))
             part = part + dot(dz0_ref[1], wa[cols, :Eh], ((1,), (1,))) + dot(dz1_ref[1], wa[cols, Eh:E], ((1,), (1,)))
@@ -960,7 +995,7 @@
 
     @pl.when(step == 2 * tiles - 1)
     def _():
-        run_rest(ticks, TAIL_TICKS)
+        run_rest(ticks, last)
         for p in pipes:
             p.finish()
         small_ref[...] = mine.total()
@@ -971,7 +1006,7 @@
     T, D = hidden.shape
     E = full_out.shape[0]
     n = nd * nf
-    rows, cols = gs[0].shape[1], sum(w for pipe in split for _, _, w in pipe)
+    rows = gs[0].shape[-2]
     MT = 256 if rows % 16 == 0 else 128
     tiles = T // MT
     early = tiles // 2
@@ -991,14 +1026,47 @@
         grid=(2 * tiles,),
         in_specs=[any_] * (len(gs) + 3) + [out_tile(E), half, half, back_tile(wide), pl.BlockSpec((MT, D), lambda k: (at_row(k), 0)), back_tile(D),
                                            out_tile(1), whole((1, D)), whole(mine.shape)],
-        out_specs=[whole((rows, cols)), out_tile(D), back_tile(D), whole(tile), whole(ntile)],
-        out_shape=(S((rows, cols), f32), S((T, D), bf16), S((T, D), bf16), S(tile, f32), S(ntile, f32)),
+        out_specs=[whole((rows, w)) for w in widths(split)] + [out_tile(D), back_tile(D), whole(tile), whole(ntile)],
+        out_shape=[S((rows, w), f32) for w in widths(split)] + [S((T, D), bf16), S((T, D), bf16), S(tile, f32), S(ntile, f32)],
         scratch_shapes=[pltpu.VMEM((E, D), bf16), pltpu.VMEM((D, E), bf16), pltpu.VMEM((D, E + wide), bf16), pltpu.VMEM((MT, D), f32),
                         pltpu.VMEM((8, D), f32), pltpu.VMEM(ntile, f32), pltpu.SemaphoreType.DMA((3,))]
         + Spread.scratch(n, tile) + Spread.scratch(n, ntile) + pipes_scratch(nd, rows, split),
         compiler_params=pltpu.CompilerParams(collective_id=cid, has_side_effects=True, vmem_limit_bytes=67043328),
         cost_estimate=pl.CostEstimate(flops=2 * T * D * 3 * E, bytes_accessed=8 * D * E, transcendentals=0),
     )(*gs, full_out, full_gate, full_a, gg, dz0, dz1, dbcdt, hidden, grad_out, r, norm_gain, mine)
+
+
+def finish_kernel(nd, nf, gate0_ref, gate1_ref, u0_ref, u1_ref, oa_ref, ob_ref, tot_ref, norm_ref,
+                  zx_ref, bc_ref, dt_ref, out_ref, conv_ref, n_ref, gg_ref, heads_ref):
+    Eh = gate0_ref.shape[1]
+    for k, ref in enumerate((gate0_ref, gate1_ref, u0_ref)):
+        zx_ref[:, k * Eh : (k + 1) * Eh] = ref[...]
+    zx_ref[:, 3 * Eh :] = u1_ref[:, :Eh]
+    wide = bc_ref.shape[1]
+    bc_ref[...] = u1_ref[:, Eh : Eh + wide]
+    dt_ref[...] = u1_ref[:, Eh + wide : Eh + wide + 128][:, : dt_ref.shape[1]]
+    half = oa_ref.shape[1]
+    out_ref[:, :half] = oa_ref[...]
+    out_ref[:, half:] = ob_ref[...]
+    k1 = conv_ref.shape[0]
+    conv_ref[...] = tot_ref[:k1, : conv_ref.shape[1]]
+    gg_ref[...] = tot_ref[k1 : k1 + 1, : gg_ref.shape[1]]
+    heads_ref[...] = tot_ref[k1 + 1 : k1 + 1 + heads_ref.shape[0], : heads_ref.shape[1]]
+    me = lax.axis_index("dp") * nf + lax.axis_index("fsdp")
+    nrow = n_ref.shape[1]
+    D = nrow * nd * nf
+    row = jnp.concatenate([norm_ref[j : j + 1, :] for j in range(D // 128)], axis=1)
+    row = pltpu.roll(jnp.broadcast_to(row, (8, D)), lax.rem(D - me * nrow, D), 1)
+    n_ref[...] = row[:1, :nrow]
+
+
+def finish(nd, nf, gate0, gate1, u0, u1, s_out, tot, d_norm, shapes):
+    S = jax.ShapeDtypeStruct
+    return pl.pallas_call(
+        functools.partial(finish_kernel, nd, nf),
+        out_shape=[S(s, f32) for s in shapes],
+        compiler_params=pltpu.CompilerParams(vmem_limit_bytes=40 << 20),
+    )(gate0, gate1, u0, u1, *s_out, tot, d_norm)
 
 
 def layer(nd, nf, hidden, grad_out, seg, shard_a, shard_gate, shard_out, head_params, sizes):
@@ -1019,19 +1087,14 @@
     rows = hidden.astype(f32)
     rinv = lax.rsqrt(jnp.mean(rows * rows, axis=-1, keepdims=True) + EPS)
     xhat = rows * rinv
-    normed = (xhat * norm_gain).astype(bf16)
+    normed = lax.optimization_barrier((xhat * norm_gain).astype(bf16))
+    normt = normed.T
     ubc = dot(normed, full_a).astype(bf16)
     gate = dot(normed, full_gate).astype(bf16)
-    pos = jnp.arange(T, dtype=jnp.int32)
-    masks = jnp.stack([jnp.ones((T,), f32)] + [((jnp.roll(seg, k) == seg) & (pos >= k)).astype(f32) for k in range(1, 4)], axis=1)
-    lastid = seg[L - 1 :: L]
-    previd = jnp.concatenate([jnp.full((1,), -1, jnp.int32), lastid[:-1]])
-    segc = jnp.stack([seg, jnp.repeat(previd, L), jnp.repeat(lastid, L)], axis=1)
-    segr = seg[None, :]
+    segc, segr = seg[:, None], seg[None, :]
     taps_u = jnp.concatenate([conv[:, :E], gate_gain[None], jnp.repeat(head_params[2], E // H)[None], jnp.zeros((1, E), f32)], axis=0)
     taps_bc = jnp.concatenate([conv[:, E:], jnp.zeros((3, 2 * N), f32)], axis=0)
-    heads_p = jnp.pad(head_params, ((0, 5), (0, 128 - H)))
-    b, c, bt, ct, pre_bc, gm, cum, cumr, sc, dt = prep(ubc, taps_bc, heads_p, masks, segc, segr, N, H)
+    masks, b, c, bt, ct, pre_bc, gm, cum, cumr, sc, dt = prep(ubc, taps_bc, head_params, segc, segr, N, H)
     gg, ssq, pre, st = fwd(ubc, gate, taps_u, masks, b, c, bt, gm, cum, cumr, sc)
     r = lax.rsqrt(jnp.sum(ssq, axis=1, keepdims=True) / E + EPS)
     gos = (grad_out.astype(f32) * r).astype(bf16)
@@ -1039,37 +1102,34 @@
     dm = dot(grad_out, full_out, ((1,), (1,))).astype(bf16)
     s = jnp.sum(gg.astype(f32) * dm.astype(f32), axis=1, keepdims=True)
     rq = jnp.concatenate([r, r * r * r * s / E], axis=1)
-    masks8 = jnp.pad(masks, ((0, 8), (0, 0)))
-    shape = lambda g: g.reshape(n, D // n, -1)
-    grad = lambda dz: shape(dot(normed, dz, ((0,), (0,))).astype(bf16))
-    back = functools.partial(bwd, u=ubc, gate=gate, pre=pre, dm=dm, rq=rq, taps=taps_u, masks=masks8, b=b, c=c, ct=ct, gm=gm, cum=cum,
-                             cumr=cumr, sc=sc, st=st)
-    dz0, dg0, db0, dc0, rs0, small0, kk0, s_out = back(0, 2, comm=(nd, nf, 4, (g_out.reshape(n, E // n, D),), (((0, 0, D // 2),), ((0, D // 2, D // 2),))))
-    dz1, dg1, db1, dc1, rs1, small1, kk1, sum0 = back(1, 2, comm=(nd, nf, 3, (grad(dz0[0]), grad(dz0[1])), (((0, 0, E // 2),), ((1, 0, E // 2),))))
+    back = functools.partial(bwd, u=ubc, gate=gate, pre=pre, dm=dm, rq=rq, taps=taps_u, masks=masks, b=b, c=c, ct=ct, gm=gm, cum=cum,
+                             cumr=cumr, sc=sc, st=st, normt=normt)
+    zn = max(nd // 2, 1)
+    rows_of = lambda g: g.reshape(g.shape[:-2] + (zn, n // zn, g.shape[-2] // n, g.shape[-1]))
+    Eh = E // 2
+    dz0, gw0, dg0, db0, dc0, rs0, small0, kk0, *s_out = back(
+        0, 2, comm=(nd, nf, 4, (rows_of(g_out),), (((0, None, 0, D // 2),), ((0, None, D // 2, D // 2),))))
+    dz1, gw1, dg1, db1, dc1, rs1, small1, kk1, gate0, u0 = back(1, 2, comm=(nd, nf, 3, (rows_of(gw0),), (((0, 0, 0, Eh),), ((0, 1, 0, Eh),))))
     small = jnp.concatenate([small0, small1], axis=1)
     kk = jnp.concatenate([kk0, kk1], axis=1)
     kkh = jnp.sum(kk.reshape(kk.shape[0], H, E // H), axis=2)
-    dbcdt, small_bc, hs = post(ubc, pre_bc, taps_bc, heads_p, masks8, segc, segr, b, c, (dg0, db0, dc0, rs0), (dg1, db1, dc1, rs1), kkh, dt)
+    dbcdt, small_bc, hs = post(ubc, pre_bc, taps_bc, head_params, masks, segc, segr, b, c, (dg0, db0, dc0, rs0), (dg1, db1, dc1, rs1), kkh, dt)
     d_conv = jnp.concatenate([jnp.stack([small[6], small[5], small[4], small[3], small[2]]),
                               jnp.stack([small_bc[4], small_bc[3], small_bc[2], small_bc[1], small_bc[0]])], axis=1)
     d_heads = jnp.concatenate([hs, jnp.sum(small[1].reshape(1, H, E // H), axis=2)], axis=0)
-    mine = jnp.concatenate([d_conv.reshape(K1, n, ncol).transpose(1, 0, 2).reshape(n, -1), small[0].reshape(n, -1),
-                            jnp.broadcast_to(d_heads.reshape(1, -1), (n, d_heads.size))], axis=1)
-    tiles = -(-mine.shape[1] // 1024)
-    mine = jnp.pad(mine, ((0, 0), (0, tiles * 1024 - mine.shape[1]))).reshape(n, tiles * 8, 128)
-    split = (((0, 0, E // 2),), ((1, 0, E // 2), (2, 0, wide)))
-    sum1, output, grad_in, tot, d_norm = tail(nd, nf, 1, (grad(dz1[0]), grad(dz1[1]), grad(dbcdt)), split, dz0, dz1, dbcdt, full_gate, full_a, gg,
-                                              full_out, hidden, grad_out, r, norm_gain[None], mine)
-    tot = tot.reshape(-1)
-    me = lax.axis_index("dp") * nf + lax.axis_index("fsdp")
-    t_norm = lax.dynamic_slice(d_norm.reshape(-1), (me * nrow,), (nrow,))
-    cut = [0, K1 * ncol, ngate, d_heads.size]
-    ends = [sum(cut[: k + 1]) for k in range(4)]
-    t_conv, t_gate, t_heads = (tot[ends[k] : ends[k + 1]] for k in range(3))
-    Eh = E // 2
-    s_zx = jnp.concatenate([sum0[:, :Eh], sum1[:, :Eh], sum0[:, Eh:], sum1[:, Eh : 2 * Eh]], axis=1)
-    return (output, grad_in, s_zx, sum1[:, 2 * Eh : 2 * Eh + 2 * N], sum1[:, 2 * Eh + 2 * N : 2 * Eh + 2 * N + H], s_out,
-            t_conv.reshape(K1, ncol), t_norm, t_gate, t_heads.reshape(d_heads.shape))
+    lanes = -(-max(ncol, ngate, H) // 128) * 128
+    cols = lambda a: jnp.pad(a.reshape(-1, n, a.shape[1] // n).transpose(1, 0, 2), ((0, 0), (0, 0), (0, lanes - a.shape[1] // n)))
+    heads_row = jnp.broadcast_to(jnp.pad(d_heads, ((0, 0), (0, lanes - H)))[None], (n, d_heads.shape[0], lanes))
+    used = K1 + 1 + d_heads.shape[0]
+    mine = jnp.concatenate([cols(d_conv), cols(small[:1]), heads_row, jnp.zeros((n, -(-used // 8) * 8 - used, lanes), f32)], axis=1)
+    g_bcdt = dot(normt, dbcdt).astype(bf16)
+    split = (((0, 0, 0, Eh),), ((0, 1, 0, Eh), (1, None, 0, wide)))
+    gate1, u1, output, grad_in, tot, d_norm = tail(nd, nf, 1, (rows_of(gw1), rows_of(g_bcdt)), split, dz0, dz1, dbcdt, full_gate, full_a, gg,
+                                                   full_out, hidden, grad_out, r, norm_gain[None], mine)
+    s_zx, s_bc, s_dt, s_w, t_conv, t_norm, t_gate, t_heads = finish(
+        nd, nf, gate0, gate1, u0, u1, s_out, tot, d_norm,
+        ((nrow, 2 * E), (nrow, 2 * N), (nrow, H), (E // n, D), (K1, ncol), (1, nrow), (1, ngate), d_heads.shape))
+    return output, grad_in, s_zx, s_bc, s_dt, s_w, t_conv, t_norm.reshape(-1), t_gate.reshape(-1), t_heads
 
 
 def per_device(nd, nf, hidden, grad_out, segment_ids, w_zx, w_bc, w_dt, w_out, conv_params, norm_gain, gate_gain, head_params):

time: 501 us -> 468 us (0.934)
  matrix products: 102 us -> 67.6 us
  Pallas kernels: 328 us -> 338 us
  local copies, waits for them, and re-layouts: 35.9 us -> 30.1 us
    dot_general x9 -> x5, matrix products: 102 us -> 67.6 us  [dot(): lax.dot_general(a, b, (dims, ((), ())), preferred_element_type=f32, preci...]
    pallas_call x2 -> x3, Pallas kernels: 117 us -> 142 us  [the longest x2 140 us: bwd(): pl.pallas_call(functools.partial(bwd_scatter_kernel, nd, nf, g0, Gh, nc,...]
    pallas_call x1, Pallas kernels: 77.9 us -> 66 us  [gather_rows(): pl.pallas_call(functools.partial(gather_kernel, nd, nf), out_shape=jax.Sh...]
    slice x9 -> x0, local copies, waits for them, and re-layouts: 10.6 us -> none  [the longest x3 2.78 us: layer(): jnp.roll(seg, k) == seg]
    unnamed x40 -> x38, local copies, waits for them, and re-layouts: 7.06 us -> 16.2 us
where the time goes in v6:
time: 468 us; the launch traced here: 460 us
  Pallas kernels  338 us (72%)
  matrix products  67.6 us (14%)
  local copies, waits for them, and re-layouts  30.1 us (6%)
  between operations  14.8 us (3%)
  other arithmetic  8.47 us (2%)
    pallas_call x2, Pallas kernels, bwd(): pl.pallas_call(functools.partial(bwd_scatter_kernel, nd, nf, g0, Gh, nc,...  140 us
    pallas_call x1, Pallas kernels, tail(): pl.pallas_call(functools.partial(tail_kernel, nd, nf, len(gs), split, til...  74.6 us
    dot_general x5, matrix products, dot(): lax.dot_general(a, b, (dims, ((), ())), preferred_element_type=f32, preci...  67.6 us
    pallas_call x1, Pallas kernels, gather_rows(): pl.pallas_call(functools.partial(gather_kernel, nd, nf), out_shape=jax.Sh...  66 us
    pallas_call x1, Pallas kernels, fwd(): pl.pallas_call(fwd_kernel, grid=(G,), in_specs=[col(0), col(0), pl.BlockS...  40.6 us
    unnamed x38, local copies, waits for them, and re-layouts  16.2 us
  transfers between devices with their start and end apart: 2, of which 0 were waited for; matrix products, arithmetic and copies ran while one was open for 14% of the time, Pallas kernels for 25%

profile of v6, /device:TPU:0, one launch (start us, length us, event | category | flops | bytes accessed | tf_op | source)
XLA Modules:
  0.0 460.2 jit_solution(6599168588891331301)
XLA Ops:
  7.2 1.8 fusion.14
  11.5 1.6 concatenate.31.src_ref
  13.0 66.0 %shard_map.186 = bf16[32,48,3456]{2,1,0:T(8,128)(2,1)} custom-call(bf16[48,3456]{1,0:T(8,128)(2,1)} %concatenate.31.src_ref), custom_call_target="tpu_custom_call" | custom-call | tf_op jit(solution)/shard_map/pallas_call | solution.py:177
  79.0 1.2 slice.64
  81.7 3.2 copy.67
  85.6 2.4 fusion.2
  88.0 1.0 copy.73.segc_ref
  90.8 17.6 %convolution_convert_fusion.1.bcdt_ref.u_ref.refs_1_ = bf16[1024,3456]{1,0:T(8,128)(2,1)} fusion(bf16[1024,1536]{0,1:T(8,128)(2,1)} %fusion.2, bf16[1536,3456]{1,0:T(8,128)(2,1)} %bitcast.29), kind=kOutput, calls=%fused_computation.4 | convolution fusion | flops 10875174912 | bytes 20840448 | tf_op jit(solution)/shard_map/dot_general | solution.py:452
  108.4 7.7 %shard_map.187 = (f32[1032,4]{1,0:T(8,128)}, bf16[1024,128]{1,0:T(8,128)(2,1)}, bf16[1024,128]{1,0:T(8,128)(2,1)}, bf16[128,1024]{1,0:T(8,128)(2,1)}, bf16[128,1...) custom-call(bf16[1024,3456]{1,0:T(8,128)(2,1)} %convolution_convert_, ...), custom_call_target="tpu_custom_call" | custom-call | tf_op jit(solution)/shard_map/pallas_call | solution.py:544
  116.9 14.8 %convolution_convert_fusion.3.gate_ref.refs_2_ = bf16[1024,3072]{1,0:T(8,128)(2,1)} fusion(bf16[1024,1536]{0,1:T(8,128)(2,1)S(1)} %copy-done.9, bf16[1536,3072]{1,0:T(8,128)(2,1)} %all-gather.3.cloned.1.call-done.refs_3_), kind=kOutput, calls=%fused_computation.10 | convolution fusion | flops 9666822144 | bytes 18874368 | tf_op jit(solution)/shard_map/dot_general | solution.py:452
  131.7 40.6 %shard_map.188 = (bf16[1024,3072]{1,0:T(8,128)(2,1)}, f32[1024,128]{1,0:T(8,128)}, bf16[1024,3072]{1,0:T(8,128)(2,1)}, bf16[8,128,3072]{2,1,0:T(8,128)(2,1)}) custom-call(bf16[1024,3456]{1,0:T(8,128)(2,1)} %convolution_convert_fusion.1.bcdt_ref.u_ref.refs_1_, bf16[1024,3072]{1,0:T(8,128)(2,1)} %convolution_convert_fusion.3.gate_ref.refs_2_, ...), custom_call_target="tpu_custom_call" | custom-call | flops 4831838208 | bytes 37748736 | tf_op jit(solution)/shard_map/pallas_call | solution.py:635
  172.3 1.2 reduce_sum.50
  173.6 1.0 copy.78.refs_11_
  174.6 15.2 %convolution_convert_fusion = bf16[3072,1536]{1,0:T(8,128)(2,1)} fusion(bf16[1024,3072]{1,0:T(8,128)(2,1)} %get-tuple-element.70.refs_5_, bf16[1024,1536]{1,0:T(8,128)(2,1)S(1)} %copy-done.16, f32[1024]{0:T(1024)S(1)} %add_rsqrt_fusion), kind=kOutput, calls=%fused_computation.1 | convolution fusion | flops 9673113600 | bytes 18878464 | tf_op jit(solution)/shard_map/dot_general | solution.py:452
  189.8 16.1 %multiply_reduce_fusion = (f32[1024]{0:T(1024)S(1)}, bf16[1024,3072]{1,0:T(8,128)(2,1)}) fusion(bf16[1024,3072]{1,0:T(8,128)(2,1)} %get-tuple-element.70.refs_5_, bf16[1024,1536]{1,0:T(8,128)(2,1)S(1)} %copy-done.16, bf16[3072,1536]{1,0:T(8,128)(2,1)} %all-gather.5.cloned.1.call-done.refs_2_), kind=kOutput, calls=%fused_computation | convolution fusion | flops 9679404032 | bytes 25169920 | tf_op jit(solution)/shard_map/dot_general | solution.py:452
  205.9 1.0 copy.74.refs_5_
  206.9 68.9 %shard_map.189 = (bf16[2,1024,1536]{2,1,0:T(8,128)(2,1)}, bf16[2,1536,1536]{2,1,0:T(8,128)(2,1)}, f32[8,128,128]{2,1,0:T(8,128)}, f32[1024,128]{1,0:T(8,128)}, f...) custom-call(bf16[4,8,96,1536]{3,2,1,0:T(8,128)(2,1)} %bitcast.47, ...), custom_call_target="tpu_custom_call" | custom-call | flops 13690208256 | bytes 25165824 | tf_op jit(solution)/shard_map/pallas_call | solution.py:818
  275.9 71.4 %shard_map.190 = (bf16[2,1024,1536]{2,1,0:T(8,128)(2,1)}, bf16[2,1536,1536]{2,1,0:T(8,128)(2,1)}, f32[8,128,128]{2,1,0:T(8,128)}, f32[1024,128]{1,0:T(8,128)}, f...) custom-call(bf16[2,4,8,48,1536]{4,3,2,1,0:T(8,128)(2,1)} %bitcast.46, ...), custom_call_target="tpu_custom_call" | custom-call | flops 13690208256 | bytes 25165824 | tf_op jit(solution)/shard_map/pallas_call | solution.py:818
  350.0 8.0 %shard_map.191 = (bf16[1024,384]{1,0:T(8,128)(2,1)}, f32[8,256]{1,0:T(8,128)}, f32[2,48]{1,0:T(2,128)}) custom-call(bf16[1024,3456]{1,0:T(8,128)(2,1)} %convolution_convert_fusion.1.bcdt_ref.u_ref.refs_1_, f32[1024,256]{1,0:T(8,128)} %get-tuple-element.77.pre_ref, f32[8,256]{1,0:T(8,128)} %concatenate.33.taps_ref, f32[3,48]{1,0:T(4,128)} %heads_ref.3, ...), custom_call_target="tpu_custom_call" | custom-call | tf_op jit(solution)/shard_map/pallas_call | solution.py:902
  359.3 3.9 convolution_convert_fusion.4
  364.1 74.6 %shard_map.192 = (f32[48,1536]{1,0:T(8,128)}, f32[48,1920]{1,0:T(8,128)}, bf16[1024,1536]{1,0:T(8,128)(2,1)}, bf16[1024,1536]{1,0:T(8,128)(2,1)}, f32[16,128]{1,0:T(8,128)}, /*index=5*/f32[16,128]{1,0:T(8,128)}) custom-call(bf16[2,4,8,48,1536]{4,3,2,1,0:T(8,128)(2,1)} %bitcast.45, bf16[4,8,48,384]{3,2,1,0:T(8,128)(2,1)} %bitcast.48, ...), custom_call_target="tpu_custom_call" | custom-call | flops 28991029248 | bytes 37748736 | tf_op jit(solution)/shard_map/pallas_call | solution.py:1024
  445.9 1.3 shard_map.193
  447.1 4.1 copy.85
  451.2 1.7 copy.86
  (88 shorter events, 19.1 us)
Async XLA Ops:
  7.2 109.7 %all-gather.3.cloned.1.call-start = ((), (), s32[]{:S(2)}) async-start(), calls=%async_computation | async-start | bytes 9732096 | tf_op jit(solution)/shard_map/all_gather | solution.py:1077
  9.1 180.7 %all-gather.5.cloned.1.call-start = ((), (), s32[]{:S(2)}) async-start(), calls=%async_computation.1 | async-start | bytes 9732096 | tf_op jit(solution)/shard_map/all_gather | solution.py:1078
  80.8 7.2 %copy-start.11 = (f32[5,3328]{1,0:T(8,128)}, f32[5,3328]{1,0:T(8,128)S(1)}, u32[]{:S(2)}) copy-start(f32[5,3328]{1,0:T(8,128)S(1)} %reshape.159) | copy-start | bytes 199684
  84.8 3.2 copy-start.14
  108.4 7.7 %slice-start = ((f32[5,3328]{1,0:T(8,128)}), f32[5,3072]{1,0:T(8,128)S(1)}, s32[]{:S(2)}) async-start(f32[5,3328]{1,0:T(8,128)} %copy-done.11), calls=%async_computation.2 | async-start | bytes 196608 | tf_op jit(solution)/shard_map/slice | solution.py:1095
  108.4 8.4 %copy-start.9 = (bf16[1024,1536]{0,1:T(8,128)(2,1)S(1)}, bf16[1024,1536]{0,1:T(8,128)(2,1)}, u32[]{:S(2)}) copy-start(bf16[1024,1536]{0,1:T(8,128)(2,1)} %fusion.2) | copy-start | bytes 9437188
  131.7 42.9 %copy-start.16 = (bf16[1024,1536]{1,0:T(8,128)(2,1)S(1)}, bf16[1024,1536]{1,0:T(8,128)(2,1)}, u32[]{:S(2)}) copy-start(bf16[1024,1536]{1,0:T(8,128)(2,1)} %refs_10_.1) | copy-start | bytes 9437188
  275.8 71.4 %copy-start.12 = (f32[8,1536]{1,0:T(8,128)S(1)}, f32[8,1536]{1,0:T(8,128)}, u32[]{:S(2)}) copy-start(f32[8,1536]{1,0:T(8,128)} %get-tuple-element.92) | copy-start | bytes 147460
  275.8 72.5 %copy-start.13 = (f32[8,1536]{1,0:T(8,128)S(1)}, f32[8,1536]{1,0:T(8,128)}, u32[]{:S(2)}) copy-start(f32[8,1536]{1,0:T(8,128)} %get-tuple-element.86) | copy-start | bytes 147460
  350.0 9.3 %copy-start.10 = (bf16[1024,1536]{0,1:T(8,128)(2,1)S(1)}, bf16[1024,1536]{0,1:T(8,128)(2,1)}, u32[]{:S(2)}) copy-start(bf16[1024,1536]{0,1:T(8,128)(2,1)} %fusion.2) | copy-start | bytes 9437188
  358.0 5.3 %copy-start.15 = (f32[2,48]{1,0:T(2,128)S(1)}, f32[2,48]{1,0:T(2,128)}, u32[]{:S(2)}) copy-start(f32[2,48]{1,0:T(2,128)} %get-tuple-element.95) | copy-start | bytes 1156
  438.7 1.0 copy-start
  439.6 1.0 copy-start.1
  440.6 1.0 copy-start.2
  441.6 1.0 copy-start.3
  442.5 1.0 copy-start.4
  443.5 1.0 copy-start.5
  444.5 0.7 copy-start.6
  445.2 0.7 copy-start.7
  445.9 5.4 %copy-start.8 = (bf16[1024,1536]{1,0:T(8,128)(2,1)S(1)}, bf16[1024,1536]{1,0:T(8,128)(2,1)}, u32[]{:S(2)}) copy-start(bf16[1024,1536]{1,0:T(8,128)(2,1)} %get-tuple-element.141) | copy-start | bytes 9437188
Sparse Core Ops, SparseCore 0:
  10.9 93.5 all-gather.2
  107.4 82.1 all-gather.4

commit v7 on v6

--- a/solution.py
+++ b/solution.py
@@ -34,7 +34,11 @@
     def idx(self, z, y, x, c):
         return (z * 2 + y) * self.nf + x * 2 + c
 
-    def barrier(self):
+    def meet(self):
+        z, zn = self.z, self.zn
+        pl.semaphore_wait(pltpu.get_barrier_semaphore(), 3 + (z + zn - 1) // zn + (2 * zn - 2 - z) // zn)
+
+    def greet(self):
         z, y, x, c, zn = self.z, self.y, self.x, self.c, self.zn
         sem = pltpu.get_barrier_semaphore()
         for there in ((z, y, 1 - x, c), (z, 1 - y, x, c), (z, y, x, 1 - c)):
@@ -47,8 +51,6 @@
         @pl.when(z < zn - 1)
         def _():
             pl.semaphore_signal(sem, inc=1, device_id=self.dev(z + 1, y, x, c), device_id_type=MESH)
-
-        pl.semaphore_wait(sem, 3 + (z + zn - 1) // zn + (2 * zn - 2 - z) // zn)
 
 
 def gather_kernel(nd, nf, src_ref, out_ref, own_sem, z_send, z_recv, x_send, x_recv, y_send, y_recv, dx_send, dx_recv, dy_send, dy_recv, c_send, c_recv):
@@ -56,7 +58,8 @@
     z, y, x, c, zn = at.z, at.y, at.x, at.c, at.zn
     half = out_ref.shape[2] // 256 * 128
     lo, hi = pl.ds(0, half), pl.ds(half, out_ref.shape[2] - half)
-    at.barrier()
+    at.greet()
+    at.meet()
 
     def copy(block, to, send, recv, cols=None, src=None):
         ref = out_ref.at[block] if cols is None else out_ref.at[block, :, cols]
@@ -327,7 +330,7 @@
                 if dist:
                     each(dist, lambda zs: up(zs).wait_send())
 
-        self.start, self.finish, self.barrier = start, finish, at.barrier
+        self.start, self.finish, self.greet, self.meet = start, finish, at.greet, at.meet
         self.diag = [functools.partial(ready, 3)] + [functools.partial(each, dist, diag) for dist in order]
         self.sides = [functools.partial(each, dist, sides) for dist in order]
         self.pass_on = [functools.partial(each, dist, pass_on) for dist in order[:-1]]
@@ -341,8 +344,8 @@
                 V((zn + 1, rows, cols), bf16), D((4, parts)), D((4, parts)), D((4, parts))] + [D((zn,))] * 9 + [D((2, zn))]
 
 
-def plan(pipes, barrier, time_of, spots):
-    ticks = {0: [barrier] + [functools.partial(p.start, col) for col in (3, 1, 2, 0) for p in pipes]}
+def plan(pipes, place, time_of, spots):
+    ticks = {0: [place.greet], 1: [place.meet] + [functools.partial(p.start, col) for col in (3, 1, 2, 0) for p in pipes]}
 
     def put(when, fn):
         tick = next((t for t, us in enumerate(time_of) if us >= when), len(time_of))
@@ -415,13 +418,15 @@
             return carry
         lax.fori_loop(1, self.n, body, 0)
 
-    def barrier(self):
+    def greet(self):
         sem = pltpu.get_barrier_semaphore()
 
-        def greet(k):
+        def one(k):
             pl.semaphore_signal(sem, inc=1, device_id=(self.peer(k) // self.nf, self.peer(k) % self.nf), device_id_type=MESH)
-        self.loop(greet)
-        pl.semaphore_wait(sem, self.n - 1)
+        self.loop(one)
+
+    def meet(self):
+        pl.semaphore_wait(pltpu.get_barrier_semaphore(), self.n - 1)
 
     def copy(self, k):
         p = self.peer(k)
@@ -567,7 +572,7 @@
 
 
 def fwd_kernel(u_ref, gate_ref, taps_ref, m_ref, b_ref, c_ref, bt_ref, gm_ref, cum_ref, cumr_ref, sc_ref,
-               gg_ref, ssq_ref, pre_ref, st_ref, state):
+               gg_ref, r_ref, pre_ref, st_ref, state, move, ssq_ref):
     T, W = u_ref.shape
     P = W // HG
     nc = T // L
@@ -583,12 +588,25 @@
     def _():
         ssq_ref[...] = jnp.zeros_like(ssq_ref)
 
+    @pl.when(step == 0)
+    def _():
+        def make(c, carry):
+            here = pl.ds(pl.multiple_of(c * L, L), L)
+            lag = lax.broadcasted_iota(jnp.int32, (L, L + 16), 0) + 16 - lax.broadcasted_iota(jnp.int32, (L, L + 16), 1)
+            for k in range(1, 4):
+                move[c, (k - 1) * L : k * L, :] = jnp.where(lag == k, m_ref[here, k : k + 1], 0.0).astype(bf16)
+            return carry
+        lax.fori_loop(0, nc, make, 0)
+
     def chunk(c, carry):
         t0 = pl.multiple_of(c * L, L)
         here = pl.ds(t0, L)
         h0 = pl.multiple_of(jnp.maximum(t0 - 16, 0), 16)
-        ext = jnp.concatenate([u_ref[pl.ds(h0, 16), :], u_ref[here, :]], axis=0).astype(f32)
-        pre = conv_rows(ext, taps, m_ref[here, :], 16)
+        v = u_ref[here, :]
+        moved = dot(move[c], jnp.concatenate([u_ref[pl.ds(h0, 16), :], v], axis=0))
+        pre = taps[4:5] + taps[3:4] * v.astype(f32)
+        for k in range(1, 4):
+            pre = pre + taps[3 - k : 4 - k] * moved[(k - 1) * L : k * L]
         pre_ref[here, :] = pre.astype(bf16)
         x = pre * sigmoid(pre)
         s0 = pl.multiple_of(c * (3 * L), L)
@@ -619,7 +637,16 @@
         ssq_ref[here, :] += tot
         return carry
 
-    lax.fori_loop(0, nc, chunk, 0)
+    lax.fori_loop(0, nc, chunk, 0, unroll=4)
+
+    @pl.when(step == pl.num_programs(0) - 1)
+    def _():
+        def root(c, carry):
+            here = pl.ds(pl.multiple_of(c * L, L), L)
+            total = jnp.sum(ssq_ref[here, :], axis=1, keepdims=True)
+            r_ref[here, :] = lax.rsqrt(total / (W * pl.num_programs(0)) + EPS)
+            return carry
+        lax.fori_loop(0, nc, root, 0)
 
 
 def fwd(u, gate, taps, masks, b, c, bt, gm, cum, cumr, sc):
@@ -637,9 +664,9 @@
         grid=(G,),
         in_specs=[col(0), col(0), pl.BlockSpec((8, W), lambda g: (0, g)), full(masks), full(b), full(c), full(bt), full(gm),
                   full(cum), grp(cumr), full(sc)],
-        out_specs=[col(0), pl.BlockSpec((T, 128), lambda g: (0, 0)), col(0), pl.BlockSpec((nc, N, W), lambda g: (0, 0, g))],
-        out_shape=(S((T, E), bf16), S((T, 128), f32), S((T, E), bf16), S((nc, N, E), bf16)),
-        scratch_shapes=[pltpu.VMEM((N, W), f32)],
+        out_specs=[col(0), pl.BlockSpec((T, 1), lambda g: (0, 0)), col(0), pl.BlockSpec((nc, N, W), lambda g: (0, 0, g))],
+        out_shape=(S((T, E), bf16), S((T, 1), f32), S((T, E), bf16), S((nc, N, E), bf16)),
+        scratch_shapes=[pltpu.VMEM((N, W), f32), pltpu.VMEM((nc, 3 * L, L + 16), bf16), pltpu.VMEM((T, 128), f32)],
         compiler_params=pltpu.CompilerParams(vmem_limit_bytes=60 << 20),
         cost_estimate=pl.CostEstimate(flops=T * E * (2 * L + 4 * N) * 2, bytes_accessed=T * E * 12, transcendentals=T * E * 4),
     )(u, gate, taps, masks, b, c, bt, gm, cum, cumr, sc)
@@ -652,7 +679,7 @@
     pipes = pipes_of(nd, nf, g_refs, sums, split, comm)
     nb = ins[15].shape[0] // MB
     time_of = [21.0 * g + (1.9 * i if i < nc else 1.9 * nc + 1.9 * (i - nc)) for g in range(Gh) for i in range(nc + nb)]
-    ticks = plan(pipes, pipes[0].barrier, time_of, BWD_SPOTS)
+    ticks = plan(pipes, pipes[0], time_of, BWD_SPOTS)
     last = len(time_of) - 1
     bwd_body(lambda i: run_ticks(ticks, pl.program_id(0) * (nc + nb) + i, last), g0, *ins, *outs, *own)
 
@@ -931,9 +958,9 @@
     scale = 4 / tiles
     time_of = [4 + 0.75 * scale * t if t < early * blocks else
                (13 + 1.65 * scale * (t - early * blocks) if t < mid else 52.6 + 0.65 * scale * (t - mid)) for t in range(2 * tiles * blocks)]
-    ticks = plan(pipes, mine.barrier, time_of, TAIL_SPOTS)
+    ticks = plan(pipes, mine, time_of, TAIL_SPOTS)
     last = len(time_of) - 1
-    ticks[0].append(mine.begin)
+    ticks[1].append(mine.begin)
     ticks.setdefault((early + tiles) * blocks + 2, []).append(norm.begin)
     fetch = [pltpu.make_async_copy(src, dst, sem.at[k]) for k, (src, dst) in enumerate(((wo_hbm, wo), (wg_hbm, wg), (wa_hbm, wa)))]
 
@@ -1036,37 +1063,67 @@
     )(*gs, full_out, full_gate, full_a, gg, dz0, dz1, dbcdt, hidden, grad_out, r, norm_gain, mine)
 
 
-def finish_kernel(nd, nf, gate0_ref, gate1_ref, u0_ref, u1_ref, oa_ref, ob_ref, tot_ref, norm_ref,
-                  zx_ref, bc_ref, dt_ref, out_ref, conv_ref, n_ref, gg_ref, heads_ref):
-    Eh = gate0_ref.shape[1]
-    for k, ref in enumerate((gate0_ref, gate1_ref, u0_ref)):
-        zx_ref[:, k * Eh : (k + 1) * Eh] = ref[...]
-    zx_ref[:, 3 * Eh :] = u1_ref[:, :Eh]
-    wide = bc_ref.shape[1]
-    bc_ref[...] = u1_ref[:, Eh : Eh + wide]
-    dt_ref[...] = u1_ref[:, Eh + wide : Eh + wide + 128][:, : dt_ref.shape[1]]
-    half = oa_ref.shape[1]
-    out_ref[:, :half] = oa_ref[...]
-    out_ref[:, half:] = ob_ref[...]
-    k1 = conv_ref.shape[0]
-    conv_ref[...] = tot_ref[:k1, : conv_ref.shape[1]]
-    gg_ref[...] = tot_ref[k1 : k1 + 1, : gg_ref.shape[1]]
-    heads_ref[...] = tot_ref[k1 + 1 : k1 + 1 + heads_ref.shape[0], : heads_ref.shape[1]]
-    me = lax.axis_index("dp") * nf + lax.axis_index("fsdp")
-    nrow = n_ref.shape[1]
-    D = nrow * nd * nf
-    row = jnp.concatenate([norm_ref[j : j + 1, :] for j in range(D // 128)], axis=1)
-    row = pltpu.roll(jnp.broadcast_to(row, (8, D)), lax.rem(D - me * nrow, D), 1)
-    n_ref[...] = row[:1, :nrow]
-
-
-def finish(nd, nf, gate0, gate1, u0, u1, s_out, tot, d_norm, shapes):
+def finish_kernel(nd, nf, gate0_ref, gate1_ref, u0_ref, u1_ref, oa_ref, ob_ref, tot_ref, norm_ref, o_ref, gi_ref,
+                  oo_ref, go_ref, zx_ref, bc_ref, dt_ref, out_ref, conv_ref, n_ref, gg_ref, heads_ref):
+    oo_ref[...] = o_ref[...]
+    go_ref[...] = gi_ref[...]
+
+    @pl.when(pl.program_id(0) == 0)
+    def _():
+        Eh = gate0_ref.shape[1]
+        for k, ref in enumerate((gate0_ref, gate1_ref, u0_ref)):
+            zx_ref[:, k * Eh : (k + 1) * Eh] = ref[...]
+        zx_ref[:, 3 * Eh :] = u1_ref[:, :Eh]
+        wide = bc_ref.shape[1]
+        bc_ref[...] = u1_ref[:, Eh : Eh + wide]
+        dt_ref[...] = u1_ref[:, Eh + wide : Eh + wide + 128][:, : dt_ref.shape[1]]
+        half = oa_ref.shape[1]
+        out_ref[:, :half] = oa_ref[...]
+        out_ref[:, half:] = ob_ref[...]
+        k1 = conv_ref.shape[0]
+        conv_ref[...] = tot_ref[:k1, : conv_ref.shape[1]]
+        gg_ref[...] = tot_ref[k1 : k1 + 1, : gg_ref.shape[1]]
+        heads_ref[...] = tot_ref[k1 + 1 : k1 + 1 + heads_ref.shape[0], : heads_ref.shape[1]]
+        me = lax.axis_index("dp") * nf + lax.axis_index("fsdp")
+        nrow = n_ref.shape[1]
+        D = nrow * nd * nf
+        row = jnp.concatenate([norm_ref[j : j + 1, :] for j in range(D // 128)], axis=1)
+        row = pltpu.roll(jnp.broadcast_to(row, (8, D)), lax.rem(D - me * nrow, D), 1)
+        n_ref[...] = row[:1, :nrow]
+
+
+def finish(nd, nf, gate0, gate1, u0, u1, s_out, tot, d_norm, output, grad_in, shapes):
     S = jax.ShapeDtypeStruct
+    tile = pl.BlockSpec((256, output.shape[1]), lambda i: (i, 0))
     return pl.pallas_call(
         functools.partial(finish_kernel, nd, nf),
-        out_shape=[S(s, f32) for s in shapes],
+        grid=(output.shape[0] // 256,),
+        in_specs=[pl.BlockSpec(a.shape, lambda i: (0, 0)) for a in (gate0, gate1, u0, u1, *s_out, tot, d_norm)] + [tile, tile],
+        out_specs=[tile, tile] + [pl.BlockSpec(s, lambda i: (0, 0)) for s in shapes],
+        out_shape=[S(output.shape, bf16), S(output.shape, bf16)] + [S(s, f32) for s in shapes],
+        compiler_params=pltpu.CompilerParams(vmem_limit_bytes=63 << 20),
+    )(gate0, gate1, u0, u1, *s_out, tot, d_norm, output, grad_in)
+
+
+def norm_kernel(hid_ref, gain_ref, normed_ref, normt_ref):
+    rows = hid_ref[...].astype(f32)
+    normed = rows * lax.rsqrt(jnp.mean(rows * rows, axis=-1, keepdims=True) + EPS) * gain_ref[...]
+    normed_ref[...] = normed.astype(bf16)
+    normt_ref[...] = normed.T.astype(bf16)
+
+
+def norm(hidden, gain):
+    T, D = hidden.shape
+    S = jax.ShapeDtypeStruct
+    row = pl.BlockSpec((256, D), lambda i: (i, 0))
+    return pl.pallas_call(
+        norm_kernel,
+        grid=(T // 256,),
+        in_specs=[row, pl.BlockSpec((1, D), lambda i: (0, 0))],
+        out_specs=[row, pl.BlockSpec((D, 256), lambda i: (0, i))],
+        out_shape=(S((T, D), bf16), S((D, T), bf16)),
         compiler_params=pltpu.CompilerParams(vmem_limit_bytes=40 << 20),
-    )(gate0, gate1, u0, u1, *s_out, tot, d_norm)
+    )(hidden, gain)
 
 
 def layer(nd, nf, hidden, grad_out, seg, shard_a, shard_gate, shard_out, head_params, sizes):
@@ -1084,19 +1141,14 @@
     norm_gain = flat[:, K1 * ncol : K1 * ncol + nrow].reshape(-1).astype(f32)
     gate_gain = flat[:, K1 * ncol + nrow : K1 * ncol + nrow + ngate].reshape(-1).astype(f32)
     full_a = full_a.reshape(D, E + wide)
-    rows = hidden.astype(f32)
-    rinv = lax.rsqrt(jnp.mean(rows * rows, axis=-1, keepdims=True) + EPS)
-    xhat = rows * rinv
-    normed = lax.optimization_barrier((xhat * norm_gain).astype(bf16))
-    normt = normed.T
+    normed, normt = norm(hidden, norm_gain[None])
     ubc = dot(normed, full_a).astype(bf16)
     gate = dot(normed, full_gate).astype(bf16)
     segc, segr = seg[:, None], seg[None, :]
     taps_u = jnp.concatenate([conv[:, :E], gate_gain[None], jnp.repeat(head_params[2], E // H)[None], jnp.zeros((1, E), f32)], axis=0)
     taps_bc = jnp.concatenate([conv[:, E:], jnp.zeros((3, 2 * N), f32)], axis=0)
     masks, b, c, bt, ct, pre_bc, gm, cum, cumr, sc, dt = prep(ubc, taps_bc, head_params, segc, segr, N, H)
-    gg, ssq, pre, st = fwd(ubc, gate, taps_u, masks, b, c, bt, gm, cum, cumr, sc)
-    r = lax.rsqrt(jnp.sum(ssq, axis=1, keepdims=True) / E + EPS)
+    gg, r, pre, st = fwd(ubc, gate, taps_u, masks, b, c, bt, gm, cum, cumr, sc)
     gos = (grad_out.astype(f32) * r).astype(bf16)
     g_out = dot(gg, gos, ((0,), (0,))).astype(bf16)
     dm = dot(grad_out, full_out, ((1,), (1,))).astype(bf16)
@@ -1126,8 +1178,8 @@
     split = (((0, 0, 0, Eh),), ((0, 1, 0, Eh), (1, None, 0, wide)))
     gate1, u1, output, grad_in, tot, d_norm = tail(nd, nf, 1, (rows_of(gw1), rows_of(g_bcdt)), split, dz0, dz1, dbcdt, full_gate, full_a, gg,
                                                    full_out, hidden, grad_out, r, norm_gain[None], mine)
-    s_zx, s_bc, s_dt, s_w, t_conv, t_norm, t_gate, t_heads = finish(
-        nd, nf, gate0, gate1, u0, u1, s_out, tot, d_norm,
+    output, grad_in, s_zx, s_bc, s_dt, s_w, t_conv, t_norm, t_gate, t_heads = finish(
+        nd, nf, gate0, gate1, u0, u1, s_out, tot, d_norm, output, grad_in,
         ((nrow, 2 * E), (nrow, 2 * N), (nrow, H), (E // n, D), (K1, ncol), (1, nrow), (1, ngate), d_heads.shape))
     return output, grad_in, s_zx, s_bc, s_dt, s_w, t_conv, t_norm.reshape(-1), t_gate.reshape(-1), t_heads
 

time: 468 us -> 474 us (1.013)
  waiting for transfers between devices: 0.71 us -> 23.7 us
  local copies, waits for them, and re-layouts: 30.1 us -> 12.1 us
    all_gather x1, waiting for transfers between devices: 0.01 us -> 23 us  [layer(): full_out = lax.all_gather(shard_out, AXES, axis=0, tiled=True)]
    unnamed x38 -> x25, local copies, waits for them, and re-layouts: 16.2 us -> 0.06 us
    pallas_call x1 -> x2, Pallas kernels: 1.26 us -> 9.46 us  [the longest x1 7.17 us: finish(): pl.pallas_call(functools.partial(finish_kernel, nd, nf), grid=(output.sha...]
    pallas_call x2, Pallas kernels: 140 us -> 135 us  [bwd(): pl.pallas_call(functools.partial(bwd_scatter_kernel, nd, nf, g0, Gh, nc,...]
  transfers between devices with their start and end apart: 2 -> 2, of which waited for: 0 -> 1; matrix products, arithmetic and copies ran while one was open for 14% -> 10% of each run, Pallas kernels for 25% -> 24%
where the time goes in v7:
time: 474 us; the launch traced here: 465 us
  Pallas kernels  336 us (71%)
  matrix products  69.9 us (15%)
  waiting for transfers between devices  23.7 us (5%)
  between operations  14.8 us (3%)
  local copies, waits for them, and re-layouts  12.1 us (3%)
  other arithmetic  7.51 us (2%)
    pallas_call x2, Pallas kernels, bwd(): pl.pallas_call(functools.partial(bwd_scatter_kernel, nd, nf, g0, Gh, nc,...  135 us
    pallas_call x1, Pallas kernels, tail(): pl.pallas_call(functools.partial(tail_kernel, nd, nf, len(gs), split, til...  73.7 us
    dot_general x5, matrix products, dot(): lax.dot_general(a, b, (dims, ((), ())), preferred_element_type=f32, preci...  69.9 us
    pallas_call x1, Pallas kernels, gather_rows(): pl.pallas_call(functools.partial(gather_kernel, nd, nf), out_shape=jax.Sh...  65.9 us
    pallas_call x1, Pallas kernels, fwd(): pl.pallas_call(fwd_kernel, grid=(G,), in_specs=[col(0), col(0), pl.BlockS...  36.2 us
    all_gather x1, waiting for transfers between devices, layer(): full_out = lax.all_gather(shard_out, AXES, axis=0, tiled=True)  23 us
  transfers between devices with their start and end apart: 2, of which 1 were waited for; matrix products, arithmetic and copies ran while one was open for 10% of the time, Pallas kernels for 24%

profile of v7, /device:TPU:0, one launch (start us, length us, event | category | flops | bytes accessed | tf_op | source)
XLA Modules:
  0.0 464.6 jit_solution(14997549848608316551)
XLA Ops:
  7.2 1.8 fusion.11
  11.5 1.6 concatenate.31.src_ref
  13.1 65.9 %shard_map.186 = bf16[32,48,3456]{2,1,0:T(8,128)(2,1)} custom-call(bf16[48,3456]{1,0:T(8,128)(2,1)} %concatenate.31.src_ref), custom_call_target="tpu_custom_call" | custom-call | tf_op jit(solution)/shard_map/pallas_call | solution.py:180
  79.0 1.2 slice.64
  80.2 1.0 reshape.106
  82.2 0.8 slice_convert_fusion.2
  83.1 1.0 copy.58.segc_ref
  86.6 2.3 shard_map.187
  88.9 18.6 %convolution_convert_fusion.1.bcdt_ref.u_ref.refs_1_ = bf16[1024,3456]{1,0:T(8,128)(2,1)} fusion(bf16[1024,1536]{1,0:T(8,128)(2,1)S(1)} %get-tuple-element.66, bf16[1536,3456]{1,0:T(8,128)(2,1)} %bitcast.27), kind=kOutput, calls=%fused_computation.2 | convolution fusion | flops 10875174912 | bytes 20840448 | tf_op jit(solution)/shard_map/dot_general | solution.py:457
  107.5 7.8 %shard_map.188 = (f32[1032,4]{1,0:T(8,128)}, bf16[1024,128]{1,0:T(8,128)(2,1)}, bf16[1024,128]{1,0:T(8,128)(2,1)}, bf16[128,1024]{1,0:T(8,128)(2,1)}, bf16[128,1...) custom-call(bf16[1024,3456]{1,0:T(8,128)(2,1)} %convolution_convert_, ...), custom_call_target="tpu_custom_call" | custom-call | tf_op jit(solution)/shard_map/pallas_call | solution.py:549
  116.0 14.3 %convolution_convert_fusion.3.gate_ref.refs_2_ = bf16[1024,3072]{1,0:T(8,128)(2,1)} fusion(bf16[1024,1536]{1,0:T(8,128)(2,1)S(1)} %copy-done.5, bf16[1536,3072]{1,0:T(8,128)(2,1)} %all-gather.3.cloned.1.call-done.refs_3_), kind=kOutput, calls=%fused_computation.5 | convolution fusion | flops 9666822144 | bytes 18874368 | tf_op jit(solution)/shard_map/dot_general | solution.py:457
  130.3 36.2 %shard_map.189 = (bf16[1024,3072]{1,0:T(8,128)(2,1)}, f32[1024,1]{1,0:T(8,128)}, bf16[1024,3072]{1,0:T(8,128)(2,1)}, bf16[8,128,3072]{2,1,0:T(8,128)(2,1)}) custom-call(bf16[1024,3456]{1,0:T(8,128)(2,1)} %convolution_convert_fusion.1.bcdt_ref.u_ref.refs_1_, bf16[1024,3072]{1,0:T(8,128)(2,1)} %convolution_convert_fusion.3.gate_ref.refs_2_, ...), custom_call_target="tpu_custom_call" | custom-call | flops 4831838208 | bytes 37748736 | tf_op jit(solution)/shard_map/pallas_call | solution.py:662
  166.6 23.0 %all-gather.5.cloned.1.call-done.refs_2_ = bf16[3072,1536]{1,0:T(8,128)(2,1)} async-done(((bf16[96,1536]{1,0:T(8,128)(2,1)}), bf16[3072,1536]{1,0:T(8,128)(2,1)}) %all-gather.5.cloned.1.call-update) | async-done | bytes 9437200 | tf_op jit(solution)/shard_map/all_gather | solution.py:1135
  189.5 17.5 %multiply_reduce_fusion = (f32[1024]{0:T(1024)S(1)}, bf16[1024,3072]{1,0:T(8,128)(2,1)}) fusion(bf16[1024,3072]{1,0:T(8,128)(2,1)} %get-tuple-element.75.refs_5_, bf16[1024,1536]{1,0:T(8,128)(2,1)} %refs_10_.1, bf16[3072,1536]{1,0:T(8,128)(2,1)} %all-gather.5.cloned.1.call-done.refs_2_), kind=kOutput, calls=%fused_computation | convolution fusion | flops 9679404032 | bytes 25169920 | tf_op jit(solution)/shard_map/dot_general | solution.py:457
  207.5 1.0 pad_maximum_fusion.refs_5_
  208.5 15.6 %convolution_convert_fusion = bf16[3072,1536]{1,0:T(8,128)(2,1)} fusion(bf16[1024,3072]{1,0:T(8,128)(2,1)} %get-tuple-element.75.refs_5_, bf16[1024,1536]{1,0:T(8,128)(2,1)} %refs_10_.1, f32[1024]{0:T(1024)S(1)} %get-tuple-element.127), kind=kOutput, calls=%fused_computation.1 | convolution fusion | flops 9673113600 | bytes 18878464 | tf_op jit(solution)/shard_map/dot_general | solution.py:457
  224.2 66.0 %shard_map.190 = (bf16[2,1024,1536]{2,1,0:T(8,128)(2,1)}, bf16[2,1536,1536]{2,1,0:T(8,128)(2,1)}, f32[8,128,128]{2,1,0:T(8,128)}, f32[1024,128]{1,0:T(8,128)}, f...) custom-call(bf16[4,8,96,1536]{3,2,1,0:T(8,128)(2,1)} %bitcast.40, ...), custom_call_target="tpu_custom_call" | custom-call | flops 13690208256 | bytes 25165824 | tf_op jit(solution)/shard_map/pallas_call | solution.py:845
  290.2 69.3 %shard_map.191 = (bf16[2,1024,1536]{2,1,0:T(8,128)(2,1)}, bf16[2,1536,1536]{2,1,0:T(8,128)(2,1)}, f32[8,128,128]{2,1,0:T(8,128)}, f32[1024,128]{1,0:T(8,128)}, f...) custom-call(bf16[2,4,8,48,1536]{4,3,2,1,0:T(8,128)(2,1)} %bitcast.39, ...), custom_call_target="tpu_custom_call" | custom-call | flops 13690208256 | bytes 25165824 | tf_op jit(solution)/shard_map/pallas_call | solution.py:845
  360.7 0.8 pad_maximum_fusion.2
  362.3 8.0 %shard_map.192 = (bf16[1024,384]{1,0:T(8,128)(2,1)}, f32[8,256]{1,0:T(8,128)}, f32[2,48]{1,0:T(2,128)}) custom-call(bf16[1024,3456]{1,0:T(8,128)(2,1)} %convolution_convert_fusion.1.bcdt_ref.u_ref.refs_1_, f32[1024,256]{1,0:T(8,128)} %get-tuple-element.84.pre_ref, f32[8,256]{1,0:T(8,128)} %concatenate.33.taps_ref, f32[3,48]{1,0:T(4,128)} %heads_ref.3, ...), custom_call_target="tpu_custom_call" | custom-call | tf_op jit(solution)/shard_map/pallas_call | solution.py:929
  370.3 0.9 fusion.12
  371.6 3.9 convolution_convert_fusion.4
  376.4 73.7 %shard_map.193 = (f32[48,1536]{1,0:T(8,128)}, f32[48,1920]{1,0:T(8,128)}, bf16[1024,1536]{1,0:T(8,128)(2,1)}, bf16[1024,1536]{1,0:T(8,128)(2,1)}, f32[16,128]{1,0:T(8,128)}, /*index=5*/f32[16,128]{1,0:T(8,128)}) custom-call(bf16[2,4,8,48,1536]{4,3,2,1,0:T(8,128)(2,1)} %bitcast.38, bf16[4,8,48,384]{3,2,1,0:T(8,128)(2,1)} %bitcast.41, ...), custom_call_target="tpu_custom_call" | custom-call | flops 28991029248 | bytes 37748736 | tf_op jit(solution)/shard_map/pallas_call | solution.py:1051
  450.1 7.2 %shard_map.194 = (bf16[1024,1536]{1,0:T(8,128)(2,1)}, bf16[1024,1536]{1,0:T(8,128)(2,1)}, f32[48,6144]{1,0:T(8,128)}, f32[48,256]{1,0:T(8,128)}, f32[48,48]{1,0:...) custom-call(f32[48,1536]{1,0:T(8,128)} %get-tuple-element.82.gate0_r, ...), custom_call_target="tpu_custom_call" | custom-call | tf_op jit(solution)/shard_map/pallas_call | solution.py:1098
  (69 shorter events, 10.3 us)
Async XLA Ops:
  7.2 108.8 %all-gather.3.cloned.1.call-start = ((), (), s32[]{:S(2)}) async-start(), calls=%async_computation | async-start | bytes 9732096 | tf_op jit(solution)/shard_map/all_gather | solution.py:1134
  9.1 180.5 %all-gather.5.cloned.1.call-start = ((), (), s32[]{:S(2)}) async-start(), calls=%async_computation.1 | async-start | bytes 9732096 | tf_op jit(solution)/shard_map/all_gather | solution.py:1135
  13.1 70.1 %copy-start.10 = (s32[1024]{0:T(1024)S(1)}, s32[1024]{0:T(1024)}, u32[]{:S(2)}) copy-start(s32[1024]{0:T(1024)} %param.13) | copy-start | bytes 12292
  13.1 73.6 %copy-start = (bf16[1024,1536]{1,0:T(8,128)(2,1)S(1)}, bf16[1024,1536]{1,0:T(8,128)(2,1)}, u32[]{:S(2)}) copy-start(bf16[1024,1536]{1,0:T(8,128)(2,1)} %refs_9_.1) | copy-start | bytes 9437188
  82.2 25.3 %copy-start.7 = (f32[5,3328]{1,0:T(8,128)}, f32[5,3328]{1,0:T(8,128)S(1)}, u32[]{:S(2)}) copy-start(f32[5,3328]{1,0:T(8,128)S(1)} %reshape.103) | copy-start | bytes 199684
  83.1 24.4 %copy-start.1 = (f32[1,1536]{1,0:T(1,128)}, f32[1,1536]{1,0:T(1,128)S(1)}, u32[]{:S(2)}) copy-start(f32[1,1536]{1,0:T(1,128)S(1)} %reshape.102.gain_ref.refs_12_) | copy-start | bytes 18436
  88.9 18.6 %copy-start.2 = (bf16[1536,1024]{1,0:T(8,128)(2,1)}, bf16[1536,1024]{1,0:T(8,128)(2,1)S(1)}, u32[]{:S(2)}) copy-start(bf16[1536,1024]{1,0:T(8,128)(2,1)S(1)} %get-tuple-element.80.refs_16_) | copy-start | bytes 9437188
  88.9 18.6 %copy-start.4 = (bf16[1024,1536]{1,0:T(8,128)(2,1)}, bf16[1024,1536]{1,0:T(8,128)(2,1)S(1)}, u32[]{:S(2)}) copy-start(bf16[1024,1536]{1,0:T(8,128)(2,1)S(1)} %get-tuple-element.66) | copy-start | bytes 9437188
  107.5 7.8 %slice-start = ((f32[5,3328]{1,0:T(8,128)}), f32[5,3072]{1,0:T(8,128)S(1)}, s32[]{:S(2)}) async-start(f32[5,3328]{1,0:T(8,128)} %copy-done.7), calls=%async_computation.2 | async-start | bytes 196608 | tf_op jit(solution)/shard_map/slice | solution.py:1148
  107.5 8.5 %copy-start.5 = (bf16[1024,1536]{1,0:T(8,128)(2,1)S(1)}, bf16[1024,1536]{1,0:T(8,128)(2,1)}, u32[]{:S(2)}) copy-start(bf16[1024,1536]{1,0:T(8,128)(2,1)} %copy-done.4) | copy-start | bytes 9437188
  189.5 17.8 %copy-start.6 = (f32[1024,1]{1,0:T(8,128)S(1)}, f32[1024,1]{1,0:T(8,128)}, u32[]{:S(2)}) copy-start(f32[1024,1]{1,0:T(8,128)} %get-tuple-element.76.refs_11_) | copy-start | bytes 12292
  290.2 69.4 %copy-start.8 = (f32[8,1536]{1,0:T(8,128)S(1)}, f32[8,1536]{1,0:T(8,128)}, u32[]{:S(2)}) copy-start(f32[8,1536]{1,0:T(8,128)} %get-tuple-element.99) | copy-start | bytes 147460
  290.2 70.5 %copy-start.9 = (f32[8,1536]{1,0:T(8,128)S(1)}, f32[8,1536]{1,0:T(8,128)}, u32[]{:S(2)}) copy-start(f32[8,1536]{1,0:T(8,128)} %get-tuple-element.93) | copy-start | bytes 147460
  362.3 9.3 %copy-start.3 = (bf16[1536,1024]{1,0:T(8,128)(2,1)S(1)}, bf16[1536,1024]{1,0:T(8,128)(2,1)}, u32[]{:S(2)}) copy-start(bf16[1536,1024]{1,0:T(8,128)(2,1)} %copy-done.2) | copy-start | bytes 9437188
  370.3 5.3 %copy-start.11 = (f32[2,48]{1,0:T(2,128)S(1)}, f32[2,48]{1,0:T(2,128)}, u32[]{:S(2)}) copy-start(f32[2,48]{1,0:T(2,128)} %get-tuple-element.102) | copy-start | bytes 1156
Sparse Core Ops, SparseCore 0:
  10.9 93.5 all-gather.2
  107.3 82.1 all-gather.4
